TPU v7x, 32 devices: a whole 2x2x4 slice. The times are simulated.
32 devices in a mesh: seq: 4 (over y, core), fsdp: 8 (over z, x).
Axes of the slice: x: 2, y: 2, z: 4, core: 2. Of those that a mesh axis runs over, the one named last changes fastest.
Arguments:
- tokens: bfloat16 [8, 1032, 1024], P('fsdp', 'seq'), may hold values from -6 to 6
- lengths: int32 [8], P('fsdp'), may hold values from 516 to 1025, as said below
- ln1_gain: bfloat16 [1024], P('fsdp'), may hold values from 0.5 to 1.5
- ln1_bias: bfloat16 [1024], P('fsdp'), may hold values from -3 to 3
- qkv_weight: bfloat16 [1024, 3072], P('fsdp'), may hold values from -0.34375 to 0.34375
- q_bias: bfloat16 [1024], P('fsdp'), may hold values from -3 to 3
- v_bias: bfloat16 [1024], P('fsdp'), may hold values from -3 to 3
- out_weight: bfloat16 [1024, 1024], P('fsdp'), may hold values from -3 to 3
- out_bias: bfloat16 [1024], P('fsdp'), may hold values from -3 to 3
- ln2_gain: bfloat16 [1024], P('fsdp'), may hold values from 0.5 to 1.5
- ln2_bias: bfloat16 [1024], P('fsdp'), may hold values from -3 to 3
- up_weight: bfloat16 [1024, 4096], P('fsdp'), may hold values from -0.1875 to 0.1875
- up_bias: bfloat16 [4096], P('fsdp'), may hold values from -3 to 3
- down_weight: bfloat16 [4096, 1024], P('fsdp'), may hold values from -0.09375 to 0.09375
- down_bias: bfloat16 [1024], P('fsdp'), may hold values from -3 to 3
- cotangent: bfloat16 [8, 1032, 1024], P('fsdp', 'seq'), may hold values from -6 to 6
Outputs:
- output: bfloat16 [8, 1032, 1024], P('fsdp', 'seq')
- grad_tokens: bfloat16 [8, 1032, 1024], P('fsdp', 'seq')
- grad_ln1_gain: float32 [1024], P('fsdp')
- grad_ln1_bias: float32 [1024], P('fsdp')
- grad_qkv_weight: float32 [1024, 3072], P('fsdp')
- grad_q_bias: float32 [1024], P('fsdp')
- grad_v_bias: float32 [1024], P('fsdp')
- grad_out_weight: float32 [1024, 1024], P('fsdp')
- grad_out_bias: float32 [1024], P('fsdp')
- grad_ln2_gain: float32 [1024], P('fsdp')
- grad_ln2_bias: float32 [1024], P('fsdp')
- grad_up_weight: float32 [1024, 4096], P('fsdp')
- grad_up_bias: float32 [4096], P('fsdp')
- grad_down_weight: float32 [4096, 1024], P('fsdp')
- grad_down_bias: float32 [1024], P('fsdp')
Inputs may be any that keep to these rules, and one draw needn't show every extreme that they name: `lengths`: each image's valid tokens are its first ones; some image has exactly 1025 valid tokens.
All inputs are finite; a program needn't handle non-finite values.
Results may differ from a plain program's by a relative error of at most 0.012.
The roundings to bfloat16 on the way count: a program that leaves them out, or rounds other values in their place, can miss the bound.
Values may be sent and summed in bfloat16 or wider, within the bound.
A program may use at most 192 MiB of HBM per device.

v0:
```python
import jax
import jax.numpy as jnp
from jax import lax
from jax.sharding import PartitionSpec as P

HEAD_DIM = 64


def norm_rows(values, gain_vec, shift_vec):
    center = values - jnp.mean(values, axis=-1, keepdims=True)
    spread = jnp.mean(center * center, axis=-1, keepdims=True)
    return center * lax.rsqrt(spread + 1e-06) * gain_vec + shift_vec


def gelu_exact(values):
    return jax.nn.gelu(values, approximate=False)


def masked_scores(queries, keys_all, length):
    raw_scores = jnp.einsum("qhd,khd->hqk", queries, keys_all, preferred_element_type=jnp.float32)
    allowed = jnp.arange(keys_all.shape[0]) < length
    return jnp.where(allowed[None, None, :], raw_scores * HEAD_DIM ** (-0.5), -1e30)


def attend_forward(element):
    queries, keys_all, values_all, length = element
    tok_count = queries.shape[0]
    queries = queries.reshape(tok_count, -1, HEAD_DIM)
    keys_all = keys_all.reshape(tok_count, -1, HEAD_DIM)
    values_all = values_all.reshape(tok_count, -1, HEAD_DIM)
    scores = masked_scores(queries, keys_all, length)
    highest_score = jnp.max(scores, axis=-1, keepdims=True)
    exp_scores = jnp.exp(scores - highest_score)
    totals = jnp.sum(exp_scores, axis=-1, keepdims=True)
    weights = (exp_scores / totals).astype(jnp.bfloat16)
    context = jnp.einsum("hqk,khd->qhd", weights, values_all, preferred_element_type=jnp.float32)
    log_total = (highest_score + jnp.log(totals))[:, :, 0]
    return (context.reshape(tok_count, -1).astype(jnp.bfloat16), log_total)


def attend_backward(element):
    queries, keys_all, values_all, log_total, grad_ctx, length = element
    tok_count = queries.shape[0]
    queries = queries.reshape(tok_count, -1, HEAD_DIM)
    keys_all = keys_all.reshape(tok_count, -1, HEAD_DIM)
    values_all = values_all.reshape(tok_count, -1, HEAD_DIM)
    grad_ctx = grad_ctx.reshape(tok_count, -1, HEAD_DIM)
    scores = masked_scores(queries, keys_all, length)
    probs = jnp.exp(scores - log_total[:, :, None])
    grad_probs = jnp.einsum(
        "qhd,khd->hqk", grad_ctx, values_all, preferred_element_type=jnp.float32
    )
    inner = jnp.sum(probs * grad_probs, axis=-1, keepdims=True)
    grad_scores = (probs * (grad_probs - inner) * HEAD_DIM ** (-0.5)).astype(jnp.bfloat16)
    grad_query = jnp.einsum(
        "hqk,khd->qhd", grad_scores, keys_all, preferred_element_type=jnp.float32
    )
    grad_key = jnp.einsum("hqk,qhd->khd", grad_scores, queries, preferred_element_type=jnp.float32)
    grad_value = jnp.einsum(
        "hqk,qhd->khd", probs.astype(jnp.bfloat16), grad_ctx, preferred_element_type=jnp.float32
    )
    stacked = jnp.stack([grad_query, grad_key, grad_value])
    return stacked.reshape(3, tok_count, -1).astype(jnp.bfloat16)


def body(
    tokens,
    lengths,
    ln1_gain,
    ln1_bias,
    qkv_weight,
    q_bias,
    v_bias,
    out_weight,
    out_bias,
    ln2_gain,
    ln2_bias,
    up_weight,
    up_bias,
    down_weight,
    down_bias,
    cotangent,
):
    attn_full = (
        lax.all_gather(ln1_gain, "fsdp", axis=0, tiled=True),
        lax.all_gather(ln1_bias, "fsdp", axis=0, tiled=True),
        lax.all_gather(qkv_weight, "fsdp", axis=0, tiled=True),
        lax.all_gather(q_bias, "fsdp", axis=0, tiled=True),
        lax.all_gather(v_bias, "fsdp", axis=0, tiled=True),
        lax.all_gather(out_weight, "fsdp", axis=0, tiled=True),
        lax.all_gather(out_bias, "fsdp", axis=0, tiled=True),
    )
    image_count, tok_rows, model_width = tokens.shape
    inputs = tokens.astype(jnp.float32)
    gain_one = attn_full[0].astype(jnp.float32)
    shift_one = attn_full[1].astype(jnp.float32)
    normed = norm_rows(inputs, gain_one, shift_one).astype(jnp.bfloat16)
    qkv_cube = attn_full[2].reshape(model_width, 3, model_width)
    joined_bias = jnp.stack([attn_full[3], jnp.zeros_like(attn_full[3]), attn_full[4]]).astype(
        jnp.float32
    )
    project = jnp.einsum("isd,dce->cise", normed, qkv_cube, preferred_element_type=jnp.float32)
    project = (project + joined_bias[:, None, None, :]).astype(jnp.bfloat16)
    by_heads = lax.all_to_all(project, "seq", split_axis=3, concat_axis=2, tiled=True)
    context_heads, log_total = lax.map(
        attend_forward, (by_heads[0], by_heads[1], by_heads[2], lengths)
    )
    context = lax.all_to_all(context_heads, "seq", split_axis=1, concat_axis=2, tiled=True)
    branch = jnp.einsum("isd,de->ise", context, attn_full[5], preferred_element_type=jnp.float32)
    middle = inputs + branch + attn_full[6].astype(jnp.float32)
    mlp_full = (
        lax.all_gather(ln2_gain, "fsdp", axis=0, tiled=True),
        lax.all_gather(ln2_bias, "fsdp", axis=0, tiled=True),
        lax.all_gather(up_weight, "fsdp", axis=0, tiled=True),
        lax.all_gather(up_bias, "fsdp", axis=0, tiled=True),
        lax.all_gather(down_weight, "fsdp", axis=0, tiled=True),
        lax.all_gather(down_bias, "fsdp", axis=0, tiled=True),
    )
    gain_two = mlp_full[0].astype(jnp.float32)
    shift_two = mlp_full[1].astype(jnp.float32)
    normed_two = norm_rows(middle, gain_two, shift_two).astype(jnp.bfloat16)
    before = jnp.einsum("isd,df->isf", normed_two, mlp_full[2], preferred_element_type=jnp.float32)
    before = before + mlp_full[3].astype(jnp.float32)
    hidden = gelu_exact(before).astype(jnp.bfloat16)
    feed_out = jnp.einsum("isf,fd->isd", hidden, mlp_full[4], preferred_element_type=jnp.float32)
    output = (middle + feed_out + mlp_full[5].astype(jnp.float32)).astype(jnp.bfloat16)
    mlp_back = (
        lax.all_gather(ln2_gain, "fsdp", axis=0, tiled=True),
        lax.all_gather(ln2_bias, "fsdp", axis=0, tiled=True),
        lax.all_gather(up_weight, "fsdp", axis=0, tiled=True),
        lax.all_gather(up_bias, "fsdp", axis=0, tiled=True),
        lax.all_gather(down_weight, "fsdp", axis=0, tiled=True),
        lax.all_gather(down_bias, "fsdp", axis=0, tiled=True),
    )
    grad_out = cotangent.astype(jnp.float32)
    g_down_bias = jnp.sum(grad_out, axis=(0, 1))
    g_down = jnp.einsum("isf,isd->fd", hidden, cotangent, preferred_element_type=jnp.float32)
    grad_hidden = jnp.einsum(
        "isd,fd->isf", cotangent, mlp_back[4], preferred_element_type=jnp.float32
    )
    unused_value, gelu_pull = jax.vjp(gelu_exact, before)
    grad_before = gelu_pull(grad_hidden)[0].astype(jnp.bfloat16)
    g_up_bias = jnp.sum(grad_before.astype(jnp.float32), axis=(0, 1))
    g_up = jnp.einsum("isd,isf->df", normed_two, grad_before, preferred_element_type=jnp.float32)
    grad_normed_two = jnp.einsum(
        "isf,df->isd", grad_before, mlp_back[2], preferred_element_type=jnp.float32
    )
    unused_norm, norm_pull = jax.vjp(
        norm_rows, middle, mlp_back[0].astype(jnp.float32), mlp_back[1].astype(jnp.float32)
    )
    grad_middle_part, g_ln2_gain, g_ln2_bias = norm_pull(grad_normed_two)
    mlp_shares = (
        lax.psum_scatter(g_ln2_gain, "fsdp", scatter_dimension=0, tiled=True),
        lax.psum_scatter(g_ln2_bias, "fsdp", scatter_dimension=0, tiled=True),
        lax.psum_scatter(g_up, "fsdp", scatter_dimension=0, tiled=True),
        lax.psum_scatter(g_up_bias, "fsdp", scatter_dimension=0, tiled=True),
        lax.psum_scatter(g_down, "fsdp", scatter_dimension=0, tiled=True),
        lax.psum_scatter(g_down_bias, "fsdp", scatter_dimension=0, tiled=True),
    )
    attn_back = (
        lax.all_gather(ln1_gain, "fsdp", axis=0, tiled=True),
        lax.all_gather(ln1_bias, "fsdp", axis=0, tiled=True),
        lax.all_gather(qkv_weight, "fsdp", axis=0, tiled=True),
        lax.all_gather(q_bias, "fsdp", axis=0, tiled=True),
        lax.all_gather(v_bias, "fsdp", axis=0, tiled=True),
        lax.all_gather(out_weight, "fsdp", axis=0, tiled=True),
        lax.all_gather(out_bias, "fsdp", axis=0, tiled=True),
    )
    grad_middle = grad_out + grad_middle_part
    grad_branch = grad_middle.astype(jnp.bfloat16)
    g_out_bias = jnp.sum(grad_branch.astype(jnp.float32), axis=(0, 1))
    g_out = jnp.einsum("isd,ise->de", context, grad_branch, preferred_element_type=jnp.float32)
    grad_context = jnp.einsum(
        "ise,de->isd", grad_branch, attn_back[5], preferred_element_type=jnp.float32
    ).astype(jnp.bfloat16)
    grad_heads = lax.all_to_all(grad_context, "seq", split_axis=2, concat_axis=1, tiled=True)
    grad_project_heads = lax.map(
        attend_backward, (by_heads[0], by_heads[1], by_heads[2], log_total, grad_heads, lengths)
    )
    grad_project = lax.all_to_all(
        grad_project_heads, "seq", split_axis=2, concat_axis=3, tiled=True
    )
    g_qkv = jnp.einsum("isd,icse->dce", normed, grad_project, preferred_element_type=jnp.float32)
    g_qkv = g_qkv.reshape(model_width, 3 * model_width)
    g_q_bias = jnp.sum(grad_project[:, 0].astype(jnp.float32), axis=(0, 1))
    g_v_bias = jnp.sum(grad_project[:, 2].astype(jnp.float32), axis=(0, 1))
    qkv_cube_back = attn_back[2].reshape(model_width, 3, model_width)
    grad_normed = jnp.einsum(
        "icse,dce->isd", grad_project, qkv_cube_back, preferred_element_type=jnp.float32
    )
    unused_first, norm_pull_one = jax.vjp(
        norm_rows, inputs, attn_back[0].astype(jnp.float32), attn_back[1].astype(jnp.float32)
    )
    grad_input_part, g_ln1_gain, g_ln1_bias = norm_pull_one(grad_normed)
    grad_tokens = (grad_middle + grad_input_part).astype(jnp.bfloat16)
    attn_shares = (
        lax.psum_scatter(g_ln1_gain, "fsdp", scatter_dimension=0, tiled=True),
        lax.psum_scatter(g_ln1_bias, "fsdp", scatter_dimension=0, tiled=True),
        lax.psum_scatter(g_qkv, "fsdp", scatter_dimension=0, tiled=True),
        lax.psum_scatter(g_q_bias, "fsdp", scatter_dimension=0, tiled=True),
        lax.psum_scatter(g_v_bias, "fsdp", scatter_dimension=0, tiled=True),
        lax.psum_scatter(g_out, "fsdp", scatter_dimension=0, tiled=True),
        lax.psum_scatter(g_out_bias, "fsdp", scatter_dimension=0, tiled=True),
    )
    summed = lax.psum(
        (
            attn_shares[0],
            attn_shares[1],
            attn_shares[2],
            attn_shares[3],
            attn_shares[4],
            attn_shares[5],
            attn_shares[6],
            mlp_shares[0],
            mlp_shares[1],
            mlp_shares[2],
            mlp_shares[3],
            mlp_shares[4],
            mlp_shares[5],
        ),
        "seq",
    )
    return (
        output,
        grad_tokens,
        summed[0],
        summed[1],
        summed[2],
        summed[3],
        summed[4],
        summed[5],
        summed[6],
        summed[7],
        summed[8],
        summed[9],
        summed[10],
        summed[11],
        summed[12],
    )


def solution(mesh):
    placed = (
        P("fsdp", "seq", None),
        P("fsdp"),
        P("fsdp"),
        P("fsdp"),
        P("fsdp", None),
        P("fsdp"),
        P("fsdp"),
        P("fsdp", None),
        P("fsdp"),
        P("fsdp"),
        P("fsdp"),
        P("fsdp", None),
        P("fsdp"),
        P("fsdp", None),
        P("fsdp"),
        P("fsdp", "seq", None),
    )
    return jax.shard_map(
        body,
        mesh=mesh,
        in_specs=placed,
        out_specs=(
            P("fsdp", "seq", None),
            P("fsdp", "seq", None),
            P("fsdp"),
            P("fsdp"),
            P("fsdp", None),
            P("fsdp"),
            P("fsdp"),
            P("fsdp", None),
            P("fsdp"),
            P("fsdp"),
            P("fsdp"),
            P("fsdp", None),
            P("fsdp"),
            P("fsdp", None),
            P("fsdp"),
        ),
        check_vma=False,
    )
```

profile of v0, /device:TPU:0, one launch (start us, length us, event | category | flops | bytes accessed | tf_op | source)
XLA Modules:
  0.0 1512.5 jit_solution(11763932829682902338)
XLA Ops:
  7.3 2.3 copy.93
  11.7 22.6 %all-gather = bf16[8,1,128]{2,1,0:T(2,128)(2,1)S(1)} all-gather(bf16[1,1,128]{2,1,0:T(2,128)(2,1)S(1)} %bitcast.217), channel_id=1, replica_groups=mesh['seq'=4,'fsdp'=8] {'fsdp'}, dimensions={0}, use_global_device_ids=true | all-gather | bytes 2304 | tf_op jit(solution)/shard_map/all_gather | solution.py:85
  34.4 17.0 %all-gather.1 = bf16[8,1,128]{2,1,0:T(2,128)(2,1)S(1)} all-gather(bf16[1,1,128]{2,1,0:T(2,128)(2,1)S(1)} %bitcast.218), channel_id=1, replica_groups=mesh['seq'=4,'fsdp'=8] {'fsdp'}, dimensions={0}, use_global_device_ids=true | all-gather | bytes 2304 | tf_op jit(solution)/shard_map/all_gather | solution.py:86
  51.5 18.4 %all-gather.2 = bf16[8,1,128]{2,1,0:T(2,128)(2,1)S(1)} all-gather(bf16[1,1,128]{2,1,0:T(2,128)(2,1)S(1)} %bitcast.219), channel_id=1, replica_groups=mesh['seq'=4,'fsdp'=8] {'fsdp'}, dimensions={0}, use_global_device_ids=true | all-gather | bytes 2304 | tf_op jit(solution)/shard_map/all_gather | solution.py:88
  69.9 18.2 %all-gather.3 = bf16[8,1,128]{2,1,0:T(2,128)(2,1)S(1)} all-gather(bf16[1,1,128]{2,1,0:T(2,128)(2,1)S(1)} %bitcast.220), channel_id=1, replica_groups=mesh['seq'=4,'fsdp'=8] {'fsdp'}, dimensions={0}, use_global_device_ids=true | all-gather | bytes 2304 | tf_op jit(solution)/shard_map/all_gather | solution.py:89
  89.2 23.9 %all-gather.14.cloned.1.call-done = bf16[1024,3072]{0,1:T(8,128)(2,1)} async-done(((bf16[128,3072]{0,1:T(8,128)(2,1)}), bf16[1024,3072]{0,1:T(8,128)(2,1)}) %all-gather.14.cloned.1.call-update) | async-done | bytes 6291472 | tf_op jit(solution)/shard_map/all_gather | solution.py:87
  113.0 4.8 fusion.41
  117.9 3.9 copy.95
  121.7 4.6 all-to-all-start
  127.0 36.3 %all-to-all-done = bf16[3,1,258,1024]{2,0,1,3:T(4,128)(2,1)} async-done(((bf16[3,1,258,1024]{2,0,1,3:T(4,128)(2,1)}), bf16[3,1,258,1024]{2,0,1,3:T(4,128)(2,1)}, u32[]{:S(2)}, u32[]{:S(2)}) %all-to-all-start) | async-done | bytes 1585184 | tf_op jit(solution)/shard_map/all_to_all | solution.py:104
  163.3 4.1 copy.128
  167.5 1.7 fusion.85
  169.2 1.9 reshape.484
  172.1 8.6 fusion.86
  180.8 9.1 fusion.7
  189.8 9.9 fusion.33
  199.7 2.1 copy.98
  202.4 5.7 reduce.20
  209.0 3.5 all-to-all-start.1
  212.5 18.6 %all-gather.4 = bf16[8,1,128]{2,1,0:T(2,128)(2,1)S(1)} all-gather(bf16[1,1,128]{2,1,0:T(2,128)(2,1)S(1)} %bitcast.221), channel_id=1, replica_groups=mesh['seq'=4,'fsdp'=8] {'fsdp'}, dimensions={0}, use_global_device_ids=true | all-gather | bytes 2304 | tf_op jit(solution)/shard_map/all_gather | solution.py:91
  231.2 17.2 %all-gather.5 = bf16[8,1,128]{2,1,0:T(2,128)(2,1)S(1)} all-gather(bf16[1,1,128]{2,1,0:T(2,128)(2,1)S(1)} %bitcast.222), channel_id=1, replica_groups=mesh['seq'=4,'fsdp'=8] {'fsdp'}, dimensions={0}, use_global_device_ids=true | all-gather | bytes 2304 | tf_op jit(solution)/shard_map/all_gather | solution.py:112
  248.3 18.5 %all-gather.6 = bf16[8,1,128]{2,1,0:T(2,128)(2,1)S(1)} all-gather(bf16[1,1,128]{2,1,0:T(2,128)(2,1)S(1)} %bitcast.223), channel_id=1, replica_groups=mesh['seq'=4,'fsdp'=8] {'fsdp'}, dimensions={0}, use_global_device_ids=true | all-gather | bytes 2304 | tf_op jit(solution)/shard_map/all_gather | solution.py:113
  266.8 26.9 %all-gather.7 = bf16[8,1,512]{2,1,0:T(2,128)(2,1)S(1)} all-gather(bf16[1,1,512]{2,1,0:T(2,128)(2,1)S(1)} %reshape.505), channel_id=1, replica_groups=mesh['seq'=4,'fsdp'=8] {'fsdp'}, dimensions={0}, use_global_device_ids=true | all-gather | bytes 9216 | tf_op jit(solution)/shard_map/all_gather | solution.py:115
  295.0 5.5 bitcast_reduce_fusion.1
  301.2 2.5 fusion.87
  304.0 16.2 %multiply_convert_fusion = (bf16[258,4096]{1,0:T(8,128)(2,1)}, f32[258,4096]{1,0:T(8,128)}, f32[258,4096]{1,0:T(8,128)}) fusion(f32[4096]{0:T(1024)S(1)} %bitcast.214, bf16[1024,4096]{1,0:T(8,128)(2,1)} %all-gather.18.cloned.1.call-done, f32[1,258,1024]{2,1,0:T(8,128)S(1)} %get-tuple-element.102, f32[1024]{0:T(1024)S(1)} %bitcast.208, ...), kind=kOutput, calls=%fused_computation.25 | convolution fusion | flops 2235328512 | bytes 20039696 | tf_op jit(solution)/shard_map/isd,df->isf/dot_general | solution.py:122
  320.2 92.4 %all-gather.20.cloned.1.call-done = bf16[4096,1024]{1,0:T(8,128)(2,1)} async-done(((bf16[512,1024]{1,0:T(8,128)(2,1)}), bf16[4096,1024]{1,0:T(8,128)(2,1)}) %all-gather.20.cloned.1.call-update) | async-done | bytes 8388624 | tf_op jit(solution)/shard_map/all_gather | solution.py:116
  412.6 12.1 convert_reduce_fusion
  424.8 2.8 fusion.54
  429.3 3.4 fusion.58
  432.7 3.2 fusion.46
  435.8 4.0 copy.100
  439.8 6.6 reduce.21
  446.4 3.7 reshape.533
  450.1 4.2 all-to-all-start.2
  454.4 8.8 all-to-all-done.2
  463.2 3.3 reshape.534
  466.6 3.2 copy.101
  472.8 10.5 fusion.34
  483.3 3.3 copy.108
  486.6 10.5 fusion.88
  497.1 27.6 %fusion.27 = bf16[4,64,1032]{2,1,0:T(8,128)(2,1)} fusion(bf16[1032,4,64]{0,2,1:T(8,128)(2,1)} %copy-done.9, f32[4,1032,1032]{1,2,0:T(8,128)} %fusion.88, f32[4,1032,1032]{1,2,0:T(8,128)} %get-tuple-element.100, f32[4,1032]{1,0:T(4,128)S(1)} %log_add_fusion), kind=kOutput, calls=%fused_computation.41 | convolution fusion | flops 575382336 | bytes 35154048 | tf_op jit(solution)/shard_map/while/body/eval_jaxpr/hqk,khd->qhd/dot_general | solution.py:55
  524.7 3.7 copy.106
  528.5 26.8 %fusion.30 = bf16[4,64,1032]{2,1,0:T(8,128)(2,1)} fusion(bf16[1032,4,64]{0,2,1:T(8,128)(2,1)S(1)} %copy-done.8, f32[4,1032,1032]{1,2,0:T(8,128)} %fusion.88, f32[4,1032,1032]{1,2,0:T(8,128)} %get-tuple-element.100, f32[4,1032]{1,0:T(4,128)S(1)} %log_add_fusion), kind=kOutput, calls=%fused_computation.42 | convolution fusion | flops 575382336 | bytes 35154048 | tf_op jit(solution)/shard_map/while/body/eval_jaxpr/hqk,qhd->khd/dot_general | solution.py:58
  555.3 3.7 copy.107
  559.0 5.0 pad_maximum_fusion
  564.0 28.3 %all_to_all.63 = bf16[1,3,1032,256]{3,1,0,2:T(4,128)(2,1)S(1)} all-to-all(bf16[1,3,1032,256]{3,1,0,2:T(4,128)(2,1)S(1)} %pad_maximum_fusion), channel_id=1, replica_groups=mesh['seq'=4,'fsdp'=8] {'seq'}, dimensions={2} | all-to-all | bytes 3170304 | tf_op jit(solution)/shard_map/all_to_all | solution.py:180
  593.2 2.2 reshape.490
  595.4 2.8 copy.129
  599.8 6.6 fusion.68
  606.5 10.3 fusion.79
  616.9 12.0 fusion.61
  629.0 182.3 %reduce-scatter.5.cloned.1.call-done = f32[128,3072]{1,0:T(8,128)} async-done(((f32[1024,3072]{1,0:T(8,128)}), f32[128,3072]{1,0:T(8,128)}) %reduce-scatter.5.cloned.1.call-update) | async-done | bytes 1572880 | tf_op jit(solution)/shard_map/reduce_scatter | solution.py:199
  811.3 282.4 %reduce-scatter.9.cloned.1.call-done = f32[128,4096]{1,0:T(8,128)} async-done(((f32[1024,4096]{1,0:T(8,128)}), f32[128,4096]{1,0:T(8,128)}) %reduce-scatter.9.cloned.1.call-update) | async-done | bytes 2097168 | tf_op jit(solution)/shard_map/reduce_scatter | solution.py:155
  1093.7 283.1 %reduce-scatter.11.cloned.1.call-done = f32[512,1024]{1,0:T(8,128)} async-done(((f32[4096,1024]{1,0:T(8,128)}), f32[512,1024]{1,0:T(8,128)}) %reduce-scatter.11.cloned.1.call-update) | async-done | bytes 2097168 | tf_op jit(solution)/shard_map/reduce_scatter | solution.py:157
  1378.7 18.6 %all-gather.8 = bf16[8,1,128]{2,1,0:T(2,128)(2,1)S(1)} all-gather(bf16[1,1,128]{2,1,0:T(2,128)(2,1)S(1)} %bitcast.224), channel_id=1, replica_groups=mesh['seq'=4,'fsdp'=8] {'fsdp'}, dimensions={0}, use_global_device_ids=true | all-gather | bytes 2304 | tf_op jit(solution)/shard_map/all_gather | solution.py:117
  1398.7 7.4 fusion.45
  1406.0 2.4 all_to_all.58
  1408.4 5.5 fusion.53
  1416.6 33.5 %all-reduce.9 = (f32[1024]{0:T(1024)S(1)}, f32[1024]{0:T(1024)S(1)}, f32[1024]{0:T(1024)S(1)}, f32[1024]{0:T(1024)S(1)}, f32[1024]{0:T(1024)S(1)}, /*index=5*/f3...) all-reduce(f32[1024]{0:T(1024)S(1)} %get-tuple-element.62, ...), channel_id=2, replica_groups=mesh['seq'=4,'fsdp'=8] {'fsdp'}, use_global_device_ids=true, to_apply=%region_12.13.clone | all-reduce | flops 12288 | bytes 98304
  1450.8 7.3 all-reduce.10
  1458.1 40.3 %all-reduce.14.cloned.1.call-done = (f32[128,3072]{1,0:T(8,128)}, f32[128,1024]{1,0:T(8,128)}, f32[128,4096]{1,0:T(8,128)}, f32[512,1024]{1,0:T(8,128)}) async-done(((f32[128,3072]{1,0:T(8,128)}, f32[128,1024]{1,0:T(8,128)}, f32[128,4096]{1,0:T(8,128)}, f32[512,1024]{1,0:T(8,128)}), (f32[128,3072]{1,0:T(8,128)}, f32[128,1024]{1,0:T(8,128)}, f32[128,4096]{1,0:T(8,128)}, ...) | async-done | bytes 6291472 | tf_op jit(solution)/shard_map/psum | solution.py:205
  1498.4 2.9 copy.137
  1501.3 1.9 copy.138
  (134 shorter events, 23.4 us)
Async XLA Ops:
  7.2 4.5 copy-start.17
  7.2 27.2 %copy-start.18 = (bf16[128]{0:T(256)(128)(2,1)S(1)}, bf16[128]{0:T(256)(128)(2,1)}, u32[]{:S(2)}) copy-start(bf16[128]{0:T(256)(128)(2,1)} %param.19) | copy-start | bytes 772
  7.2 44.3 %copy-start.19 = (bf16[128]{0:T(256)(128)(2,1)S(1)}, bf16[128]{0:T(256)(128)(2,1)}, u32[]{:S(2)}) copy-start(bf16[128]{0:T(256)(128)(2,1)} %param.21) | copy-start | bytes 772
  7.2 62.6 %copy-start.20 = (bf16[128]{0:T(256)(128)(2,1)S(1)}, bf16[128]{0:T(256)(128)(2,1)}, u32[]{:S(2)}) copy-start(bf16[128]{0:T(256)(128)(2,1)} %param.22) | copy-start | bytes 772
  7.2 80.8 %copy-start = (bf16[1,258,1024]{2,1,0:T(8,128)(2,1)S(1)}, bf16[1,258,1024]{2,1,0:T(8,128)(2,1)}, u32[]{:S(2)}) copy-start(bf16[1,258,1024]{2,1,0:T(8,128)(2,1)} %param.16) | copy-start | bytes 1585156
  7.2 105.8 %all-gather.14.cloned.1.call-start = ((), (), s32[]{:S(2)}) async-start(), calls=%async_computation.8 | async-start | bytes 7077888 | tf_op jit(solution)/shard_map/all_gather | solution.py:87
  9.6 291.6 %all-gather.16.cloned.1.call-start = ((), (), s32[]{:S(2)}) async-start(), calls=%async_computation.9 | async-start | bytes 2359296 | tf_op jit(solution)/shard_map/all_gather | solution.py:90
  10.4 293.6 %all-gather.18.cloned.1.call-start = ((), (), s32[]{:S(2)}) async-start(), calls=%async_computation.10 | async-start | bytes 9437184 | tf_op jit(solution)/shard_map/all_gather | solution.py:114
  11.1 401.5 %all-gather.20.cloned.1.call-start = ((), (), s32[]{:S(2)}) async-start(), calls=%async_computation.11 | async-start | bytes 9437184 | tf_op jit(solution)/shard_map/all_gather | solution.py:116
  88.5 0.6 copy-start.14
  121.7 41.6 %all-to-all-start = ((bf16[3,1,258,1024]{2,0,1,3:T(4,128)(2,1)}), bf16[3,1,258,1024]{2,0,1,3:T(4,128)(2,1)}, u32[]{:S(2)}, u32[]{:S(2)}) async-start(bf16[3,1,258,1024]{2,0,1,3:T(4,128)(2,1)} %copy.95), calls=%async_computation | async-start | bytes 6291456 | tf_op jit(solution)/shard_map/all_to_all | solution.py:104
  171.0 9.7 copy-start.9
  171.6 9.2 copy-start.7
  172.1 17.7 %copy-start.10 = (bf16[1032,4,64]{0,2,1:T(8,128)(2,1)}, bf16[1032,4,64]{0,2,1:T(8,128)(2,1)S(1)}, u32[]{:S(2)}) copy-start(bf16[1032,4,64]{0,2,1:T(8,128)(2,1)S(1)} %reshape.482) | copy-start | bytes 1585156
  199.7 12.8 copy-start.16
  199.7 12.8 copy-start.21
  199.7 31.4 %copy-start.22 = (bf16[128]{0:T(256)(128)(2,1)S(1)}, bf16[128]{0:T(256)(128)(2,1)}, u32[]{:S(2)}) copy-start(bf16[128]{0:T(256)(128)(2,1)} %param.25) | copy-start | bytes 772
  199.7 48.6 %copy-start.23 = (bf16[128]{0:T(256)(128)(2,1)S(1)}, bf16[128]{0:T(256)(128)(2,1)}, u32[]{:S(2)}) copy-start(bf16[128]{0:T(256)(128)(2,1)} %param.26) | copy-start | bytes 772
  209.0 84.8 %all-to-all-start.1 = ((bf16[4,2,33024]{2,1,0:T(2,128)(2,1)}), bf16[4,2,33024]{2,1,0:T(2,128)(2,1)S(1)}, u32[]{:S(2)}, u32[]{:S(2)}) async-start(bf16[4,2,33024]{2,1,0:T(2,128)(2,1)} %reshape.531), calls=%async_computation.1 | async-start | bytes 1056768 | tf_op jit(solution)/shard_map/all_to_all | solution.py:108
  212.4 416.6 %reduce-scatter.7.cloned.1.call-start = ((), (), s32[]{:S(2)}) async-start(), calls=%async_computation.13 | async-start | bytes 4718592 | tf_op jit(solution)/shard_map/reduce_scatter | solution.py:202
  304.0 108.6 %copy-start.3 = (bf16[1,258,1024]{2,1,0:T(8,128)(2,1)S(1)}, bf16[1,258,1024]{2,1,0:T(8,128)(2,1)}, u32[]{:S(2)}) copy-start(bf16[1,258,1024]{2,1,0:T(8,128)(2,1)} %param.31) | copy-start | bytes 1585156
  412.6 12.1 copy-start.25
  424.8 2.8 copy-start.11
  427.6 1.7 copy-start.6
  428.0 1.0 copy-start.1
  450.1 13.1 all-to-all-start.2
  454.3 357.0 %reduce-scatter.5.cloned.1.call-start = ((), (), s32[]{:S(2)}) async-start(), calls=%async_computation.12 | async-start | bytes 14155776 | tf_op jit(solution)/shard_map/reduce_scatter | solution.py:199
  497.1 31.4 %copy-start.8 = (bf16[1032,4,64]{0,2,1:T(8,128)(2,1)S(1)}, bf16[1032,4,64]{0,2,1:T(8,128)(2,1)}, u32[]{:S(2)}) copy-start(bf16[1032,4,64]{0,2,1:T(8,128)(2,1)} %copy-done.7) | copy-start | bytes 1585156
  606.5 487.2 %reduce-scatter.9.cloned.1.call-start = ((), (), s32[]{:S(2)}) async-start(), calls=%async_computation.14 | async-start | bytes 18874368 | tf_op jit(solution)/shard_map/reduce_scatter | solution.py:155
  616.9 759.9 %reduce-scatter.11.cloned.1.call-start = ((), (), s32[]{:S(2)}) async-start(), calls=%async_computation.15 | async-start | bytes 18874368 | tf_op jit(solution)/shard_map/reduce_scatter | solution.py:157
  628.9 747.9 %copy-start.26 = (u32[32]{0:T(128)S(1)}, u32[32]{0:T(128)}, u32[]{:S(2)}) copy-start(u32[32]{0:T(128)} %constant.129) | copy-start | bytes 388
  629.0 749.7 %copy-start.24 = (bf16[128]{0:T(256)(128)(2,1)S(1)}, bf16[128]{0:T(256)(128)(2,1)}, u32[]{:S(2)}) copy-start(bf16[128]{0:T(256)(128)(2,1)} %param.30) | copy-start | bytes 772
  629.0 869.4 %all-reduce.14.cloned.1.call-start = ((), (), s32[]{:S(2)}) async-start(), calls=%async_computation.16 | async-start | bytes 12582912 | tf_op jit(solution)/shard_map/psum | solution.py:205
  1408.4 5.6 copy-start.5
  1408.4 5.9 copy-start.15
  1408.4 6.6 copy-start.4
  1414.0 1.3 copy-start.2
  1498.4 4.7 copy-start.13
  1498.4 6.1 copy-start.12
Sparse Core Ops, SparseCore 0:
  10.7 102.3 all-gather.13
  115.2 47.2 all-gather.15
  164.6 123.2 all-gather.17
  289.9 122.7 all-gather.19
  432.8 86.5 reduce-scatter.6
  606.6 204.6 reduce-scatter.4
  815.1 278.5 reduce-scatter.8
  1097.5 279.2 reduce-scatter.10
  1379.4 118.9 all-reduce.13
where the time goes:
time: 1520 us; the launch traced here: 1510 us
  waiting for transfers between devices  952 us (63%)
  blocking collectives  245 us (16%)
  matrix products  181 us (12%)
  local copies, waits for them, and re-layouts  74.3 us (5%)
  other arithmetic  31.7 us (2%)
  between operations  16.6 us (1%)
    reduce_scatter x1, waiting for transfers between devices, body(): lax.psum_scatter(g_down, 'fsdp', scatter_dimension=0, tiled=True)  283 us
    reduce_scatter x1, waiting for transfers between devices, body(): lax.psum_scatter(g_up, 'fsdp', scatter_dimension=0, tiled=True)  282 us
    reduce_scatter x1, waiting for transfers between devices, body(): lax.psum_scatter(g_qkv, 'fsdp', scatter_dimension=0, tiled=True)  182 us
    all_gather x1, waiting for transfers between devices, body(): lax.all_gather(down_weight, 'fsdp', axis=0, tiled=True)  92.4 us
    psum x1, waiting for transfers between devices, body(): lax.psum((attn_shares[0], attn_shares[1], attn_shares[2], attn_shares[3],...  40.3 us
    all_to_all x1, waiting for transfers between devices, body(): lax.all_to_all(project, 'seq', split_axis=3, concat_axis=2, tiled=True)  36.3 us
    unnamed x1, blocking collectives  33.5 us
  transfers between devices with their start and end apart: 12, of which 8 were waited for; matrix products, arithmetic and copies ran while one was open for 17% of the time, Pallas kernels for 0%

commit v1 on v0

v1 whole, which is shorter than its diff:
```python
import functools
import math

import jax
import jax.numpy as jnp
from jax import lax
from jax.experimental import pallas as pl
from jax.experimental.pallas import tpu as pltpu
from jax.sharding import PartitionSpec as P

HEAD_DIM = 64
BF = jnp.bfloat16
F32 = jnp.float32
MESH = pl.DeviceIdType.MESH


def dot_nn(left, right):
    return lax.dot_general(left, right, (((1,), (0,)), ((), ())), preferred_element_type=F32)


def dot_nt(left, right):
    return lax.dot_general(left, right, (((1,), (1,)), ((), ())), preferred_element_type=F32)


def dot_tn(left, right):
    return lax.dot_general(left, right, (((0,), (0,)), ((), ())), preferred_element_type=F32)


def unit_rows(values):
    center = values - jnp.mean(values, axis=-1, keepdims=True)
    rate = lax.rsqrt(jnp.mean(center * center, axis=-1, keepdims=True) + 1e-6)
    return center * rate, rate


def norm_pull(grad, gain, unit, rate):
    scaled = grad * gain
    return rate * (
        scaled
        - jnp.mean(scaled, axis=-1, keepdims=True)
        - unit * jnp.mean(scaled * unit, axis=-1, keepdims=True)
    )


def layer_kernel(
    z,
    tok, cot, mask, sm_in, qkv_in, out_in, up_in, dn_in,
    o_out, o_tok, o_qkv, o_ow, o_up, o_dn, o_sm,
    xg, cg, nrm, ctx, n2, hid, gbf, pq, wqkv, wout, wup, wdn, smg, vec, gvec, lse, mid, gmid,
    gctx, dqkv, dkt, dvt, gpart, gown, grecv, opart, oown, orecv,
    dw_qkv, dw_out, dw_up, dw_dn, dw_sm, xr_qkv, xr_out, xr_up, xr_dn, xr_sm,
    zr_qkv, zr_out, zr_up, zr_dn, zr_sm,
    loc_sem, ag_zs, ag_zr, ag_xs, ag_xr, sq_s, sq_r, rs_s, rs_r, fx_s, fx_r, fz_s, fz_r,
):
    D, T, TP, R, A, w, wf, HP = z["D"], z["T"], z["TP"], z["R"], z["A"], z["w"], z["wf"], z["HP"]
    N, DH, LB, g = 2 * A, D // 4, D // 128, z["g"]
    half = D // 2
    s = lax.axis_index("seq")
    f = lax.axis_index("fsdp")
    y, c = lax.div(s, 2), lax.rem(s, 2)
    a, b = lax.div(f, 2), lax.rem(f, 2)
    s_core, s_y, s_diag = y * 2 + 1 - c, (1 - y) * 2 + c, (1 - y) * 2 + 1 - c
    f_x = a * 2 + 1 - b
    to_core, to_y, to_x = {"seq": s_core}, {"seq": s_y}, {"fsdp": f_x}

    def up_z(d):
        return lax.rem(a + d, A)

    def from_z(d):
        return lax.rem(a - d + A, A)

    started = []

    def send(src, dst, ssem, rsem, dev, keep=True, kind=None):
        copy = pltpu.make_async_remote_copy(
            src_ref=src, dst_ref=dst, send_sem=ssem, recv_sem=rsem, device_id=dev, device_id_type=MESH
        )
        copy.start()
        if keep:
            started.append((copy, kind))

    def arrive(dst, rsem, dev):
        pltpu.make_async_remote_copy(
            src_ref=dst, dst_ref=dst, send_sem=rsem, recv_sem=rsem, device_id=dev, device_id_type=MESH
        ).wait_recv()

    def rows_of(k, size):
        return pl.ds(pl.multiple_of(k * size, size), size)

    core_cols = pl.ds(pl.multiple_of(c * half, half), half)
    blocks = {
        0: lambda k: smg.at[k],
        1: lambda k: wqkv.at[rows_of(k, w)],
        2: lambda k: wout.at[rows_of(k, w), core_cols],
        3: lambda k: wup.at[rows_of(k, w)],
        4: lambda k: wdn.at[rows_of(k, wf)],
    }

    def ag_z(m):
        for d in range(1, A):
            send(blocks[m](f), blocks[m](f), ag_zs.at[m, d - 1], ag_zr.at[m, d - 1], {"fsdp": up_z(d) * 2 + b})

    def ag_x(m):
        send(blocks[m](f), blocks[m](f), ag_xs.at[m, 0], ag_xr.at[m, 0], to_x)

    def ag_relay(m):
        for d in range(1, A):
            k = from_z(d) * 2 + b
            arrive(blocks[m](k), ag_zr.at[m, d - 1], to_x)
            send(blocks[m](k), blocks[m](k), ag_xs.at[m, d], ag_xr.at[m, d], to_x)

    def ag_wait(m):
        for d in range(A):
            arrive(blocks[m](from_z(d) * 2 + 1 - b), ag_xr.at[m, d], to_x)

    def sq_send(kind, ref):
        send(ref(s), ref(s), sq_s.at[kind, 0], sq_r.at[kind, 0], to_core, kind=kind)
        send(ref(s), ref(s), sq_s.at[kind, 1], sq_r.at[kind, 1], to_y, kind=kind)

    def sq_core(kind, ref):
        arrive(ref(s_core), sq_r.at[kind, 0], to_core)

    def sq_relay(kind, ref):
        arrive(ref(s_y), sq_r.at[kind, 1], to_y)
        send(ref(s_y), ref(s_y), sq_s.at[kind, 2], sq_r.at[kind, 2], to_core, kind=kind)

    def sq_diag(kind, ref):
        arrive(ref(s_diag), sq_r.at[kind, 2], to_core)

    def x_slot(k):
        return xg.at[k]

    def c_slot(k):
        return cg.at[k]

    def ctx_slot(hp):
        return lambda k: ctx.at[k, :, hp * 128 : hp * 128 + 128]

    KX, KC, KG, KO, KCTX, KFIN = 0, 1, 2, 3, 4, 4 + HP

    def order(i):
        hb, lb = lax.div(3 - i, 2), lax.rem(3 - i, 2)
        return lax.rem(y + hb, 2) * 2 + lax.rem(c + lb, 2)

    def seq_stage(i, kind, part, own, recv, value):
        @pl.when(i < 3)
        def _():
            part[jnp.minimum(i, 2)] = value.astype(BF)

        @pl.when(i == 0)
        def _():
            send(part.at[0], recv.at[0], rs_s.at[kind, 0], rs_r.at[kind, 0], to_core, keep=False)

        @pl.when(i == 1)
        def _():
            arrive(recv.at[0], rs_r.at[kind, 0], to_core)
            part[1] = (part[1].astype(F32) + recv[0].astype(F32)).astype(BF)
            send(part.at[1], recv.at[1], rs_s.at[kind, 1], rs_r.at[kind, 1], to_y, keep=False)

        @pl.when(i == 2)
        def _():
            send(part.at[2], recv.at[2], rs_s.at[kind, 2], rs_r.at[kind, 2], to_core, keep=False)

        @pl.when(i == 3)
        def _():
            own[...] = value

    def seq_sent(kind, part):
        for j in range(3):
            pltpu.make_async_remote_copy(
                src_ref=part.at[j], dst_ref=part.at[j], send_sem=rs_s.at[kind, j], recv_sem=rs_r.at[kind, j],
                device_id=to_core, device_id_type=MESH,
            ).wait_send()

    def seq_total(kind, own, recv):
        arrive(recv.at[2], rs_r.at[kind, 2], to_core)
        arrive(recv.at[1], rs_r.at[kind, 1], to_y)
        return own[...] + recv[2].astype(F32) + recv[1].astype(F32)

    grads = {0: (dw_sm, xr_sm, zr_sm, o_sm), 1: (dw_dn, xr_dn, zr_dn, o_dn), 2: (dw_up, xr_up, zr_up, o_up), 3: (dw_out, xr_out, zr_out, o_ow)}
    for hp in range(HP):
        grads[4 + hp] = (dw_qkv.at[hp], xr_qkv.at[hp], zr_qkv.at[hp], o_qkv.at[hp])

    def rs_x(m):
        dw, xr, zr, out = grads[m]
        send(dw.at[:, 1 - b], xr, fx_s.at[m], fx_r.at[m], to_x)

    def rs_mid(m):
        dw, xr, zr, out = grads[m]
        arrive(xr, fx_r.at[m], to_x)
        dw[:, b] = (dw[:, b].astype(F32) + xr[...].astype(F32)).astype(dw.dtype)
        for d in range(1, A):
            k = up_z(d)
            send(dw.at[k, b], zr.at[d - 1], fz_s.at[m, d - 1], fz_r.at[m, d - 1], {"fsdp": k * 2 + b})

    def fin_slot(m):
        return lambda k: grads[m][3].at[k]

    def rs_fin(m):
        dw, xr, zr, out = grads[m]
        total = dw[a, b].astype(F32)
        for d in range(1, A):
            arrive(zr.at[d - 1], fz_r.at[m, d - 1], {"fsdp": from_z(d) * 2 + b})
            total = total + zr[d - 1].astype(F32)
        out[s] = total.astype(out.dtype)
        sq_send(KFIN + m, fin_slot(m))

    local = []

    def bring(src, dst):
        copy = pltpu.make_async_copy(src, dst, loc_sem.at[len(local)])
        copy.start()
        local.append(copy)

    bring(sm_in, smg.at[f])
    for hp in range(HP):
        for part in range(3):
            cols = pl.ds(pl.multiple_of(part * D + s * DH + hp * 128, 128), 128)
            lo = hp * 384 + part * 128
            bring(qkv_in.at[:, cols], wqkv.at[rows_of(f, w), lo : lo + 128])
    bring(out_in.at[:, core_cols], wout.at[rows_of(f, w), core_cols])
    if z["up_whole"]:
        for k in range(N):
            cols = pl.ds(pl.multiple_of((k * 4 + s) * wf, wf), wf)
            bring(up_in.at[:, cols], wup.at[rows_of(f, w), k * wf : (k + 1) * wf])
    else:
        bring(up_in, wup.at[rows_of(f, w)])
    bring(dn_in.at[rows_of(s, wf)], wdn.at[rows_of(f, wf)])

    def padded(ref):
        return jnp.concatenate([ref[...].astype(F32), jnp.zeros((TP - T, D), F32)], axis=0)

    xg[s] = padded(tok).astype(BF)
    cg[s] = padded(cot).astype(BF)
    gvec[...] = jnp.zeros_like(gvec)

    barrier = pltpu.get_barrier_semaphore()
    peers = [to_core, to_y, {"seq": s_diag}, to_x] + [{"fsdp": up_z(d) * 2 + b} for d in range(1, A)]
    for dev in peers:
        pl.semaphore_signal(barrier, inc=1, device_id=dev, device_id_type=MESH)
    for copy in local:
        copy.wait()
    pl.semaphore_wait(barrier, len(peers))

    ag_z(0)
    ag_x(0)
    sq_send(KX, x_slot)
    ag_z(1)
    ag_x(1)
    ag_z(2)
    ag_z(3)
    ag_z(4)
    ag_relay(0)
    ag_wait(0)
    for j in range(LB):
        piece = smg[j * g].astype(F32)
        for i in range(1, g):
            piece = piece + smg[j * g + i].astype(F32)
        vec[:, j * 128 : (j + 1) * 128] = piece

    def row(k):
        return vec[k : k + 1, :]

    def first_norm(k):
        unit, _ = unit_rows(xg[k].astype(F32))
        nrm[k] = (unit * row(0) + row(1)).astype(BF)

    first_norm(s)
    sq_core(KX, x_slot)
    first_norm(s_core)
    sq_relay(KX, x_slot)
    sq_send(KC, c_slot)
    first_norm(s_y)
    ag_relay(1)
    ag_x(2)
    sq_diag(KX, x_slot)
    first_norm(s_diag)
    ag_wait(1)

    pieces = []
    for hp in range(HP):
        cols = pl.ds(pl.multiple_of(s * DH + hp * 128, 128), 128)
        pieces += [vec[2:3, cols], jnp.zeros((1, 128), F32), vec[3:4, cols]]
    proj_bias = jnp.concatenate(pieces, axis=1)
    lanes = lax.broadcasted_iota(jnp.int32, (1, HP * 384), 1)
    proj_scale = jnp.where(lax.rem(lanes, 384) < 128, HEAD_DIM ** (-0.5), 1.0).astype(F32)

    @pl.loop(0, 4)
    def _(k):
        value = dot_nn(nrm[k], wqkv[...]) + proj_bias
        pq[k] = (value * proj_scale).astype(BF)

    flat = pq.reshape(R, HP * 384)
    lane = lax.broadcasted_iota(jnp.int32, (1, 128), 1)
    first = (lane < HEAD_DIM).astype(F32)
    picks = (first.astype(BF), (1.0 - first).astype(BF))

    def tiles(fn):
        full = R // 256

        @pl.loop(0, full)
        def _(i):
            fn(pl.ds(pl.multiple_of(i * 256, 256), 256), 256)

        if R % 256:
            fn(pl.ds(full * 256, R % 256), R % 256)

    ctx_rows = ctx.reshape(4 * R, DH)

    def forward_tile(hp, rows, count, start):
        lo = hp * 384
        query = flat[rows, lo : lo + 128]
        keys = flat[:, lo + 128 : lo + 256]
        vals = flat[:, lo + 256 : lo + 384]
        both = []
        for h in range(2):
            scores = dot_nt(query * picks[h], keys) + mask[...]
            top = jnp.max(scores, axis=-1, keepdims=True)
            grown = jnp.exp(scores - top)
            total = jnp.sum(grown, axis=-1, keepdims=True)
            lse[hp * 2 + h, rows, :] = top + jnp.log(total)
            both.append(dot_nn((grown * (1.0 / total)).astype(BF), vals))
        here = jnp.where(lane < HEAD_DIM, both[0], both[1]).astype(BF)
        ctx_rows[pl.ds(pl.multiple_of(s * R + start, 16), count), hp * 128 : hp * 128 + 128] = here

    def attend_forward(hp):
        full = R // 256

        @pl.loop(0, full)
        def _(i):
            forward_tile(hp, pl.ds(pl.multiple_of(i * 256, 256), 256), 256, i * 256)

        if R % 256:
            forward_tile(hp, pl.ds(full * 256, R % 256), R % 256, full * 256)

    for hp in range(HP):
        attend_forward(hp)
        sq_send(KCTX + hp, ctx_slot(hp))
        if hp == 0:
            ag_relay(2)
            sq_relay(KC, c_slot)
    ag_x(3)
    ag_wait(2)
    send(wout.at[:, core_cols], wout.at[:, core_cols], sq_s.at[KO, 0], sq_r.at[KO, 0], to_core)
    for hp in range(HP):
        sq_core(KCTX + hp, ctx_slot(hp))
        sq_relay(KCTX + hp, ctx_slot(hp))
    ag_relay(3)
    ag_x(4)
    other_cols = pl.ds(pl.multiple_of((1 - c) * half, half), half)
    arrive(wout.at[:, other_cols], sq_r.at[KO, 0], to_core)
    for hp in range(HP):
        sq_diag(KCTX + hp, ctx_slot(hp))

    @pl.loop(0, 4)
    def _(i):
        k = order(i)
        rows = pl.ds(pl.multiple_of(k * TP, 16), TP)
        joined = jnp.concatenate([ctx[j, rows, :] for j in range(4)], axis=1)
        value = xg[k].astype(F32) + dot_nn(joined, wout[...]) + row(4)
        unit, _ = unit_rows(value)
        n2[k] = (unit * row(5) + row(6)).astype(BF)

        @pl.when(i == 3)
        def _():
            mid[...] = value

    for copy in [copy for copy, kind in started if kind == KX]:
        copy.wait_send()
    ag_relay(4)
    sq_core(KC, c_slot)
    sq_diag(KC, c_slot)
    ag_wait(3)
    ag_wait(4)

    @pl.loop(0, 4)
    def _(i):
        k = order(i)
        before = dot_nn(n2[k], wup[...]) + row(8)
        cdf = 0.5 + 0.5 * lax.erf(before * (0.5**0.5))
        slope = cdf + before * (jnp.exp(before * before * -0.5) * (1.0 / math.sqrt(2.0 * math.pi)))
        hid[k] = (before * cdf).astype(BF)
        grad = (dot_nt(cg[k], wdn[...]) * slope).astype(BF)
        gbf[k] = grad
        gvec[8:9, :] += jnp.sum(grad.astype(F32), axis=0, keepdims=True)
        seq_stage(i, 0, gpart, gown, grecv, dot_nt(grad, wup[...]))
        seq_stage(i, 1, opart, oown, orecv, dot_nn(hid[k], wdn[...]))

    gn = seq_total(0, gown, grecv)
    seq_sent(0, gpart)
    unit, rate = unit_rows(mid[...])
    gvec[5:6, :] = jnp.sum(gn * unit, axis=0, keepdims=True)
    gvec[6:7, :] = jnp.sum(gn, axis=0, keepdims=True)
    c_own = cg[s].astype(F32)
    gvec[7:8, :] = jnp.sum(c_own, axis=0, keepdims=True)
    gm = c_own + norm_pull(gn, row(5), unit, rate)
    gmid[...] = gm
    branch = gm.astype(BF)
    gvec[4:5, :] = jnp.sum(branch.astype(F32), axis=0, keepdims=True)
    xg[s] = branch
    sq_send(KG, x_slot)

    def weight_grad(left, right, dw, size, cols=None):
        per = max(256 // size, 1)

        @pl.loop(0, dw.shape[0] * 2 // per)
        def _(i):
            lo = pl.ds(pl.multiple_of(i * per * size, per * size), per * size)
            value = dot_tn(left[:, lo], right).astype(BF)
            for j in range(per):
                k = i * per + j
                dw[lax.div(k, 2), lax.rem(k, 2)] = value[j * size : (j + 1) * size]

    weight_grad(hid.reshape(R, D), cg.reshape(R, D)[...], dw_dn, wf)
    rs_x(1)
    weight_grad(n2.reshape(R, D), gbf.reshape(R, D)[...], dw_up, w)
    rs_x(2)
    out_total = seq_total(1, oown, orecv)
    o_out[...] = (mid[...] + out_total + row(7))[:T].astype(BF)
    sq_core(KG, x_slot)
    sq_relay(KG, x_slot)
    rs_mid(1)
    sq_diag(KG, x_slot)

    @pl.loop(0, 4)
    def _(k):
        mine = wout[pl.ds(pl.multiple_of(s * DH, DH), DH), :]
        gctx[k] = dot_nt(xg[k], mine).astype(BF)

    own_cols = pl.ds(pl.multiple_of(s * DH, DH), DH)
    right = xg.reshape(R, D)[:, own_cols]
    for j in range(4):
        value = dot_tn(ctx[j], right).astype(BF)
        for i in range(DH // w):
            k = j * (DH // w) + i
            dw_out[k // 2, k % 2] = value[i * w : (i + 1) * w]
    rs_x(3)
    rs_mid(2)

    flat_g = gctx.reshape(R, DH)
    flat_d = dqkv.reshape(R, HP * 384)

    def backward_tile(hp, rows, count):
        lo = hp * 384
        query = flat[rows, lo : lo + 128]
        keys = flat[:, lo + 128 : lo + 256]
        vals = flat[:, lo + 256 : lo + 384]
        grad = flat_g[rows, hp * 128 : hp * 128 + 128]
        both = []
        for h in range(2):
            qh, gh = query * picks[h], grad * picks[h]
            probs = jnp.exp(dot_nt(qh, keys) + mask[...] - lse[hp * 2 + h, rows, :])
            dp = dot_nt(gh, vals)
            inner = jnp.sum(probs * dp, axis=-1, keepdims=True)
            ds = (probs * (dp - inner)).astype(BF)
            both.append(dot_nn(ds, keys))
            dkt[...] += dot_tn(qh, ds)
            dvt[...] += dot_tn(gh, probs.astype(BF))
        dq = jnp.where(lane < HEAD_DIM, both[0], both[1]) * HEAD_DIM ** (-0.5)
        flat_d[rows, lo : lo + 128] = dq.astype(BF)

    for hp in range(HP):
        lo = hp * 384
        dkt[...] = jnp.zeros_like(dkt)
        dvt[...] = jnp.zeros_like(dvt)
        tiles(functools.partial(backward_tile, hp))
        flat_d[:, lo + 128 : lo + 256] = dkt[...].T.astype(BF)
        flat_d[:, lo + 256 : lo + 384] = dvt[...].T.astype(BF)
        weight_grad(nrm.reshape(R, D), flat_d[:, lo : lo + 384], dw_qkv.at[hp], w)
        rs_x(4 + hp)
        if hp == 0:
            rs_fin(1)
            rs_fin(2)
            rs_mid(3)
        off = pl.ds(pl.multiple_of(s * DH + hp * 128, 128), 128)
        gvec[2:3, off] = jnp.sum(flat_d[:, lo : lo + 128].astype(F32), axis=0, keepdims=True)
        gvec[3:4, off] = jnp.sum(flat_d[:, lo + 256 : lo + 384].astype(F32), axis=0, keepdims=True)

    @pl.loop(0, 4)
    def _(i):
        seq_stage(i, 2, gpart, gown, grecv, dot_nt(dqkv[order(i)], wqkv[...]))

    for hp in range(HP):
        rs_mid(4 + hp)
    rs_fin(3)
    for m in (1, 2, 3):
        sq_relay(KFIN + m, fin_slot(m))
    gn = seq_total(2, gown, grecv)
    unit, rate = unit_rows(padded(tok))
    gvec[0:1, :] = jnp.sum(gn * unit, axis=0, keepdims=True)
    gvec[1:2, :] = jnp.sum(gn, axis=0, keepdims=True)
    for k in range(N):
        j = k // g
        dw_sm[k // 2, k % 2] = gvec[:, j * 128 : (j + 1) * 128]
    rs_x(0)
    o_tok[...] = (gmid[...] + norm_pull(gn, row(0), unit, rate))[:T].astype(BF)
    rs_mid(0)
    for hp in range(HP):
        rs_fin(4 + hp)
    rs_fin(0)
    rest = [4 + hp for hp in range(HP)] + [0]
    for m in rest:
        sq_relay(KFIN + m, fin_slot(m))
    for m in [1, 2, 3] + rest:
        sq_core(KFIN + m, fin_slot(m))
        sq_diag(KFIN + m, fin_slot(m))
    for copy, kind in started:
        if kind != KX:
            copy.wait_send()
    for kind in (1, 2):
        seq_sent(kind, opart if kind == 1 else gpart)


def make_body(mesh):
    N = mesh.shape["fsdp"]
    A = N // 2

    def body(
        tokens, lengths, ln1_gain, ln1_bias, qkv_weight, q_bias, v_bias, out_weight, out_bias,
        ln2_gain, ln2_bias, up_weight, up_bias, down_weight, down_bias, cotangent,
    ):
        _, T, D = tokens.shape
        w, FF = D // N, up_weight.shape[1]
        wf = FF // (4 * N)
        TP = -(-T // 16) * 16
        R = 4 * TP
        DH = D // 4
        HP = DH // 128
        FQ = FF // 4
        assert FQ == D and wf == w
        g = max(128 // w, 1)
        s = lax.axis_index("seq")
        f = lax.axis_index("fsdp")
        up_whole = wf % 128 == 0
        ub = lax.dynamic_slice(up_bias, (s * wf,), (wf,))
        packed = jnp.stack([ln1_gain, ln1_bias, q_bias, v_bias, out_bias, ln2_gain, ln2_bias, down_bias, ub])
        if g == 1:
            small = jnp.pad(packed, ((0, 7), (0, 0)))
        else:
            small = lax.dynamic_update_slice(jnp.zeros((16, 128), BF), packed, (0, lax.rem(f, g) * w))
        if not up_whole:
            up_weight = lax.dynamic_index_in_dim(up_weight.reshape(w, N, 4, wf), s, 2, False).reshape(w, FQ)
        place = jnp.arange(R)
        slot, inside = place // TP, place % TP
        valid = (inside < T) & (slot * T + inside < lengths[0])
        mask = jnp.where(valid, 0.0, -1e30).astype(F32)[None, :]

        z = dict(D=D, T=T, TP=TP, R=R, A=A, w=w, wf=wf, HP=HP, g=g, up_whole=up_whole)
        vm = pltpu.VMEM
        A1 = max(A - 1, 1)
        M = 4 + HP
        C = 384
        scratch = [
            vm((4, TP, D), BF),
            vm((4, TP, D), BF),
            vm((4, TP, D), BF),
            vm((4, R, DH), BF),
            vm((4, TP, D), BF),
            vm((4, TP, D), BF),
            vm((4, TP, D), BF),
            vm((4, TP, HP * C), BF),
            vm((D, HP * C), BF),
            vm((D, D), BF),
            vm((D, FQ), BF),
            vm((FQ, D), BF),
            vm((N, 16, 128), BF),
            vm((16, D), F32),
            vm((16, D), F32),
            vm((HP * 2, R, 1), F32),
            vm((TP, D), F32),
            vm((TP, D), F32),
            vm((4, TP, DH), BF),
            vm((4, TP, HP * C), BF),
            vm((128, R), F32),
            vm((128, R), F32),
            vm((3, TP, D), BF), vm((TP, D), F32), vm((3, TP, D), BF),
            vm((3, TP, D), BF), vm((TP, D), F32), vm((3, TP, D), BF),
            vm((HP, A, 2, w, C), BF), vm((A, 2, w, DH), BF), vm((A, 2, w, FQ), BF), vm((A, 2, wf, D), BF), vm((A, 2, 16, 128), F32),
            vm((HP, A, w, C), BF), vm((A, w, DH), BF), vm((A, w, FQ), BF), vm((A, wf, D), BF), vm((A, 16, 128), F32),
            vm((HP, A1, w, C), BF), vm((A1, w, DH), BF), vm((A1, w, FQ), BF), vm((A1, wf, D), BF), vm((A1, 16, 128), F32),
        ]
        dma = pltpu.SemaphoreType.DMA
        scratch += [
            dma((3 + 3 * HP + (N if up_whole else 1),)),
            dma((5, A1)), dma((5, A1)), dma((5, A)), dma((5, A)),
            dma((4 + HP + M, 3)), dma((4 + HP + M, 3)),
            dma((3, 3)), dma((3, 3)),
            dma((M,)), dma((M,)), dma((M, A1)), dma((M, A1)),
        ]
        here = pl.BlockSpec(memory_space=pltpu.VMEM)
        there = pl.BlockSpec(memory_space=pl.ANY)
        out_shapes = [
            jax.ShapeDtypeStruct((T, D), BF),
            jax.ShapeDtypeStruct((T, D), BF),
            jax.ShapeDtypeStruct((HP, 4, w, C), BF),
            jax.ShapeDtypeStruct((4, w, DH), BF),
            jax.ShapeDtypeStruct((4, w, FQ), BF),
            jax.ShapeDtypeStruct((4, wf, D), BF),
            jax.ShapeDtypeStruct((4, 16, 128), F32),
        ]
        out, gtok, gq, go, gu, gd, gs = pl.pallas_call(
            functools.partial(layer_kernel, z),
            out_shape=out_shapes,
            in_specs=[here, here, here, there, there, there, there, there],
            out_specs=[here] * 7,
            scratch_shapes=scratch,
            compiler_params=pltpu.CompilerParams(
                collective_id=0, has_side_effects=True, vmem_limit_bytes=67_000_000
            ),
            name="layer",
        )(tokens[0], cotangent[0], mask, small, qkv_weight, out_weight, up_weight, down_weight)

        g_qkv = gq.reshape(HP, 4, w, 3, 128).transpose(2, 3, 1, 0, 4).reshape(w, 3 * D).astype(F32)
        g_out = go.transpose(1, 0, 2).reshape(w, D).astype(F32)
        g_up = gu.reshape(4, w, N, wf).transpose(1, 2, 0, 3).reshape(w, FF).astype(F32)
        g_down = gd.reshape(4 * wf, D).astype(F32)
        if g > 1:
            gs = lax.dynamic_slice(gs, (0, 0, lax.rem(f, g) * w), (4, 16, w))
        sums = jnp.sum(gs[:, :8], axis=0)
        return (
            out[None], gtok[None], sums[0], sums[1], g_qkv, sums[2], sums[3], g_out, sums[4],
            sums[5], sums[6], g_up, gs[:, 8].reshape(4 * wf), g_down, sums[7],
        )

    return body


def solution(mesh):
    row, mat, act = P("fsdp"), P("fsdp", None), P("fsdp", "seq", None)
    return jax.shard_map(
        make_body(mesh),
        mesh=mesh,
        in_specs=(act, row, row, row, mat, row, row, mat, row, row, row, mat, row, mat, row, act),
        out_specs=(act, act, row, row, mat, row, row, mat, row, row, row, mat, row, mat, row),
        check_vma=False,
    )
```

time: 1520 us -> 262 us (0.17)
  waiting for transfers between devices: 952 us -> 0 us
  blocking collectives: 245 us -> 0 us
  Pallas kernels: 0 us -> 244 us
  matrix products: 181 us -> 0 us
  local copies, waits for them, and re-layouts: 74.3 us -> 13.7 us
  other arithmetic: 31.7 us -> 3.02 us
  between operations: 16.6 us -> 1.39 us
    reduce_scatter x4 -> x0, waiting for transfers between devices: 748 us -> none  [the longest x1 283 us: body(): lax.psum_scatter(g_down, 'fsdp', scatter_dimension=0, tiled=True)]
    pallas_call x0 -> x1, Pallas kernels: none -> 244 us  [body(): pl.pallas_call(functools.partial(layer_kernel, z), out_shape=out_shapes,...]
    dot_general x18 -> x0, matrix products: 181 us -> none  [the longest x1 27.6 us: attend_backward(): jnp.einsum('hqk,khd->qhd', grad_scores, keys_all, preferred_element_type=...]
    all_gather x9 -> x0, blocking collectives: 176 us -> none  [the longest x1 26.9 us: body(): lax.all_gather(up_bias, 'fsdp', axis=0, tiled=True)]
    all_gather x4 -> x0, waiting for transfers between devices: 116 us -> none  [the longest x1 92.4 us: body(): lax.all_gather(down_weight, 'fsdp', axis=0, tiled=True)]
    all_to_all x3 -> x0, waiting for transfers between devices: 45.2 us -> none  [the longest x1 36.3 us: body(): lax.all_to_all(project, 'seq', split_axis=3, concat_axis=2, tiled=True)]
    psum x1 -> x0, waiting for transfers between devices: 40.3 us -> none  [body(): lax.psum((attn_shares[0], attn_shares[1], attn_shares[2], attn_shares[3],...]
    unnamed x1 -> x0, blocking collectives: 33.5 us -> none
  transfers between devices with their start and end apart: 12 -> 0, of which waited for: 8 -> 0; matrix products, arithmetic and copies ran while one was open for 17% -> 0% of each run, Pallas kernels for 0% -> 0%
where the time goes in v1:
time: 262 us
  Pallas kernels  244 us (93%)
  local copies, waits for them, and re-layouts  13.7 us (5%)
  other arithmetic  3.02 us (1%)
    pallas_call x1, Pallas kernels, body(): pl.pallas_call(functools.partial(layer_kernel, z), out_shape=out_shapes,...  244 us
    unnamed x17, local copies, waits for them, and re-layouts  6.39 us

profile of v1, /device:TPU:0, one launch (start us, length us, event | category | flops | bytes accessed | tf_op | source)
XLA Modules:
  0.0 261.8 jit_solution(14514536639022089125)
XLA Ops:
  0.6 0.0 copy-start
  0.7 0.7 copy-done
  1.3 0.1 dynamic-slice_bitcast_fusion
  1.4 0.8 stack.39
  2.2 0.6 pad.4.sm_in
  3.5 0.6 and_select_fusion.mask
  4.1 243.7 %layer.1 = (bf16[258,1024]{1,0:T(8,128)(2,1)}, bf16[258,1024]{1,0:T(8,128)(2,1)}, bf16[2,4,128,384]{3,2,1,0:T(8,128)(2,1)}, bf16[4,128,256]{2,1,0:T(8,128)(2,1)}...) custom-call(bf16[258,1024]{1,0:T(8,128)(2,1)} %bitcast.57, ...), custom_call_target="tpu_custom_call" | custom-call | tf_op jit(solution)/shard_map/layer/pallas_call | solution.py:600
  247.9 0.7 slice_reduce_fusion
  248.6 0.5 slice_bitcast_fusion
  249.1 1.3 slice.38
  250.4 1.5 copy.43
  251.9 0.1 bitcast_bitcast_fusion
  252.1 1.4 copy.40
  253.4 0.0 copy-start.2
  253.4 1.9 reshape.114
  255.3 0.0 copy-done.2
  255.3 0.3 copy.37
  255.6 0.1 copy.38
  255.7 0.0 copy-start.1
  255.7 1.6 copy.41
  257.4 0.0 copy-start.5
  257.4 0.0 copy-done.1
  257.4 1.6 bitcast_convert_fusion
  259.0 0.0 copy-start.4
  259.0 0.0 copy-start.3
  259.0 0.0 copy-done.5
  259.0 0.2 copy.39
  259.2 1.0 copy.42
  260.2 0.0 copy-done.4
  260.2 0.8 copy.47
  261.0 0.0 copy-done.3
  261.0 0.8 copy.48
  (1 shorter events, 0.0 us)
Async XLA Ops:
  0.6 0.7 copy-start
  253.4 1.9 copy-start.2
  255.7 1.6 copy-start.1
  257.4 1.6 copy-start.5
  259.0 1.3 copy-start.4
  259.0 2.0 copy-start.3

commit v2 on v1

v2 whole, which is shorter than its diff:
```python
import functools
import math

import jax
import jax.numpy as jnp
from jax import lax
from jax.experimental import pallas as pl
from jax.experimental.pallas import tpu as pltpu
from jax.sharding import PartitionSpec as P

HEAD_DIM = 64
BF = jnp.bfloat16
F32 = jnp.float32
MESH = pl.DeviceIdType.MESH


def dot_nn(left, right):
    return lax.dot_general(left, right, (((1,), (0,)), ((), ())), preferred_element_type=F32)


def dot_nt(left, right):
    return lax.dot_general(left, right, (((1,), (1,)), ((), ())), preferred_element_type=F32)


def dot_tn(left, right):
    return lax.dot_general(left, right, (((0,), (0,)), ((), ())), preferred_element_type=F32)


def unit_rows(values):
    center = values - jnp.mean(values, axis=-1, keepdims=True)
    rate = lax.rsqrt(jnp.mean(center * center, axis=-1, keepdims=True) + 1e-6)
    return center * rate, rate


def norm_pull(grad, gain, unit, rate):
    scaled = grad * gain
    return rate * (
        scaled
        - jnp.mean(scaled, axis=-1, keepdims=True)
        - unit * jnp.mean(scaled * unit, axis=-1, keepdims=True)
    )


def layer_kernel(
    z,
    tok, cot, mask, sm_in, qkv_in, out_in, up_in, dn_in,
    o_out, o_tok, o_qkv, o_ow, o_up, o_dn, o_sm,
    xg, cg, nrm, ctx, n2, hid, gbf, pq, wqkv, wout, wup, wdn, smg, vec, gvec, lse, mid, gmid,
    gctx, dqkv, dkt, dvt, gpart, gown, grecv, opart, oown, orecv,
    dw_qkv, dw_out, dw_up, dw_dn, dw_sm, rr_qkv, rr_out, rr_up, rr_dn, rr_sm,
    loc_sem, ag_s, ag_r, rg_s, rg_r, sq_s, sq_r, rs_s, rs_r, sa_s, sa_r, sg_s, sg_r,
):
    D, T, TP, R, A, w, wf, HP = z["D"], z["T"], z["TP"], z["R"], z["A"], z["w"], z["wf"], z["HP"]
    N, H, DH, LB, g = 2 * A, A, D // 4, D // 128, z["g"]
    s = lax.axis_index("seq")
    f = lax.axis_index("fsdp")
    y, c = lax.div(s, 2), lax.rem(s, 2)
    s_core, s_y, s_diag = y * 2 + 1 - c, (1 - y) * 2 + c, (1 - y) * 2 + 1 - c
    to_core, to_y = {"seq": s_core}, {"seq": s_y}

    odd = lax.rem(f, 2)
    place = (1 - odd) * lax.div(f, 2) + odd * (N - 1 - lax.div(f, 2))

    def at_place(q):
        late = lax.div(q, A)
        return (1 - late) * 2 * q + late * (2 * (N - 1 - q) + 1)

    def ahead(d):
        return at_place(lax.rem(place + d + N, N))

    to_ring = ({"fsdp": ahead(1)}, {"fsdp": ahead(-1)})

    def send(src, dst, ssem, rsem, dev):
        pltpu.make_async_remote_copy(
            src_ref=src, dst_ref=dst, send_sem=ssem, recv_sem=rsem, device_id=dev, device_id_type=MESH
        ).start()

    def arrive(dst, rsem, dev):
        pltpu.make_async_remote_copy(
            src_ref=dst, dst_ref=dst, send_sem=rsem, recv_sem=rsem, device_id=dev, device_id_type=MESH
        ).wait_recv()

    def sent(src, ssem, dev):
        pltpu.make_async_remote_copy(
            src_ref=src, dst_ref=src, send_sem=ssem, recv_sem=ssem, device_id=dev, device_id_type=MESH
        ).wait_send()

    def thirds(first, last):
        count = max(last - first, 0)
        cut = [first + (count * k) // 3 for k in range(4)]
        return [range(cut[k], cut[k + 1]) for k in range(3)]

    quarter = pl.ds(pl.multiple_of(s * DH, DH), DH)

    def rows_of(k, size, half=None):
        if half is None:
            return pl.ds(pl.multiple_of(k * size, size), size)
        return pl.ds(pl.multiple_of(k * size + half * (size // 2), size // 2), size // 2)

    blocks = {
        0: lambda k, half=None: wqkv.at[rows_of(k, w, half)],
        1: lambda k, half=None: wout.at[rows_of(k, w, half), quarter],
        2: lambda k, half=None: wup.at[rows_of(k, w, half)],
        3: lambda k, half=None: wdn.at[rows_of(k, wf, half)],
    }

    def ag_block(m, way, d, back):
        k = ahead(-back if way == 0 else back)
        return blocks[m](k, way if d == H else None)

    def ag_own(m):
        for way in range(2):
            ref = ag_block(m, way, 1, 0)
            send(ref, ref, ag_s.at[m, way, 0], ag_r.at[m, way, 0], to_ring[way])

    def ag_take(m, d):
        for way in range(2):
            arrive(ag_block(m, way, d, d), ag_r.at[m, way, d - 1], to_ring[way])
            if d < H:
                ref = ag_block(m, way, d + 1, d)
                send(ref, ref, ag_s.at[m, way, d], ag_r.at[m, way, d], to_ring[way])

    def ag_fwd(m, third):
        for d in thirds(1, H)[third]:
            ag_take(m, d)

    def ag_last(m):
        ag_take(m, H)

    def ag_sent(m):
        for way in range(2):
            for d in range(1, H + 1):
                sent(ag_block(m, way, d, d - 1), ag_s.at[m, way, d - 1], to_ring[way])

    def sq_send(kind, ref):
        send(ref(s), ref(s), sq_s.at[kind, 0], sq_r.at[kind, 0], to_core)
        send(ref(s), ref(s), sq_s.at[kind, 1], sq_r.at[kind, 1], to_y)

    def sq_core(kind, ref):
        arrive(ref(s_core), sq_r.at[kind, 0], to_core)

    def sq_relay(kind, ref):
        arrive(ref(s_y), sq_r.at[kind, 1], to_y)
        send(ref(s_y), ref(s_y), sq_s.at[kind, 2], sq_r.at[kind, 2], to_core)

    def sq_diag(kind, ref):
        arrive(ref(s_diag), sq_r.at[kind, 2], to_core)

    def sq_sent(kind, ref):
        sent(ref(s), sq_s.at[kind, 0], to_core)
        sent(ref(s), sq_s.at[kind, 1], to_y)
        sent(ref(s_y), sq_s.at[kind, 2], to_core)

    def x_slot(k):
        return xg.at[k]

    def c_slot(k):
        return cg.at[k]

    def out_slot(k):
        return wout.at[:, pl.ds(pl.multiple_of(k * DH, DH), DH)]

    def ctx_slot(hp):
        return lambda k: ctx.at[k, :, hp * 128 : hp * 128 + 128]

    KX, KC, KG, KO, KCTX, KFIN = 0, 1, 2, 3, 4, 4 + HP

    def order(i):
        hb, lb = lax.div(3 - i, 2), lax.rem(3 - i, 2)
        return lax.rem(y + hb, 2) * 2 + lax.rem(c + lb, 2)

    def seq_stage(i, kind, part, own, recv, value):
        @pl.when(i < 3)
        def _():
            part[jnp.minimum(i, 2)] = value.astype(BF)

        @pl.when(i == 0)
        def _():
            send(part.at[0], recv.at[0], rs_s.at[kind, 0], rs_r.at[kind, 0], to_core)

        @pl.when(i == 1)
        def _():
            arrive(recv.at[0], rs_r.at[kind, 0], to_core)
            part[1] = (part[1].astype(F32) + recv[0].astype(F32)).astype(BF)
            send(part.at[1], recv.at[1], rs_s.at[kind, 1], rs_r.at[kind, 1], to_y)

        @pl.when(i == 2)
        def _():
            send(part.at[2], recv.at[2], rs_s.at[kind, 2], rs_r.at[kind, 2], to_core)

        @pl.when(i == 3)
        def _():
            own[...] = value

    def seq_sent(kind, part):
        for j in range(3):
            sent(part.at[j], rs_s.at[kind, j], to_core)

    def seq_total(kind, own, recv):
        arrive(recv.at[2], rs_r.at[kind, 2], to_core)
        arrive(recv.at[1], rs_r.at[kind, 1], to_y)
        return own[...] + recv[2].astype(F32) + recv[1].astype(F32)

    grads = {0: (dw_dn, rr_dn, o_dn), 1: (dw_up, rr_up, o_up), 2: (dw_out, rr_out, o_ow)}
    for hp in range(HP):
        grads[3 + hp] = (dw_qkv.at[hp], rr_qkv.at[hp], o_qkv.at[hp])
    MG = 3 + HP

    def rg_rows(m, way, j):
        size = grads[m][0].shape[1]
        return slice(way * (size // 2), (way + 1) * (size // 2)) if j == 0 else slice(0, size)

    def rg_owner(way, j):
        return ahead(H - j if way == 0 else j - H)

    def rg_src(m, way, j):
        return grads[m][0].at[rg_owner(way, j), rg_rows(m, way, j)]

    def rg_send(m, way, j):
        dst = grads[m][1].at[way, j, rg_rows(m, way, j)]
        send(rg_src(m, way, j), dst, rg_s.at[m, way, j], rg_r.at[m, way, j], to_ring[way])

    def rg_arrive(m, way, j):
        arrive(grads[m][1].at[way, j, rg_rows(m, way, j)], rg_r.at[m, way, j], to_ring[way])

    def rg_own(m):
        for way in range(2):
            rg_send(m, way, 0)

    def rg_fwd(m, third):
        dw, rr, _ = grads[m]
        for j in thirds(1, H)[third]:
            for way in range(2):
                rows = rg_rows(m, way, j - 1)
                owner = rg_owner(way, j)
                rg_arrive(m, way, j - 1)
                dw[owner, rows] = (dw[owner, rows].astype(F32) + rr[way, j - 1, rows].astype(F32)).astype(dw.dtype)
                rg_send(m, way, j)

    def fin_slot(m):
        return lambda k: grads[m][2].at[k]

    def rg_fin(m):
        dw, rr, out = grads[m]
        total = dw[f].astype(F32)
        for way in range(2):
            rg_arrive(m, way, H - 1)
            total = total + rr[way, H - 1].astype(F32)
        out[s] = total.astype(out.dtype)
        sq_send(KFIN + m, fin_slot(m))

    def rg_sent(m):
        for way in range(2):
            for j in range(H):
                sent(rg_src(m, way, j), rg_s.at[m, way, j], to_ring[way])

    def other(d):
        return lax.rem(f + d, N)

    local = []

    def bring(src, dst):
        copy = pltpu.make_async_copy(src, dst, loc_sem.at[len(local)])
        copy.start()
        local.append(copy)

    bring(sm_in, smg.at[f])
    for hp in range(HP):
        for part in range(3):
            cols = pl.ds(pl.multiple_of(part * D + s * DH + hp * 128, 128), 128)
            lo = hp * 384 + part * 128
            bring(qkv_in.at[:, cols], wqkv.at[rows_of(f, w), lo : lo + 128])
    bring(out_in.at[:, quarter], wout.at[rows_of(f, w), quarter])
    if z["up_whole"]:
        for k in range(N):
            cols = pl.ds(pl.multiple_of((k * 4 + s) * wf, wf), wf)
            bring(up_in.at[:, cols], wup.at[rows_of(f, w), k * wf : (k + 1) * wf])
    else:
        bring(up_in, wup.at[rows_of(f, w)])
    bring(dn_in.at[rows_of(s, wf)], wdn.at[rows_of(f, wf)])

    def padded(ref):
        return jnp.concatenate([ref[...].astype(F32), jnp.zeros((TP - T, D), F32)], axis=0)

    barrier = pltpu.get_barrier_semaphore()
    peers = [to_core, to_y] + [{"fsdp": other(d)} for d in range(1, N)]
    for dev in peers:
        pl.semaphore_signal(barrier, inc=1, device_id=dev, device_id_type=MESH)
    xg[s] = padded(tok).astype(BF)
    cg[s] = padded(cot).astype(BF)
    gvec[...] = jnp.zeros_like(gvec)
    for copy in local:
        copy.wait()
    pl.semaphore_wait(barrier, len(peers))

    for d in range(1, N):
        send(smg.at[f], smg.at[f], sa_s.at[d - 1], sa_r.at[d - 1], {"fsdp": other(d)})
    sq_send(KX, x_slot)
    ag_own(0)
    ag_own(1)
    sq_send(KC, c_slot)
    for d in range(1, N):
        arrive(smg.at[other(N - d)], sa_r.at[d - 1], to_ring[0])
    for j in range(LB):
        piece = smg[j * g].astype(F32)
        for i in range(1, g):
            piece = piece + smg[j * g + i].astype(F32)
        vec[:, j * 128 : (j + 1) * 128] = piece

    def row(k):
        return vec[k : k + 1, :]

    def first_norm(k):
        unit, _ = unit_rows(xg[k].astype(F32))
        nrm[k] = (unit * row(0) + row(1)).astype(BF)

    first_norm(s)
    ag_fwd(0, 0)
    sq_core(KX, x_slot)
    first_norm(s_core)
    ag_fwd(1, 0)
    ag_own(2)
    sq_relay(KX, x_slot)
    ag_fwd(0, 1)
    first_norm(s_y)
    ag_fwd(1, 1)
    sq_diag(KX, x_slot)
    first_norm(s_diag)
    ag_fwd(0, 2)
    ag_own(3)
    ag_fwd(1, 2)
    ag_last(0)

    pieces = []
    for hp in range(HP):
        cols = pl.ds(pl.multiple_of(s * DH + hp * 128, 128), 128)
        pieces += [vec[2:3, cols], jnp.zeros((1, 128), F32), vec[3:4, cols]]
    proj_bias = jnp.concatenate(pieces, axis=1)
    lanes = lax.broadcasted_iota(jnp.int32, (1, HP * 384), 1)
    proj_scale = jnp.where(lax.rem(lanes, 384) < 128, HEAD_DIM ** (-0.5), 1.0).astype(F32)

    @pl.loop(0, 4)
    def _(k):
        value = dot_nn(nrm[k], wqkv[...]) + proj_bias
        pq[k] = (value * proj_scale).astype(BF)

    ag_last(1)
    sq_send(KO, out_slot)

    flat = pq.reshape(R, HP * 384)
    lane = lax.broadcasted_iota(jnp.int32, (1, 128), 1)
    first = (lane < HEAD_DIM).astype(F32)
    picks = (first.astype(BF), (1.0 - first).astype(BF))

    def forward_tile(hp, k):
        lo = hp * 384
        query = pq[k, :, lo : lo + 128]
        keys = flat[:, lo + 128 : lo + 256]
        vals = flat[:, lo + 256 : lo + 384]
        both, logs = [], []
        for h in range(2):
            scores = dot_nt(query * picks[h], keys) + mask[...]
            top = jnp.max(scores, axis=-1, keepdims=True)
            grown = jnp.exp(scores - top)
            total = jnp.sum(grown, axis=-1, keepdims=True)
            logs.append(top + jnp.log(total))
            both.append(dot_nn((grown * (1.0 / total)).astype(BF), vals))
        here = jnp.where(lane < HEAD_DIM, both[0], both[1]).astype(BF)
        rows = pl.ds(pl.multiple_of(k * TP, 16), TP)
        ctx[s, rows, hp * 128 : hp * 128 + 128] = here
        lse[hp, rows, :] = jnp.where(lane < HEAD_DIM, logs[0], logs[1])

    for hp in range(HP):
        @pl.loop(0, 4)
        def _(i):
            forward_tile(hp, i)

            if hp < 2:
                @pl.when(i == 1)
                def _():
                    ag_fwd(2, hp)

                @pl.when(i == 3)
                def _():
                    ag_fwd(3, hp)

        sq_send(KCTX + hp, ctx_slot(hp))
        if hp == 0:
            sq_relay(KC, c_slot)
        if hp == 1:
            sq_relay(KO, out_slot)
            sq_relay(KCTX, ctx_slot(0))
    for hp in range(HP, 2):
        ag_fwd(2, hp)
        ag_fwd(3, hp)
    if HP == 1:
        sq_relay(KO, out_slot)
        sq_relay(KCTX, ctx_slot(0))
    ag_fwd(2, 2)
    sq_core(KO, out_slot)
    sq_diag(KO, out_slot)
    for hp in range(1, HP):
        sq_relay(KCTX + hp, ctx_slot(hp))
    for hp in range(HP):
        sq_core(KCTX + hp, ctx_slot(hp))
        sq_diag(KCTX + hp, ctx_slot(hp))

    @pl.loop(0, 4)
    def _(i):
        k = order(i)
        rows = pl.ds(pl.multiple_of(k * TP, 16), TP)
        joined = jnp.concatenate([ctx[j, rows, :] for j in range(4)], axis=1)
        value = xg[k].astype(F32) + dot_nn(joined, wout[...]) + row(4)
        unit, _ = unit_rows(value)
        n2[k] = (unit * row(5) + row(6)).astype(BF)

        @pl.when(i == 3)
        def _():
            mid[...] = value

    sq_sent(KX, x_slot)
    ag_fwd(3, 2)
    ag_last(2)

    @pl.loop(0, 4)
    def _(k):
        before = dot_nn(n2[k], wup[...]) + row(8)
        cdf = 0.5 + 0.5 * lax.erf(before * (0.5**0.5))
        slope = cdf + before * (jnp.exp(before * before * -0.5) * (1.0 / math.sqrt(2.0 * math.pi)))
        hid[k] = (before * cdf).astype(BF)
        gbf[k] = slope.astype(BF)

    def weight_grad(left, right, dw, size):
        per = max(256 // size, 1)

        @pl.loop(0, dw.shape[0] // per)
        def _(i):
            lo = pl.ds(pl.multiple_of(i * per * size, per * size), per * size)
            value = dot_tn(left[:, lo], right).astype(BF)
            for j in range(per):
                dw[i * per + j] = value[j * size : (j + 1) * size]

    sq_core(KC, c_slot)
    sq_diag(KC, c_slot)
    weight_grad(hid.reshape(R, D), cg.reshape(R, D)[...], dw_dn, wf)
    rg_own(0)
    ag_last(3)

    @pl.loop(0, 4)
    def _(i):
        k = order(i)
        grad = (dot_nt(cg[k], wdn[...]) * gbf[k].astype(F32)).astype(BF)
        gbf[k] = grad
        gvec[8:9, :] += jnp.sum(grad.astype(F32), axis=0, keepdims=True)
        seq_stage(i, 0, gpart, gown, grecv, dot_nt(grad, wup[...]))
        seq_stage(i, 1, opart, oown, orecv, dot_nn(hid[k], wdn[...]))

    rg_fwd(0, 0)
    weight_grad(n2.reshape(R, D), gbf.reshape(R, D)[...], dw_up, w)
    rg_own(1)

    gn = seq_total(0, gown, grecv)
    seq_sent(0, gpart)
    unit, rate = unit_rows(mid[...])
    gvec[5:6, :] = jnp.sum(gn * unit, axis=0, keepdims=True)
    gvec[6:7, :] = jnp.sum(gn, axis=0, keepdims=True)
    c_own = cg[s].astype(F32)
    gvec[7:8, :] = jnp.sum(c_own, axis=0, keepdims=True)
    gm = c_own + norm_pull(gn, row(5), unit, rate)
    gmid[...] = gm
    branch = gm.astype(BF)
    gvec[4:5, :] = jnp.sum(branch.astype(F32), axis=0, keepdims=True)
    xg[s] = branch
    sq_send(KG, x_slot)
    rg_fwd(0, 1)
    rg_fwd(1, 0)
    sq_core(KG, x_slot)
    out_total = seq_total(1, oown, orecv)
    o_out[...] = (mid[...] + out_total + row(7))[:T].astype(BF)
    sq_relay(KG, x_slot)
    rg_fwd(0, 2)
    sq_diag(KG, x_slot)

    @pl.loop(0, 4)
    def _(k):
        gctx[k] = dot_nt(xg[k], wout[pl.ds(pl.multiple_of(s * DH, DH), DH), :]).astype(BF)

    right = xg.reshape(R, D)[:, quarter]
    for j in range(4):
        value = dot_tn(ctx[j], right).astype(BF)
        for i in range(DH // w):
            dw_out[j * (DH // w) + i] = value[i * w : (i + 1) * w]
    rg_own(2)

    flat_g = gctx.reshape(R, DH)
    flat_d = dqkv.reshape(R, HP * 384)

    def backward_tile(hp, rows):
        lo = hp * 384
        query = flat[rows, lo : lo + 128]
        keys = flat[:, lo + 128 : lo + 256]
        vals = flat[:, lo + 256 : lo + 384]
        grad = flat_g[rows, hp * 128 : hp * 128 + 128]
        logs = lse[hp, rows, :]
        both = []
        for h in range(2):
            qh, gh = query * picks[h], grad * picks[h]
            probs = jnp.exp(dot_nt(qh, keys) + mask[...] - logs[:, h * HEAD_DIM : h * HEAD_DIM + 1])
            dp = dot_nt(gh, vals)
            inner = jnp.sum(probs * dp, axis=-1, keepdims=True)
            ds = (probs * (dp - inner)).astype(BF)
            both.append(dot_nn(ds, keys))
            dkt[...] += dot_tn(qh, ds)
            dvt[...] += dot_tn(gh, probs.astype(BF))
        dq = jnp.where(lane < HEAD_DIM, both[0], both[1]) * HEAD_DIM ** (-0.5)
        flat_d[rows, lo : lo + 128] = dq.astype(BF)

    polls = {
        (0, 0): lambda: rg_fwd(1, 1),
        (0, 1): lambda: rg_fin(0),
        (0, 2): lambda: rg_fwd(2, 0),
        (0, 3): lambda: rg_fwd(1, 2),
        (1, 0): lambda: rg_fwd(2, 1),
        (1, 1): lambda: rg_fwd(3, 0),
        (1, 2): lambda: rg_fin(1),
        (1, 3): lambda: [rg_fwd(2, 2), rg_fwd(3, 1)],
    }

    def poll_at(poll):
        poll()

    full = R // 256
    for hp in range(HP):
        lo = hp * 384
        dkt[...] = jnp.zeros_like(dkt)
        dvt[...] = jnp.zeros_like(dvt)

        @pl.loop(0, full)
        def _(i):
            backward_tile(hp, pl.ds(pl.multiple_of(i * 256, 256), 256))
            for (which, when), poll in polls.items():
                if which == hp and when < full:
                    pl.when(i == when)(functools.partial(poll_at, poll))

        if R % 256:
            backward_tile(hp, pl.ds(full * 256, R % 256))
        flat_d[:, lo + 128 : lo + 256] = dkt[...].T.astype(BF)
        flat_d[:, lo + 256 : lo + 384] = dvt[...].T.astype(BF)
        weight_grad(nrm.reshape(R, D), flat_d[:, lo : lo + 384], dw_qkv.at[hp], w)
        rg_own(3 + hp)
        off = pl.ds(pl.multiple_of(s * DH + hp * 128, 128), 128)
        gvec[2:3, off] = jnp.sum(flat_d[:, lo : lo + 128].astype(F32), axis=0, keepdims=True)
        gvec[3:4, off] = jnp.sum(flat_d[:, lo + 256 : lo + 384].astype(F32), axis=0, keepdims=True)
    for (which, when), poll in polls.items():
        if which >= HP or when >= full:
            poll()

    @pl.loop(0, 4)
    def _(i):
        seq_stage(i, 2, gpart, gown, grecv, dot_nt(dqkv[order(i)], wqkv[...]))

    last = 2 + HP
    if HP > 1:
        rg_fwd(3, 2)
        rg_fwd(last, 0)
    sq_relay(KFIN + 0, fin_slot(0))
    rg_fin(2)
    if HP > 1:
        rg_fin(3)
        rg_fwd(last, 1)
        sq_relay(KFIN + 1, fin_slot(1))
        sq_relay(KFIN + 2, fin_slot(2))
        rg_fwd(last, 2)
    else:
        rg_fwd(3, 2)
        sq_relay(KFIN + 1, fin_slot(1))
        sq_relay(KFIN + 2, fin_slot(2))
    gn = seq_total(2, gown, grecv)
    unit, rate = unit_rows(padded(tok))
    gvec[0:1, :] = jnp.sum(gn * unit, axis=0, keepdims=True)
    gvec[1:2, :] = jnp.sum(gn, axis=0, keepdims=True)
    for k in range(N):
        j = k // g
        dw_sm[k] = gvec[:, j * 128 : (j + 1) * 128]
    for d in range(1, N):
        send(dw_sm.at[other(d)], rr_sm.at[d - 1], sg_s.at[d - 1], sg_r.at[d - 1], {"fsdp": other(d)})
    o_tok[...] = (gmid[...] + norm_pull(gn, row(0), unit, rate))[:T].astype(BF)
    rg_fin(last)
    total = dw_sm[f]
    for d in range(1, N):
        arrive(rr_sm.at[d - 1], sg_r.at[d - 1], to_ring[0])
        total = total + rr_sm[d - 1]
    o_sm[s] = total

    def sm_slot(k):
        return o_sm.at[k]

    sq_send(KFIN + MG, sm_slot)
    finals = [(KFIN + m, fin_slot(m)) for m in range(MG)] + [(KFIN + MG, sm_slot)]
    for kind, ref in finals[3:]:
        sq_relay(kind, ref)
    for kind, ref in finals:
        sq_core(kind, ref)
        sq_diag(kind, ref)

    for m in range(4):
        ag_sent(m)
    for m in range(MG):
        rg_sent(m)
    for kind, ref in [(KC, c_slot), (KG, x_slot), (KO, out_slot)] + finals:
        sq_sent(kind, ref)
    for hp in range(HP):
        sq_sent(KCTX + hp, ctx_slot(hp))
    seq_sent(1, opart)
    seq_sent(2, gpart)
    for d in range(1, N):
        sent(smg.at[f], sa_s.at[d - 1], to_ring[0])
        sent(dw_sm.at[other(d)], sg_s.at[d - 1], to_ring[0])


def make_body(mesh):
    N = mesh.shape["fsdp"]
    A = N // 2

    def body(
        tokens, lengths, ln1_gain, ln1_bias, qkv_weight, q_bias, v_bias, out_weight, out_bias,
        ln2_gain, ln2_bias, up_weight, up_bias, down_weight, down_bias, cotangent,
    ):
        _, T, D = tokens.shape
        w, FF = D // N, up_weight.shape[1]
        wf = FF // (4 * N)
        TP = -(-T // 16) * 16
        R = 4 * TP
        DH = D // 4
        HP = DH // 128
        FQ = FF // 4
        assert FQ == D and wf == w
        g = max(128 // w, 1)
        s = lax.axis_index("seq")
        f = lax.axis_index("fsdp")
        up_whole = wf % 128 == 0
        ub = lax.dynamic_slice(up_bias, (s * wf,), (wf,))
        packed = jnp.stack([ln1_gain, ln1_bias, q_bias, v_bias, out_bias, ln2_gain, ln2_bias, down_bias, ub])
        if g == 1:
            small = jnp.pad(packed, ((0, 7), (0, 0)))
        else:
            small = lax.dynamic_update_slice(jnp.zeros((16, 128), BF), packed, (0, lax.rem(f, g) * w))
        if not up_whole:
            up_weight = lax.dynamic_index_in_dim(up_weight.reshape(w, N, 4, wf), s, 2, False).reshape(w, FQ)
        place = jnp.arange(R)
        slot, inside = place // TP, place % TP
        valid = (inside < T) & (slot * T + inside < lengths[0])
        mask = jnp.where(valid, 0.0, -1e30).astype(F32)[None, :]

        z = dict(D=D, T=T, TP=TP, R=R, A=A, w=w, wf=wf, HP=HP, g=g, up_whole=up_whole)
        vm = pltpu.VMEM
        C = 384
        scratch = [
            vm((4, TP, D), BF),
            vm((4, TP, D), BF),
            vm((4, TP, D), BF),
            vm((4, R, DH), BF),
            vm((4, TP, D), BF),
            vm((4, TP, D), BF),
            vm((4, TP, D), BF),
            vm((4, TP, HP * C), BF),
            vm((D, HP * C), BF),
            vm((D, D), BF),
            vm((D, FQ), BF),
            vm((FQ, D), BF),
            vm((N, 16, 128), BF),
            vm((16, D), F32),
            vm((16, D), F32),
            vm((HP, R, 128), F32),
            vm((TP, D), F32),
            vm((TP, D), F32),
            vm((4, TP, DH), BF),
            vm((4, TP, HP * C), BF),
            vm((128, R), F32),
            vm((128, R), F32),
            vm((3, TP, D), BF), vm((TP, D), F32), vm((3, TP, D), BF),
            vm((3, TP, D), BF), vm((TP, D), F32), vm((3, TP, D), BF),
            vm((HP, N, w, C), BF), vm((N, w, DH), BF), vm((N, w, FQ), BF), vm((N, wf, D), BF), vm((N, 16, 128), F32),
            vm((HP, 2, A, w, C), BF), vm((2, A, w, DH), BF), vm((2, A, w, FQ), BF), vm((2, A, wf, D), BF), vm((N - 1, 16, 128), F32),
        ]
        dma = pltpu.SemaphoreType.DMA
        scratch += [
            dma((3 + 3 * HP + (N if up_whole else 1),)),
            dma((4, 2, A)), dma((4, 2, A)), dma((3 + HP, 2, A)), dma((3 + HP, 2, A)),
            dma((8 + 2 * HP, 3)), dma((8 + 2 * HP, 3)),
            dma((3, 3)), dma((3, 3)),
            dma((N - 1,)), dma((N - 1,)), dma((N - 1,)), dma((N - 1,)),
        ]
        here = pl.BlockSpec(memory_space=pltpu.VMEM)
        there = pl.BlockSpec(memory_space=pl.ANY)
        out_shapes = [
            jax.ShapeDtypeStruct((T, D), BF),
            jax.ShapeDtypeStruct((T, D), BF),
            jax.ShapeDtypeStruct((HP, 4, w, C), BF),
            jax.ShapeDtypeStruct((4, w, DH), BF),
            jax.ShapeDtypeStruct((4, w, FQ), BF),
            jax.ShapeDtypeStruct((4, wf, D), BF),
            jax.ShapeDtypeStruct((4, 16, 128), F32),
        ]
        out, gtok, gq, go, gu, gd, gs = pl.pallas_call(
            functools.partial(layer_kernel, z),
            out_shape=out_shapes,
            in_specs=[here, here, here, there, there, there, there, there],
            out_specs=[here] * 7,
            scratch_shapes=scratch,
            compiler_params=pltpu.CompilerParams(
                collective_id=0, has_side_effects=True, vmem_limit_bytes=67_000_000
            ),
            name="layer",
        )(tokens[0], cotangent[0], mask, small, qkv_weight, out_weight, up_weight, down_weight)

        g_qkv = gq.reshape(HP, 4, w, 3, 128).transpose(2, 3, 1, 0, 4).reshape(w, 3 * D).astype(F32)
        g_out = go.transpose(1, 0, 2).reshape(w, D).astype(F32)
        g_up = gu.reshape(4, w, N, wf).transpose(1, 2, 0, 3).reshape(w, FF).astype(F32)
        g_down = gd.reshape(4 * wf, D).astype(F32)
        if g > 1:
            gs = lax.dynamic_slice(gs, (0, 0, lax.rem(f, g) * w), (4, 16, w))
        sums = jnp.sum(gs[:, :8], axis=0)
        return (
            out[None], gtok[None], sums[0], sums[1], g_qkv, sums[2], sums[3], g_out, sums[4],
            sums[5], sums[6], g_up, gs[:, 8].reshape(4 * wf), g_down, sums[7],
        )

    return body


def solution(mesh):
    row, mat, act = P("fsdp"), P("fsdp", None), P("fsdp", "seq", None)
    return jax.shard_map(
        make_body(mesh),
        mesh=mesh,
        in_specs=(act, row, row, row, mat, row, row, mat, row, row, row, mat, row, mat, row, act),
        out_specs=(act, act, row, row, mat, row, row, mat, row, row, row, mat, row, mat, row),
        check_vma=False,
    )
```

time: 262 us -> 201 us (0.77)
  Pallas kernels: 244 us -> 182 us
    pallas_call x1, Pallas kernels: 244 us -> 182 us  [body(): pl.pallas_call(functools.partial(layer_kernel, z), out_shape=out_shapes,...]
where the time goes in v2:
time: 201 us; the launch traced here: 200 us
  Pallas kernels  182 us (91%)
  local copies, waits for them, and re-layouts  13.7 us (7%)
  other arithmetic  3.02 us (2%)
    pallas_call x1, Pallas kernels, body(): pl.pallas_call(functools.partial(layer_kernel, z), out_shape=out_shapes,...  182 us
    unnamed x17, local copies, waits for them, and re-layouts  6.39 us

profile of v2, /device:TPU:0, one launch (start us, length us, event | category | flops | bytes accessed | tf_op | source)
XLA Modules:
  0.0 200.4 jit_solution(17413410829383559573)
XLA Ops:
  0.6 0.0 copy-start
  0.7 0.7 copy-done
  1.3 0.1 dynamic-slice_bitcast_fusion
  1.4 0.8 stack.39
  2.2 0.6 pad.4.sm_in
  3.5 0.6 and_select_fusion.mask
  4.1 182.3 %layer.1 = (bf16[258,1024]{1,0:T(8,128)(2,1)}, bf16[258,1024]{1,0:T(8,128)(2,1)}, bf16[2,4,128,384]{3,2,1,0:T(8,128)(2,1)}, bf16[4,128,256]{2,1,0:T(8,128)(2,1)}...) custom-call(bf16[258,1024]{1,0:T(8,128)(2,1)} %bitcast.57, ...), custom_call_target="tpu_custom_call" | custom-call | tf_op jit(solution)/shard_map/layer/pallas_call | solution.py:705
  186.4 0.7 slice_reduce_fusion
  187.1 0.5 slice_bitcast_fusion
  187.7 1.3 slice.38
  189.0 1.5 copy.43
  190.5 0.1 bitcast_bitcast_fusion
  190.6 1.4 copy.40
  192.0 0.0 copy-start.2
  192.0 1.9 reshape.114
  193.8 0.0 copy-done.2
  193.8 0.3 copy.37
  194.1 0.1 copy.38
  194.3 0.0 copy-start.1
  194.3 1.6 copy.41
  195.9 0.0 copy-start.5
  195.9 0.0 copy-done.1
  195.9 1.6 bitcast_convert_fusion
  197.5 0.0 copy-start.4
  197.5 0.0 copy-start.3
  197.5 0.0 copy-done.5
  197.6 0.2 copy.39
  197.8 1.0 copy.42
  198.8 0.0 copy-done.4
  198.8 0.8 copy.47
  199.6 0.0 copy-done.3
  199.6 0.8 copy.48
  (1 shorter events, 0.0 us)
Async XLA Ops:
  0.6 0.7 copy-start
  192.0 1.9 copy-start.2
  194.3 1.6 copy-start.1
  195.9 1.6 copy-start.5
  197.5 1.3 copy-start.4
  197.5 2.0 %copy-start.3 = (bf16[258,1024]{1,0:T(8,128)(2,1)S(1)}, bf16[258,1024]{1,0:T(8,128)(2,1)}, u32[]{:S(2)}) copy-start(bf16[258,1024]{1,0:T(8,128)(2,1)} %get-tuple-element.23) | copy-start | bytes 1585156

commit v3 on v2

--- a/solution.py
+++ b/solution.py
@@ -43,12 +43,12 @@
 
 def layer_kernel(
     z,
-    tok, cot, mask, sm_in, qkv_in, out_in, up_in, dn_in,
+    tok, cot, len_in, sm_in, qkv_in, out_in, up_in, dn_in,
     o_out, o_tok, o_qkv, o_ow, o_up, o_dn, o_sm,
     xg, cg, nrm, ctx, n2, hid, gbf, pq, wqkv, wout, wup, wdn, smg, vec, gvec, lse, mid, gmid,
-    gctx, dqkv, dkt, dvt, gpart, gown, grecv, opart, oown, orecv,
+    gctx, dkt, dvt, gpart, gown, grecv, opart, orecv, mask,
     dw_qkv, dw_out, dw_up, dw_dn, dw_sm, rr_qkv, rr_out, rr_up, rr_dn, rr_sm,
-    loc_sem, ag_s, ag_r, rg_s, rg_r, sq_s, sq_r, rs_s, rs_r, sa_s, sa_r, sg_s, sg_r,
+    loc_sem, ag_s, ag_r, rg_s, rg_r, sq_s, sq_r, rs_s, rs_r, sa_s, sa_r, sg_s, sg_r, sm_s, sm_r,
 ):
     D, T, TP, R, A, w, wf, HP = z["D"], z["T"], z["TP"], z["R"], z["A"], z["w"], z["wf"], z["HP"]
     N, H, DH, LB, g = 2 * A, A, D // 4, D // 128, z["g"]
@@ -97,12 +97,14 @@
             return pl.ds(pl.multiple_of(k * size, size), size)
         return pl.ds(pl.multiple_of(k * size + half * (size // 2), size // 2), size // 2)
 
+    OUT, UP, DN = HP, HP + 1, HP + 2
     blocks = {
-        0: lambda k, half=None: wqkv.at[rows_of(k, w, half)],
-        1: lambda k, half=None: wout.at[rows_of(k, w, half), quarter],
-        2: lambda k, half=None: wup.at[rows_of(k, w, half)],
-        3: lambda k, half=None: wdn.at[rows_of(k, wf, half)],
+        OUT: lambda k, half=None: wout.at[rows_of(k, w, half), quarter],
+        UP: lambda k, half=None: wup.at[rows_of(k, w, half)],
+        DN: lambda k, half=None: wdn.at[rows_of(k, wf, half)],
     }
+    for hp in range(HP):
+        blocks[hp] = lambda k, half=None, hp=hp: wqkv.at[rows_of(k, w, half), hp * 384 : hp * 384 + 384]
 
     def ag_block(m, way, d, back):
         k = ahead(-back if way == 0 else back)
@@ -156,6 +158,9 @@
 
     def c_slot(k):
         return cg.at[k]
+
+    def g_slot(k):
+        return nrm.at[k]
 
     def out_slot(k):
         return wout.at[:, pl.ds(pl.multiple_of(k * DH, DH), DH)]
@@ -283,12 +288,17 @@
         return jnp.concatenate([ref[...].astype(F32), jnp.zeros((TP - T, D), F32)], axis=0)
 
     barrier = pltpu.get_barrier_semaphore()
-    peers = [to_core, to_y] + [{"fsdp": other(d)} for d in range(1, N)]
+    peers = [to_core, to_y, {"seq": s_diag}] + [{"fsdp": other(d)} for d in range(1, N)]
     for dev in peers:
         pl.semaphore_signal(barrier, inc=1, device_id=dev, device_id_type=MESH)
     xg[s] = padded(tok).astype(BF)
     cg[s] = padded(cot).astype(BF)
     gvec[...] = jnp.zeros_like(gvec)
+    column = lax.broadcasted_iota(jnp.int32, (1, R), 1)
+    slot = sum((column >= TP * k).astype(jnp.int32) for k in range(1, 4))
+    inside = column - slot * TP
+    valid = (inside < T) & (slot * T + inside < len_in[0])
+    mask[...] = jnp.where(valid, 0.0, -1e30).astype(F32)
     for copy in local:
         copy.wait()
     pl.semaphore_wait(barrier, len(peers))
@@ -296,8 +306,8 @@
     for d in range(1, N):
         send(smg.at[f], smg.at[f], sa_s.at[d - 1], sa_r.at[d - 1], {"fsdp": other(d)})
     sq_send(KX, x_slot)
-    ag_own(0)
-    ag_own(1)
+    for m in (0, 1, OUT):
+        ag_own(m)
     sq_send(KC, c_slot)
     for d in range(1, N):
         arrive(smg.at[other(N - d)], sa_r.at[d - 1], to_ring[0])
@@ -310,53 +320,59 @@
     def row(k):
         return vec[k : k + 1, :]
 
-    def first_norm(k):
+    def first_norm(k, into=nrm):
         unit, _ = unit_rows(xg[k].astype(F32))
-        nrm[k] = (unit * row(0) + row(1)).astype(BF)
+        into[k] = (unit * row(0) + row(1)).astype(BF)
+
+    def project(hp):
+        cols = pl.ds(pl.multiple_of(s * DH + hp * 128, 128), 128)
+        bias = jnp.concatenate([vec[2:3, cols], jnp.zeros((1, 128), F32), vec[3:4, cols]], axis=1)
+        lanes = lax.broadcasted_iota(jnp.int32, (1, 384), 1)
+        scale = jnp.where(lanes < 128, HEAD_DIM ** (-0.5), 1.0).astype(F32)
+        here = slice(hp * 384, hp * 384 + 384)
+
+        @pl.loop(0, 4)
+        def _(k):
+            pq[k, :, here] = ((dot_nn(nrm[k], wqkv[:, here]) + bias) * scale).astype(BF)
 
     first_norm(s)
     ag_fwd(0, 0)
     sq_core(KX, x_slot)
     first_norm(s_core)
     ag_fwd(1, 0)
-    ag_own(2)
+    ag_fwd(OUT, 0)
+    ag_fwd(0, 1)
+    ag_fwd(1, 1)
+    ag_fwd(OUT, 1)
     sq_relay(KX, x_slot)
-    ag_fwd(0, 1)
     first_norm(s_y)
-    ag_fwd(1, 1)
+    ag_fwd(0, 2)
+    ag_fwd(1, 2)
+    ag_fwd(OUT, 2)
+    ag_own(UP)
+    ag_own(DN)
     sq_diag(KX, x_slot)
     first_norm(s_diag)
-    ag_fwd(0, 2)
-    ag_own(3)
-    ag_fwd(1, 2)
     ag_last(0)
-
-    pieces = []
-    for hp in range(HP):
-        cols = pl.ds(pl.multiple_of(s * DH + hp * 128, 128), 128)
-        pieces += [vec[2:3, cols], jnp.zeros((1, 128), F32), vec[3:4, cols]]
-    proj_bias = jnp.concatenate(pieces, axis=1)
-    lanes = lax.broadcasted_iota(jnp.int32, (1, HP * 384), 1)
-    proj_scale = jnp.where(lax.rem(lanes, 384) < 128, HEAD_DIM ** (-0.5), 1.0).astype(F32)
-
-    @pl.loop(0, 4)
-    def _(k):
-        value = dot_nn(nrm[k], wqkv[...]) + proj_bias
-        pq[k] = (value * proj_scale).astype(BF)
-
-    ag_last(1)
-    sq_send(KO, out_slot)
+    project(0)
 
     flat = pq.reshape(R, HP * 384)
     lane = lax.broadcasted_iota(jnp.int32, (1, 128), 1)
     first = (lane < HEAD_DIM).astype(F32)
     picks = (first.astype(BF), (1.0 - first).astype(BF))
 
-    def forward_tile(hp, k):
-        lo = hp * 384
-        query = pq[k, :, lo : lo + 128]
-        keys = flat[:, lo + 128 : lo + 256]
-        vals = flat[:, lo + 256 : lo + 384]
+    def lanes_at(off):
+        return pl.ds(pl.multiple_of(off, 128), 128)
+
+    def slot_rows(k):
+        return pl.ds(pl.multiple_of(k * TP, 16), TP)
+
+    @pl.loop(0, 8)
+    def _(t):
+        hp, k = lax.div(t, 4), lax.rem(t, 4)
+        query = pq[k, :, lanes_at(hp * 384)]
+        keys = flat[:, lanes_at(hp * 384 + 128)]
+        vals = flat[:, lanes_at(hp * 384 + 256)]
         both, logs = [], []
         for h in range(2):
             scores = dot_nt(query * picks[h], keys) + mask[...]
@@ -365,51 +381,51 @@
             total = jnp.sum(grown, axis=-1, keepdims=True)
             logs.append(top + jnp.log(total))
             both.append(dot_nn((grown * (1.0 / total)).astype(BF), vals))
-        here = jnp.where(lane < HEAD_DIM, both[0], both[1]).astype(BF)
-        rows = pl.ds(pl.multiple_of(k * TP, 16), TP)
-        ctx[s, rows, hp * 128 : hp * 128 + 128] = here
+        rows = slot_rows(k)
+        ctx[s, rows, lanes_at(hp * 128)] = jnp.where(lane < HEAD_DIM, both[0], both[1]).astype(BF)
         lse[hp, rows, :] = jnp.where(lane < HEAD_DIM, logs[0], logs[1])
 
-    for hp in range(HP):
-        @pl.loop(0, 4)
-        def _(i):
-            forward_tile(hp, i)
-
-            if hp < 2:
-                @pl.when(i == 1)
-                def _():
-                    ag_fwd(2, hp)
-
-                @pl.when(i == 3)
-                def _():
-                    ag_fwd(3, hp)
-
-        sq_send(KCTX + hp, ctx_slot(hp))
-        if hp == 0:
+        @pl.when(t == 0)
+        def _():
+            ag_last(OUT)
+            sq_send(KO, out_slot)
+            ag_last(1)
+            project(1)
+
+        @pl.when(t == 2)
+        def _():
+            ag_fwd(UP, 0)
             sq_relay(KC, c_slot)
-        if hp == 1:
-            sq_relay(KO, out_slot)
-            sq_relay(KCTX, ctx_slot(0))
-    for hp in range(HP, 2):
-        ag_fwd(2, hp)
-        ag_fwd(3, hp)
-    if HP == 1:
-        sq_relay(KO, out_slot)
-        sq_relay(KCTX, ctx_slot(0))
-    ag_fwd(2, 2)
+
+        @pl.when(t == 3)
+        def _():
+            sq_send(KCTX, ctx_slot(0))
+
+        @pl.when(t == 5)
+        def _():
+            ag_fwd(DN, 0)
+
+        @pl.when(t == 7)
+        def _():
+            sq_send(KCTX + 1, ctx_slot(1))
+
+    sq_relay(KO, out_slot)
+    ag_fwd(UP, 1)
+    sq_relay(KCTX, ctx_slot(0))
     sq_core(KO, out_slot)
     sq_diag(KO, out_slot)
-    for hp in range(1, HP):
-        sq_relay(KCTX + hp, ctx_slot(hp))
-    for hp in range(HP):
-        sq_core(KCTX + hp, ctx_slot(hp))
-        sq_diag(KCTX + hp, ctx_slot(hp))
+    sq_core(KCTX, ctx_slot(0))
+    sq_core(KCTX + 1, ctx_slot(1))
+    ag_fwd(DN, 1)
+    sq_relay(KCTX + 1, ctx_slot(1))
+    sq_diag(KCTX, ctx_slot(0))
+    sq_diag(KCTX + 1, ctx_slot(1))
+    ag_fwd(UP, 2)
 
     @pl.loop(0, 4)
     def _(i):
         k = order(i)
-        rows = pl.ds(pl.multiple_of(k * TP, 16), TP)
-        joined = jnp.concatenate([ctx[j, rows, :] for j in range(4)], axis=1)
+        joined = jnp.concatenate([ctx[j, slot_rows(k), :] for j in range(4)], axis=1)
         value = xg[k].astype(F32) + dot_nn(joined, wout[...]) + row(4)
         unit, _ = unit_rows(value)
         n2[k] = (unit * row(5) + row(6)).astype(BF)
@@ -418,17 +434,23 @@
         def _():
             mid[...] = value
 
-    sq_sent(KX, x_slot)
-    ag_fwd(3, 2)
-    ag_last(2)
+    ag_fwd(DN, 2)
+    sq_core(KC, c_slot)
+    sq_diag(KC, c_slot)
+    ag_last(UP)
+    ag_last(DN)
 
     @pl.loop(0, 4)
-    def _(k):
+    def _(i):
+        k = order(i)
         before = dot_nn(n2[k], wup[...]) + row(8)
         cdf = 0.5 + 0.5 * lax.erf(before * (0.5**0.5))
         slope = cdf + before * (jnp.exp(before * before * -0.5) * (1.0 / math.sqrt(2.0 * math.pi)))
         hid[k] = (before * cdf).astype(BF)
-        gbf[k] = slope.astype(BF)
+        grad = (dot_nt(cg[k], wdn[...]) * slope).astype(BF)
+        gbf[k] = grad
+        gvec[8:9, :] += jnp.sum(grad.astype(F32), axis=0, keepdims=True)
+        seq_stage(i, 0, gpart, gown, grecv, dot_nt(grad, wup[...]))
 
     def weight_grad(left, right, dw, size):
         per = max(256 // size, 1)
@@ -440,24 +462,16 @@
             for j in range(per):
                 dw[i * per + j] = value[j * size : (j + 1) * size]
 
-    sq_core(KC, c_slot)
-    sq_diag(KC, c_slot)
     weight_grad(hid.reshape(R, D), cg.reshape(R, D)[...], dw_dn, wf)
     rg_own(0)
-    ag_last(3)
-
-    @pl.loop(0, 4)
-    def _(i):
-        k = order(i)
-        grad = (dot_nt(cg[k], wdn[...]) * gbf[k].astype(F32)).astype(BF)
-        gbf[k] = grad
-        gvec[8:9, :] += jnp.sum(grad.astype(F32), axis=0, keepdims=True)
-        seq_stage(i, 0, gpart, gown, grecv, dot_nt(grad, wup[...]))
-        seq_stage(i, 1, opart, oown, orecv, dot_nn(hid[k], wdn[...]))
-
-    rg_fwd(0, 0)
     weight_grad(n2.reshape(R, D), gbf.reshape(R, D)[...], dw_up, w)
     rg_own(1)
+    rg_fwd(0, 0)
+
+    @pl.loop(0, 4)
+    def _(k):
+        first_norm(k, n2)
+
 
     gn = seq_total(0, gown, grecv)
     seq_sent(0, gpart)
@@ -470,38 +484,47 @@
     gmid[...] = gm
     branch = gm.astype(BF)
     gvec[4:5, :] = jnp.sum(branch.astype(F32), axis=0, keepdims=True)
-    xg[s] = branch
-    sq_send(KG, x_slot)
-    rg_fwd(0, 1)
+    nrm[s] = branch
+    sq_send(KG, g_slot)
+
+    @pl.loop(0, 4)
+    def _(i):
+        seq_stage(i, 1, opart, gown, orecv, dot_nn(hid[order(i)], wdn[...]))
+
     rg_fwd(1, 0)
-    sq_core(KG, x_slot)
-    out_total = seq_total(1, oown, orecv)
-    o_out[...] = (mid[...] + out_total + row(7))[:T].astype(BF)
-    sq_relay(KG, x_slot)
-    rg_fwd(0, 2)
-    sq_diag(KG, x_slot)
-
-    @pl.loop(0, 4)
-    def _(k):
-        gctx[k] = dot_nt(xg[k], wout[pl.ds(pl.multiple_of(s * DH, DH), DH), :]).astype(BF)
-
-    right = xg.reshape(R, D)[:, quarter]
-    for j in range(4):
-        value = dot_tn(ctx[j], right).astype(BF)
-        for i in range(DH // w):
-            dw_out[j * (DH // w) + i] = value[i * w : (i + 1) * w]
-    rg_own(2)
 
     flat_g = gctx.reshape(R, DH)
-    flat_d = dqkv.reshape(R, HP * 384)
-
-    def backward_tile(hp, rows):
+    dkt[...] = jnp.zeros_like(dkt)
+    dvt[...] = jnp.zeros_like(dvt)
+
+    def branch_back(k):
+        gctx[k] = dot_nt(nrm[k], wout[pl.ds(pl.multiple_of(s * DH, DH), DH), :]).astype(BF)
+
+    def close_pair(hp):
         lo = hp * 384
-        query = flat[rows, lo : lo + 128]
-        keys = flat[:, lo + 128 : lo + 256]
-        vals = flat[:, lo + 256 : lo + 384]
-        grad = flat_g[rows, hp * 128 : hp * 128 + 128]
-        logs = lse[hp, rows, :]
+        flat[:, lo + 128 : lo + 256] = dkt[hp].T.astype(BF)
+        flat[:, lo + 256 : lo + 384] = dvt[hp].T.astype(BF)
+        weight_grad(n2.reshape(R, D), flat[:, lo : lo + 384], dw_qkv.at[hp], w)
+        rg_own(3 + hp)
+        off = lanes_at(s * DH + hp * 128)
+        gvec[2:3, off] = jnp.sum(flat[:, lo : lo + 128].astype(F32), axis=0, keepdims=True)
+        gvec[3:4, off] = jnp.sum(flat[:, lo + 256 : lo + 384].astype(F32), axis=0, keepdims=True)
+
+    branch_back(s)
+    sq_core(KG, g_slot)
+    branch_back(s_core)
+
+    @pl.loop(0, 8)
+    def _(t):
+        late, u = lax.div(t, 4), lax.rem(t, 4)
+        hp = (1 - late) * lax.rem(u, 2) + late * lax.div(u, 2)
+        flip = (1 - late) * lax.div(u, 2) + late * lax.rem(u, 2)
+        k = lax.rem(y + late, 2) * 2 + lax.rem(c + flip, 2)
+        query = pq[k, :, lanes_at(hp * 384)]
+        keys = flat[:, lanes_at(hp * 384 + 128)]
+        vals = flat[:, lanes_at(hp * 384 + 256)]
+        grad = gctx[k, :, lanes_at(hp * 128)]
+        logs = lse[hp, slot_rows(k), :]
         both = []
         for h in range(2):
             qh, gh = query * picks[h], grad * picks[h]
@@ -510,82 +533,72 @@
             inner = jnp.sum(probs * dp, axis=-1, keepdims=True)
             ds = (probs * (dp - inner)).astype(BF)
             both.append(dot_nn(ds, keys))
-            dkt[...] += dot_tn(qh, ds)
-            dvt[...] += dot_tn(gh, probs.astype(BF))
+            dkt[hp] += dot_tn(qh, ds)
+            dvt[hp] += dot_tn(gh, probs.astype(BF))
         dq = jnp.where(lane < HEAD_DIM, both[0], both[1]) * HEAD_DIM ** (-0.5)
-        flat_d[rows, lo : lo + 128] = dq.astype(BF)
-
-    polls = {
-        (0, 0): lambda: rg_fwd(1, 1),
-        (0, 1): lambda: rg_fin(0),
-        (0, 2): lambda: rg_fwd(2, 0),
-        (0, 3): lambda: rg_fwd(1, 2),
-        (1, 0): lambda: rg_fwd(2, 1),
-        (1, 1): lambda: rg_fwd(3, 0),
-        (1, 2): lambda: rg_fin(1),
-        (1, 3): lambda: [rg_fwd(2, 2), rg_fwd(3, 1)],
-    }
-
-    def poll_at(poll):
-        poll()
-
-    full = R // 256
-    for hp in range(HP):
-        lo = hp * 384
-        dkt[...] = jnp.zeros_like(dkt)
-        dvt[...] = jnp.zeros_like(dvt)
-
-        @pl.loop(0, full)
-        def _(i):
-            backward_tile(hp, pl.ds(pl.multiple_of(i * 256, 256), 256))
-            for (which, when), poll in polls.items():
-                if which == hp and when < full:
-                    pl.when(i == when)(functools.partial(poll_at, poll))
-
-        if R % 256:
-            backward_tile(hp, pl.ds(full * 256, R % 256))
-        flat_d[:, lo + 128 : lo + 256] = dkt[...].T.astype(BF)
-        flat_d[:, lo + 256 : lo + 384] = dvt[...].T.astype(BF)
-        weight_grad(nrm.reshape(R, D), flat_d[:, lo : lo + 384], dw_qkv.at[hp], w)
-        rg_own(3 + hp)
-        off = pl.ds(pl.multiple_of(s * DH + hp * 128, 128), 128)
-        gvec[2:3, off] = jnp.sum(flat_d[:, lo : lo + 128].astype(F32), axis=0, keepdims=True)
-        gvec[3:4, off] = jnp.sum(flat_d[:, lo + 256 : lo + 384].astype(F32), axis=0, keepdims=True)
-    for (which, when), poll in polls.items():
-        if which >= HP or when >= full:
-            poll()
+        pq[k, :, lanes_at(hp * 384)] = dq.astype(BF)
+
+        @pl.when(t == 1)
+        def _():
+            rg_fwd(0, 1)
+
+        @pl.when(t == 3)
+        def _():
+            rg_fwd(1, 1)
+            sq_relay(KG, g_slot)
+            branch_back(s_y)
+            sq_diag(KG, g_slot)
+            branch_back(s_diag)
+            right = nrm.reshape(R, D)[:, quarter]
+            for j in range(4):
+                value = dot_tn(ctx[j], right).astype(BF)
+                for i in range(DH // w):
+                    dw_out[j * (DH // w) + i] = value[i * w : (i + 1) * w]
+            rg_own(2)
+
+        @pl.when(t == 4)
+        def _():
+            rg_fwd(0, 2)
+
+        @pl.when(t == 5)
+        def _():
+            close_pair(0)
+            rg_fwd(2, 0)
+
+        @pl.when(t == 6)
+        def _():
+            rg_fwd(1, 2)
+
+        @pl.when(t == 7)
+        def _():
+            rg_fwd(2, 1)
+
+    close_pair(1)
+    rg_fin(0)
+    out_total = seq_total(1, gown, orecv)
+    o_out[...] = (mid[...] + out_total + row(7))[:T].astype(BF)
 
     @pl.loop(0, 4)
     def _(i):
-        seq_stage(i, 2, gpart, gown, grecv, dot_nt(dqkv[order(i)], wqkv[...]))
-
-    last = 2 + HP
-    if HP > 1:
-        rg_fwd(3, 2)
-        rg_fwd(last, 0)
-    sq_relay(KFIN + 0, fin_slot(0))
-    rg_fin(2)
-    if HP > 1:
-        rg_fin(3)
-        rg_fwd(last, 1)
-        sq_relay(KFIN + 1, fin_slot(1))
-        sq_relay(KFIN + 2, fin_slot(2))
-        rg_fwd(last, 2)
-    else:
-        rg_fwd(3, 2)
-        sq_relay(KFIN + 1, fin_slot(1))
-        sq_relay(KFIN + 2, fin_slot(2))
-    gn = seq_total(2, gown, grecv)
-    unit, rate = unit_rows(padded(tok))
-    gvec[0:1, :] = jnp.sum(gn * unit, axis=0, keepdims=True)
-    gvec[1:2, :] = jnp.sum(gn, axis=0, keepdims=True)
+        seq_stage(i, 2, gpart, gown, grecv, dot_nt(pq[order(i)], wqkv[...]))
+
+    rg_fwd(3, 0)
+    rg_fwd(2, 2)
+    arrive(grecv.at[2], rs_r.at[2, 2], to_core)
+    here = gown[...] + grecv[2].astype(F32)
+    away = gpart[1].astype(F32)
+    unit, rate = unit_rows(xg[s].astype(F32))
+    unit_y, _ = unit_rows(xg[s_y].astype(F32))
+    gvec[0:1, :] = jnp.sum(here * unit + away * unit_y, axis=0, keepdims=True)
+    gvec[1:2, :] = jnp.sum(here + away, axis=0, keepdims=True)
     for k in range(N):
         j = k // g
         dw_sm[k] = gvec[:, j * 128 : (j + 1) * 128]
     for d in range(1, N):
         send(dw_sm.at[other(d)], rr_sm.at[d - 1], sg_s.at[d - 1], sg_r.at[d - 1], {"fsdp": other(d)})
-    o_tok[...] = (gmid[...] + norm_pull(gn, row(0), unit, rate))[:T].astype(BF)
-    rg_fin(last)
+    rg_fwd(4, 0)
+    rg_fin(1)
+    rg_fwd(3, 1)
     total = dw_sm[f]
     for d in range(1, N):
         arrive(rr_sm.at[d - 1], sg_r.at[d - 1], to_ring[0])
@@ -595,19 +608,36 @@
     def sm_slot(k):
         return o_sm.at[k]
 
-    sq_send(KFIN + MG, sm_slot)
-    finals = [(KFIN + m, fin_slot(m)) for m in range(MG)] + [(KFIN + MG, sm_slot)]
-    for kind, ref in finals[3:]:
+    three = ((to_core, s_core), (to_y, s_y), ({"seq": s_diag}, s_diag))
+    for d, (dev, _) in enumerate(three):
+        send(o_sm.at[s], o_sm.at[s], sm_s.at[d], sm_r.at[d], dev)
+    rg_fwd(4, 1)
+    rg_fin(2)
+    rg_fwd(3, 2)
+    sq_relay(KFIN + 0, fin_slot(0))
+    rg_fwd(4, 2)
+    arrive(grecv.at[1], rs_r.at[2, 1], to_y)
+    gn = here + grecv[1].astype(F32)
+    o_tok[...] = (gmid[...] + norm_pull(gn, row(0), unit, rate))[:T].astype(BF)
+    rg_fin(3)
+    sq_relay(KFIN + 1, fin_slot(1))
+    rg_fin(4)
+    sq_relay(KFIN + 2, fin_slot(2))
+    finals = [(KFIN + m, fin_slot(m)) for m in range(MG)]
+    for kind, ref in (finals[3], finals[4]):
         sq_relay(kind, ref)
     for kind, ref in finals:
         sq_core(kind, ref)
         sq_diag(kind, ref)
-
-    for m in range(4):
+    for d, (dev, k) in enumerate(three):
+        arrive(o_sm.at[k], sm_r.at[d], dev)
+        sent(o_sm.at[s], sm_s.at[d], dev)
+
+    for m in range(3 + HP):
         ag_sent(m)
     for m in range(MG):
         rg_sent(m)
-    for kind, ref in [(KC, c_slot), (KG, x_slot), (KO, out_slot)] + finals:
+    for kind, ref in [(KX, x_slot), (KC, c_slot), (KG, g_slot), (KO, out_slot)] + finals:
         sq_sent(kind, ref)
     for hp in range(HP):
         sq_sent(KCTX + hp, ctx_slot(hp))
@@ -616,6 +646,33 @@
     for d in range(1, N):
         sent(smg.at[f], sa_s.at[d - 1], to_ring[0])
         sent(dw_sm.at[other(d)], sg_s.at[d - 1], to_ring[0])
+
+
+def finish_kernel(z, out, tok, gq, go, gu, gd, gs, *outs):
+    o_out, o_tok, o_qkv, o_ow, o_up, o_dn = outs[:6]
+    D, wf, HP, N = z["D"], z["wf"], z["HP"], 2 * z["A"]
+    DH = D // 4
+    for s in range(4):
+        for hp in range(HP):
+            for part in range(3):
+                lo = part * D + s * DH + hp * 128
+                o_qkv[:, lo : lo + 128] = gq[hp, s, :, part * 128 : part * 128 + 128].astype(F32)
+        o_ow[:, s * DH : (s + 1) * DH] = go[s].astype(F32)
+        if z["up_whole"]:
+            for k in range(N):
+                o_up[:, (k * 4 + s) * wf : (k * 4 + s + 1) * wf] = gu[s, :, k * wf : (k + 1) * wf].astype(F32)
+    if not z["up_whole"]:
+        o_up[...] = gu[...].astype(F32)
+    o_dn[...] = gd[0].astype(F32)
+
+    @pl.when(pl.program_id(0) == 0)
+    def _():
+        o_out[...] = out[...]
+        o_tok[...] = tok[...]
+        total = gs[0] + gs[1] + gs[2] + gs[3]
+        for k in range(8):
+            outs[6 + k][...] = total[k : k + 1]
+        outs[14][...] = jnp.concatenate([gs[s, 8:9] for s in range(4)], axis=1)
 
 
 def make_body(mesh):
@@ -634,24 +691,22 @@
         DH = D // 4
         HP = DH // 128
         FQ = FF // 4
-        assert FQ == D and wf == w
+        assert FQ == D and wf == w and HP == 2
         g = max(128 // w, 1)
         s = lax.axis_index("seq")
         f = lax.axis_index("fsdp")
         up_whole = wf % 128 == 0
         ub = lax.dynamic_slice(up_bias, (s * wf,), (wf,))
-        packed = jnp.stack([ln1_gain, ln1_bias, q_bias, v_bias, out_bias, ln2_gain, ln2_bias, down_bias, ub])
+        packed = jnp.stack(
+            [ln1_gain, ln1_bias, q_bias, v_bias, out_bias, ln2_gain, ln2_bias, down_bias, ub]
+            + [jnp.zeros_like(ub)] * 7
+        )
         if g == 1:
-            small = jnp.pad(packed, ((0, 7), (0, 0)))
+            small = packed
         else:
             small = lax.dynamic_update_slice(jnp.zeros((16, 128), BF), packed, (0, lax.rem(f, g) * w))
         if not up_whole:
             up_weight = lax.dynamic_index_in_dim(up_weight.reshape(w, N, 4, wf), s, 2, False).reshape(w, FQ)
-        place = jnp.arange(R)
-        slot, inside = place // TP, place % TP
-        valid = (inside < T) & (slot * T + inside < lengths[0])
-        mask = jnp.where(valid, 0.0, -1e30).astype(F32)[None, :]
-
         z = dict(D=D, T=T, TP=TP, R=R, A=A, w=w, wf=wf, HP=HP, g=g, up_whole=up_whole)
         vm = pltpu.VMEM
         C = 384
@@ -675,21 +730,21 @@
             vm((TP, D), F32),
             vm((TP, D), F32),
             vm((4, TP, DH), BF),
-            vm((4, TP, HP * C), BF),
-            vm((128, R), F32),
-            vm((128, R), F32),
+            vm((HP, 128, R), F32),
+            vm((HP, 128, R), F32),
             vm((3, TP, D), BF), vm((TP, D), F32), vm((3, TP, D), BF),
-            vm((3, TP, D), BF), vm((TP, D), F32), vm((3, TP, D), BF),
+            vm((3, TP, D), BF), vm((3, TP, D), BF),
+            vm((1, R), F32),
             vm((HP, N, w, C), BF), vm((N, w, DH), BF), vm((N, w, FQ), BF), vm((N, wf, D), BF), vm((N, 16, 128), F32),
             vm((HP, 2, A, w, C), BF), vm((2, A, w, DH), BF), vm((2, A, w, FQ), BF), vm((2, A, wf, D), BF), vm((N - 1, 16, 128), F32),
         ]
         dma = pltpu.SemaphoreType.DMA
         scratch += [
             dma((3 + 3 * HP + (N if up_whole else 1),)),
-            dma((4, 2, A)), dma((4, 2, A)), dma((3 + HP, 2, A)), dma((3 + HP, 2, A)),
-            dma((8 + 2 * HP, 3)), dma((8 + 2 * HP, 3)),
+            dma((3 + HP, 2, A)), dma((3 + HP, 2, A)), dma((3 + HP, 2, A)), dma((3 + HP, 2, A)),
+            dma((7 + 2 * HP, 3)), dma((7 + 2 * HP, 3)),
             dma((3, 3)), dma((3, 3)),
-            dma((N - 1,)), dma((N - 1,)), dma((N - 1,)), dma((N - 1,)),
+            dma((N - 1,)), dma((N - 1,)), dma((N - 1,)), dma((N - 1,)), dma((3,)), dma((3,)),
         ]
         here = pl.BlockSpec(memory_space=pltpu.VMEM)
         there = pl.BlockSpec(memory_space=pl.ANY)
@@ -705,25 +760,54 @@
         out, gtok, gq, go, gu, gd, gs = pl.pallas_call(
             functools.partial(layer_kernel, z),
             out_shape=out_shapes,
-            in_specs=[here, here, here, there, there, there, there, there],
+            in_specs=[here, here, pl.BlockSpec(memory_space=pltpu.SMEM), there, there, there, there, there],
             out_specs=[here] * 7,
             scratch_shapes=scratch,
             compiler_params=pltpu.CompilerParams(
                 collective_id=0, has_side_effects=True, vmem_limit_bytes=67_000_000
             ),
             name="layer",
-        )(tokens[0], cotangent[0], mask, small, qkv_weight, out_weight, up_weight, down_weight)
-
-        g_qkv = gq.reshape(HP, 4, w, 3, 128).transpose(2, 3, 1, 0, 4).reshape(w, 3 * D).astype(F32)
-        g_out = go.transpose(1, 0, 2).reshape(w, D).astype(F32)
-        g_up = gu.reshape(4, w, N, wf).transpose(1, 2, 0, 3).reshape(w, FF).astype(F32)
-        g_down = gd.reshape(4 * wf, D).astype(F32)
+        )(tokens[0], cotangent[0], lengths, small, qkv_weight, out_weight, up_weight, down_weight)
+
+        if not up_whole:
+            gu = gu.reshape(4, w, N, wf).transpose(1, 2, 0, 3).reshape(w, FF)
         if g > 1:
             gs = lax.dynamic_slice(gs, (0, 0, lax.rem(f, g) * w), (4, 16, w))
-        sums = jnp.sum(gs[:, :8], axis=0)
+        parts = 4
+        rb = w // parts
+        whole = lambda shape: pl.BlockSpec(shape, lambda i: (0,) * len(shape))
+        vectors = [jax.ShapeDtypeStruct((1, w), F32)] * 8 + [jax.ShapeDtypeStruct((1, 4 * wf), F32)]
+        up_spec = pl.BlockSpec((4, rb, FQ), lambda i: (0, i, 0)) if up_whole else pl.BlockSpec((rb, FF), lambda i: (i, 0))
+        done = pl.pallas_call(
+            functools.partial(finish_kernel, z),
+            grid=(parts,),
+            out_shape=[
+                jax.ShapeDtypeStruct((T, D), BF), jax.ShapeDtypeStruct((T, D), BF),
+                jax.ShapeDtypeStruct((w, 3 * D), F32), jax.ShapeDtypeStruct((w, D), F32),
+                jax.ShapeDtypeStruct((w, FF), F32), jax.ShapeDtypeStruct((4 * wf, D), F32),
+            ] + vectors,
+            in_specs=[
+                whole((T, D)), whole((T, D)),
+                pl.BlockSpec((HP, 4, rb, C), lambda i: (0, 0, i, 0)),
+                pl.BlockSpec((4, rb, DH), lambda i: (0, i, 0)),
+                up_spec,
+                pl.BlockSpec((1, wf, D), lambda i: (i, 0, 0)),
+                whole((4, 16, w)),
+            ],
+            out_specs=[
+                whole((T, D)), whole((T, D)),
+                pl.BlockSpec((rb, 3 * D), lambda i: (i, 0)),
+                pl.BlockSpec((rb, D), lambda i: (i, 0)),
+                pl.BlockSpec((rb, FF), lambda i: (i, 0)),
+                pl.BlockSpec((wf, D), lambda i: (i, 0)),
+            ] + [whole((1, w))] * 8 + [whole((1, 4 * wf))],
+            name="finish",
+        )(out, gtok, gq, go, gu, gd, gs)
+        out, gtok, g_qkv, g_out, g_up, g_down = done[:6]
+        sums = [v.reshape(-1) for v in done[6:]]
         return (
             out[None], gtok[None], sums[0], sums[1], g_qkv, sums[2], sums[3], g_out, sums[4],
-            sums[5], sums[6], g_up, gs[:, 8].reshape(4 * wf), g_down, sums[7],
+            sums[5], sums[6], g_up, sums[8], g_down, sums[7],
         )
 
     return body

time: 201 us -> 170 us (0.85)
  Pallas kernels: 182 us -> 166 us
  local copies, waits for them, and re-layouts: 13.7 us -> 2.08 us
  other arithmetic: 3.02 us -> 0 us
    pallas_call x1, Pallas kernels: 182 us -> 160 us  [body(): pl.pallas_call(functools.partial(layer_kernel, z), out_shape=out_shapes,...]
    unnamed x17 -> x2, local copies, waits for them, and re-layouts: 6.39 us -> 0.02 us
    pallas_call x0 -> x1, Pallas kernels: none -> 6.06 us  [body(): pl.pallas_call(functools.partial(finish_kernel, z), grid=(parts,), out_sh...]
    convert_element_type x6 -> x0, local copies, waits for them, and re-layouts: 3.97 us -> none  [the longest x3 3.34 us: body(): gu.reshape(4, w, N, wf).transpose(1, 2, 0, 3).reshape(w, FF).astype(F32)]
where the time goes in v3:
time: 170 us
  Pallas kernels  166 us (98%)
  local copies, waits for them, and re-layouts  2.08 us (1%)
    pallas_call x1, Pallas kernels, body(): pl.pallas_call(functools.partial(layer_kernel, z), out_shape=out_shapes,...  160 us
    pallas_call x1, Pallas kernels, body(): pl.pallas_call(functools.partial(finish_kernel, z), grid=(parts,), out_sh...  6.06 us

profile of v3, /device:TPU:0, one launch (start us, length us, event | category | flops | bytes accessed | tf_op | source)
XLA Modules:
  0.0 169.7 jit_solution(9624869209413346262)
XLA Ops:
  0.6 0.0 copy-start
  1.3 0.0 copy-done
  1.3 0.1 dynamic-slice_bitcast_fusion
  1.4 2.0 %stack.47.sm_in = bf16[16,128]{1,0:T(8,128)(2,1)} concatenate(bf16[1,128]{1,0:T(2,128)(2,1)} %bitcast.25, bf16[1,128]{1,0:T(2,128)(2,1)} %bitcast.26, bf16[1,128]{1,0:T(2,128)(2,1)} %bitcast.27, bf16[1,128]{1,0:T(2,128)(2,1)} %bitcast.28, bf16[1,128]{1,0:T(2,128)(2,1)} %bitcast.29, bf16[1,128]{1,0:T(2,128)(2,1)} %bitcast.30, bf16[1,128]{1,0:T(2,128)(2,1)} %bitcast.31, ...), dimensions={0} | concatenate | bytes 8192 | tf_op jit(solution)/shard_map/stack | solution.py:700
  3.4 160.1 %layer.1 = (bf16[258,1024]{1,0:T(8,128)(2,1)}, bf16[258,1024]{1,0:T(8,128)(2,1)}, bf16[2,4,128,384]{3,2,1,0:T(8,128)(2,1)}, bf16[4,128,256]{2,1,0:T(8,128)(2,1)}...) custom-call(bf16[258,1024]{1,0:T(8,128)(2,1)} %bitcast.23, ...), custom_call_target="tpu_custom_call" | custom-call | tf_op jit(solution)/shard_map/layer/pallas_call | solution.py:760
  163.5 6.1 %finish.1 = (bf16[258,1024]{1,0:T(8,128)(2,1)}, bf16[258,1024]{1,0:T(8,128)(2,1)}, f32[128,3072]{1,0:T(8,128)}, f32[128,1024]{1,0:T(8,128)}, f32[128,4096]{1,0:T...) custom-call(bf16[258,1024]{1,0:T(8,128)(2,1)} %get-tuple-element.37., ...), custom_call_target="tpu_custom_call" | custom-call | tf_op jit(solution)/shard_map/finish/pallas_call | solution.py:781
  (3 shorter events, 0.0 us)
Async XLA Ops:
  0.6 0.7 copy-start

commit v4 on v3

--- a/solution.py
+++ b/solution.py
@@ -41,14 +41,19 @@
     )
 
 
+def layer_entry(z, *refs):
+    layer_kernel(z, *refs[:3], refs[3:11], *refs[11:])
+
+
 def layer_kernel(
     z,
-    tok, cot, len_in, sm_in, qkv_in, out_in, up_in, dn_in,
-    o_out, o_tok, o_qkv, o_ow, o_up, o_dn, o_sm,
+    tok_in, cot_in, len_in, vecs_in, ub_in, qkv_in, out_in, up_in, dn_in,
+    h_out, h_tok, h_qkv, h_ow, h_up, h_dn, h_sm,
+    tok, cot, lens, vecs, ub4, o_qkv, o_ow, o_up, o_dn, o_sm,
     xg, cg, nrm, ctx, n2, hid, gbf, pq, wqkv, wout, wup, wdn, smg, vec, gvec, lse, mid, gmid,
-    gctx, dkt, dvt, gpart, gown, grecv, opart, orecv, mask,
+    gctx, dkt, dvt, gpart, gown, grecv, opart, oown, orecv, mask,
     dw_qkv, dw_out, dw_up, dw_dn, dw_sm, rr_qkv, rr_out, rr_up, rr_dn, rr_sm,
-    loc_sem, ag_s, ag_r, rg_s, rg_r, sq_s, sq_r, rs_s, rs_r, sa_s, sa_r, sg_s, sg_r, sm_s, sm_r,
+    loc_sem, put_sem, ag_s, ag_r, rg_s, rg_r, sq_s, sq_r, rs_s, rs_r, sa_s, sa_r, sg_s, sg_r, sm_s, sm_r,
 ):
     D, T, TP, R, A, w, wf, HP = z["D"], z["T"], z["TP"], z["R"], z["A"], z["w"], z["wf"], z["HP"]
     N, H, DH, LB, g = 2 * A, A, D // 4, D // 128, z["g"]
@@ -113,14 +118,14 @@
     def ag_own(m):
         for way in range(2):
             ref = ag_block(m, way, 1, 0)
-            send(ref, ref, ag_s.at[m, way, 0], ag_r.at[m, way, 0], to_ring[way])
+            send(ref, ref, ag_s.at[m], ag_r.at[m, way, 0], to_ring[way])
 
     def ag_take(m, d):
         for way in range(2):
             arrive(ag_block(m, way, d, d), ag_r.at[m, way, d - 1], to_ring[way])
             if d < H:
                 ref = ag_block(m, way, d + 1, d)
-                send(ref, ref, ag_s.at[m, way, d], ag_r.at[m, way, d], to_ring[way])
+                send(ref, ref, ag_s.at[m], ag_r.at[m, way, d], to_ring[way])
 
     def ag_fwd(m, third):
         for d in thirds(1, H)[third]:
@@ -130,28 +135,26 @@
         ag_take(m, H)
 
     def ag_sent(m):
-        for way in range(2):
-            for d in range(1, H + 1):
-                sent(ag_block(m, way, d, d - 1), ag_s.at[m, way, d - 1], to_ring[way])
+        size = (N - 1) * (wf if m == DN else w)
+        every = {OUT: wout.at[:size, quarter], UP: wup.at[:size], DN: wdn.at[:size]}
+        sent(every[m] if m in every else wqkv.at[:size, m * 384 : m * 384 + 384], ag_s.at[m], to_ring[0])
 
     def sq_send(kind, ref):
-        send(ref(s), ref(s), sq_s.at[kind, 0], sq_r.at[kind, 0], to_core)
-        send(ref(s), ref(s), sq_s.at[kind, 1], sq_r.at[kind, 1], to_y)
+        send(ref(s), ref(s), sq_s.at[kind], sq_r.at[kind, 0], to_core)
+        send(ref(s), ref(s), sq_s.at[kind], sq_r.at[kind, 1], to_y)
 
     def sq_core(kind, ref):
         arrive(ref(s_core), sq_r.at[kind, 0], to_core)
 
     def sq_relay(kind, ref):
         arrive(ref(s_y), sq_r.at[kind, 1], to_y)
-        send(ref(s_y), ref(s_y), sq_s.at[kind, 2], sq_r.at[kind, 2], to_core)
+        send(ref(s_y), ref(s_y), sq_s.at[kind], sq_r.at[kind, 2], to_core)
 
     def sq_diag(kind, ref):
         arrive(ref(s_diag), sq_r.at[kind, 2], to_core)
 
-    def sq_sent(kind, ref):
-        sent(ref(s), sq_s.at[kind, 0], to_core)
-        sent(ref(s), sq_s.at[kind, 1], to_y)
-        sent(ref(s_y), sq_s.at[kind, 2], to_core)
+    def sq_sent(kind, three):
+        sent(three, sq_s.at[kind], to_core)
 
     def x_slot(k):
         return xg.at[k]
@@ -174,32 +177,35 @@
         hb, lb = lax.div(3 - i, 2), lax.rem(3 - i, 2)
         return lax.rem(y + hb, 2) * 2 + lax.rem(c + lb, 2)
 
-    def seq_stage(i, kind, part, own, recv, value):
+    def seq_across(kind, part, recv):
+        send(part.at[1], recv.at[1], rs_s.at[kind], rs_r.at[kind, 1], to_y)
+
+    def seq_stage(i, kind, part, own, recv, value, defer=False):
         @pl.when(i < 3)
         def _():
             part[jnp.minimum(i, 2)] = value.astype(BF)
 
         @pl.when(i == 0)
         def _():
-            send(part.at[0], recv.at[0], rs_s.at[kind, 0], rs_r.at[kind, 0], to_core)
+            send(part.at[0], recv.at[0], rs_s.at[kind], rs_r.at[kind, 0], to_core)
 
         @pl.when(i == 1)
         def _():
             arrive(recv.at[0], rs_r.at[kind, 0], to_core)
             part[1] = (part[1].astype(F32) + recv[0].astype(F32)).astype(BF)
-            send(part.at[1], recv.at[1], rs_s.at[kind, 1], rs_r.at[kind, 1], to_y)
+            if not defer:
+                seq_across(kind, part, recv)
 
         @pl.when(i == 2)
         def _():
-            send(part.at[2], recv.at[2], rs_s.at[kind, 2], rs_r.at[kind, 2], to_core)
+            send(part.at[2], recv.at[2], rs_s.at[kind], rs_r.at[kind, 2], to_core)
 
         @pl.when(i == 3)
         def _():
             own[...] = value
 
     def seq_sent(kind, part):
-        for j in range(3):
-            sent(part.at[j], rs_s.at[kind, j], to_core)
+        sent(part, rs_s.at[kind], to_core)
 
     def seq_total(kind, own, recv):
         arrive(recv.at[2], rs_r.at[kind, 2], to_core)
@@ -223,7 +229,7 @@
 
     def rg_send(m, way, j):
         dst = grads[m][1].at[way, j, rg_rows(m, way, j)]
-        send(rg_src(m, way, j), dst, rg_s.at[m, way, j], rg_r.at[m, way, j], to_ring[way])
+        send(rg_src(m, way, j), dst, rg_s.at[m], rg_r.at[m, way, j], to_ring[way])
 
     def rg_arrive(m, way, j):
         arrive(grads[m][1].at[way, j, rg_rows(m, way, j)], rg_r.at[m, way, j], to_ring[way])
@@ -255,62 +261,69 @@
         sq_send(KFIN + m, fin_slot(m))
 
     def rg_sent(m):
-        for way in range(2):
-            for j in range(H):
-                sent(rg_src(m, way, j), rg_s.at[m, way, j], to_ring[way])
+        sent(grads[m][0].at[: N - 1], rg_s.at[m], to_ring[0])
 
     def other(d):
         return lax.rem(f + d, N)
 
-    local = []
-
-    def bring(src, dst):
-        copy = pltpu.make_async_copy(src, dst, loc_sem.at[len(local)])
-        copy.start()
-        local.append(copy)
-
-    bring(sm_in, smg.at[f])
+    barrier = pltpu.get_barrier_semaphore()
+    peers = [to_core, to_y, {"seq": s_diag}] + [{"fsdp": other(d)} for d in range(1, N)]
+    for dev in peers:
+        pl.semaphore_signal(barrier, inc=1, device_id=dev, device_id_type=MESH)
+
+    def bring(k, src, dst):
+        pltpu.make_async_copy(src, dst, loc_sem.at[k]).start()
+
+    bring(0, tok_in, tok)
+    for k in range(8):
+        bring(1, vecs_in[k], vecs.at[k])
+    bring(2, ub_in, ub4)
     for hp in range(HP):
         for part in range(3):
             cols = pl.ds(pl.multiple_of(part * D + s * DH + hp * 128, 128), 128)
             lo = hp * 384 + part * 128
-            bring(qkv_in.at[:, cols], wqkv.at[rows_of(f, w), lo : lo + 128])
-    bring(out_in.at[:, quarter], wout.at[rows_of(f, w), quarter])
+            bring(3, qkv_in.at[:, cols], wqkv.at[rows_of(f, w), lo : lo + 128])
+    bring(4, out_in.at[:, quarter], wout.at[rows_of(f, w), quarter])
+    bring(5, cot_in, cot)
+    bring(6, len_in, lens)
     if z["up_whole"]:
         for k in range(N):
             cols = pl.ds(pl.multiple_of((k * 4 + s) * wf, wf), wf)
-            bring(up_in.at[:, cols], wup.at[rows_of(f, w), k * wf : (k + 1) * wf])
+            bring(7, up_in.at[:, cols], wup.at[rows_of(f, w), k * wf : (k + 1) * wf])
     else:
-        bring(up_in, wup.at[rows_of(f, w)])
-    bring(dn_in.at[rows_of(s, wf)], wdn.at[rows_of(f, wf)])
+        bring(7, up_in, wup.at[rows_of(f, w)])
+    bring(8, dn_in.at[rows_of(s, wf)], wdn.at[rows_of(f, wf)])
+
+    def put(src, dst, k):
+        pltpu.make_async_copy(src, dst, put_sem.at[k]).start()
 
     def padded(ref):
         return jnp.concatenate([ref[...].astype(F32), jnp.zeros((TP - T, D), F32)], axis=0)
 
-    barrier = pltpu.get_barrier_semaphore()
-    peers = [to_core, to_y, {"seq": s_diag}] + [{"fsdp": other(d)} for d in range(1, N)]
-    for dev in peers:
-        pl.semaphore_signal(barrier, inc=1, device_id=dev, device_id_type=MESH)
+    gvec[...] = jnp.zeros_like(gvec)
+    own_rows = [tok, vecs, ub4, wqkv.at[rows_of(f, w)], wout.at[rows_of(f, w), quarter], cot, lens, wup.at[rows_of(f, w)], wdn.at[rows_of(f, wf)]]
+    for k, dst in enumerate(own_rows):
+        pltpu.make_async_copy(dst, dst, loc_sem.at[k]).wait()
+    quarters = ub4[...].astype(F32)
+    ub = sum(quarters[k : k + 1] * (s == k).astype(F32) for k in range(4))
+    vector_rows = [vecs[k].astype(F32) for k in range(8)] + [ub, jnp.zeros((7, 128), F32)]
+    smg[f] = jnp.concatenate(vector_rows, axis=0).astype(BF)
     xg[s] = padded(tok).astype(BF)
     cg[s] = padded(cot).astype(BF)
-    gvec[...] = jnp.zeros_like(gvec)
     column = lax.broadcasted_iota(jnp.int32, (1, R), 1)
     slot = sum((column >= TP * k).astype(jnp.int32) for k in range(1, 4))
     inside = column - slot * TP
-    valid = (inside < T) & (slot * T + inside < len_in[0])
+    valid = (inside < T) & (slot * T + inside < lens[0])
     mask[...] = jnp.where(valid, 0.0, -1e30).astype(F32)
-    for copy in local:
-        copy.wait()
     pl.semaphore_wait(barrier, len(peers))
 
     for d in range(1, N):
-        send(smg.at[f], smg.at[f], sa_s.at[d - 1], sa_r.at[d - 1], {"fsdp": other(d)})
+        send(smg.at[f], smg.at[f], sa_s.at[0], sa_r.at[0], {"fsdp": other(d)})
     sq_send(KX, x_slot)
     for m in (0, 1, OUT):
         ag_own(m)
     sq_send(KC, c_slot)
-    for d in range(1, N):
-        arrive(smg.at[other(N - d)], sa_r.at[d - 1], to_ring[0])
+    arrive(smg.at[: N - 1], sa_r.at[0], to_ring[0])
     for j in range(LB):
         piece = smg[j * g].astype(F32)
         for i in range(1, g):
@@ -401,8 +414,9 @@
         def _():
             sq_send(KCTX, ctx_slot(0))
 
-        @pl.when(t == 5)
-        def _():
+        @pl.when(t == 6)
+        def _():
+            ag_fwd(UP, 1)
             ag_fwd(DN, 0)
 
         @pl.when(t == 7)
@@ -410,17 +424,15 @@
             sq_send(KCTX + 1, ctx_slot(1))
 
     sq_relay(KO, out_slot)
-    ag_fwd(UP, 1)
     sq_relay(KCTX, ctx_slot(0))
     sq_core(KO, out_slot)
     sq_diag(KO, out_slot)
     sq_core(KCTX, ctx_slot(0))
     sq_core(KCTX + 1, ctx_slot(1))
-    ag_fwd(DN, 1)
+    ag_fwd(UP, 2)
     sq_relay(KCTX + 1, ctx_slot(1))
     sq_diag(KCTX, ctx_slot(0))
     sq_diag(KCTX + 1, ctx_slot(1))
-    ag_fwd(UP, 2)
 
     @pl.loop(0, 4)
     def _(i):
@@ -434,23 +446,23 @@
         def _():
             mid[...] = value
 
-    ag_fwd(DN, 2)
+        @pl.when(i == 0)
+        def _():
+            ag_fwd(DN, 1)
+
     sq_core(KC, c_slot)
     sq_diag(KC, c_slot)
     ag_last(UP)
-    ag_last(DN)
 
     @pl.loop(0, 4)
-    def _(i):
-        k = order(i)
+    def _(k):
         before = dot_nn(n2[k], wup[...]) + row(8)
         cdf = 0.5 + 0.5 * lax.erf(before * (0.5**0.5))
         slope = cdf + before * (jnp.exp(before * before * -0.5) * (1.0 / math.sqrt(2.0 * math.pi)))
         hid[k] = (before * cdf).astype(BF)
-        grad = (dot_nt(cg[k], wdn[...]) * slope).astype(BF)
-        gbf[k] = grad
-        gvec[8:9, :] += jnp.sum(grad.astype(F32), axis=0, keepdims=True)
-        seq_stage(i, 0, gpart, gown, grecv, dot_nt(grad, wup[...]))
+        gbf[k] = slope.astype(BF)
+
+    ag_fwd(DN, 2)
 
     def weight_grad(left, right, dw, size):
         per = max(256 // size, 1)
@@ -464,14 +476,34 @@
 
     weight_grad(hid.reshape(R, D), cg.reshape(R, D)[...], dw_dn, wf)
     rg_own(0)
+    ag_last(DN)
+
+    @pl.loop(0, 4)
+    def _(i):
+        k = order(i)
+        grad = (dot_nt(cg[k], wdn[...]) * gbf[k].astype(F32)).astype(BF)
+        gbf[k] = grad
+        gvec[8:9, :] += jnp.sum(grad.astype(F32), axis=0, keepdims=True)
+        seq_stage(i, 0, gpart, gown, grecv, dot_nt(grad, wup[...]))
+
+        @pl.when(i == 2)
+        def _():
+            rg_fwd(0, 0)
+
     weight_grad(n2.reshape(R, D), gbf.reshape(R, D)[...], dw_up, w)
     rg_own(1)
-    rg_fwd(0, 0)
 
     @pl.loop(0, 4)
     def _(k):
         first_norm(k, n2)
 
+    rg_fwd(0, 1)
+
+    @pl.loop(0, 4)
+    def _(i):
+        seq_stage(i, 1, opart, oown, orecv, dot_nn(hid[order(i)], wdn[...]), defer=True)
+
+    rg_fwd(1, 0)
 
     gn = seq_total(0, gown, grecv)
     seq_sent(0, gpart)
@@ -487,11 +519,7 @@
     nrm[s] = branch
     sq_send(KG, g_slot)
 
-    @pl.loop(0, 4)
-    def _(i):
-        seq_stage(i, 1, opart, gown, orecv, dot_nn(hid[order(i)], wdn[...]))
-
-    rg_fwd(1, 0)
+    seq_across(1, opart, orecv)
 
     flat_g = gctx.reshape(R, DH)
     dkt[...] = jnp.zeros_like(dkt)
@@ -538,13 +566,16 @@
         dq = jnp.where(lane < HEAD_DIM, both[0], both[1]) * HEAD_DIM ** (-0.5)
         pq[k, :, lanes_at(hp * 384)] = dq.astype(BF)
 
+        @pl.when(t == 0)
+        def _():
+            rg_fwd(0, 2)
+
         @pl.when(t == 1)
         def _():
-            rg_fwd(0, 1)
+            rg_fwd(1, 1)
 
         @pl.when(t == 3)
         def _():
-            rg_fwd(1, 1)
             sq_relay(KG, g_slot)
             branch_back(s_y)
             sq_diag(KG, g_slot)
@@ -555,35 +586,44 @@
                 for i in range(DH // w):
                     dw_out[j * (DH // w) + i] = value[i * w : (i + 1) * w]
             rg_own(2)
+            rg_fin(0)
 
         @pl.when(t == 4)
         def _():
-            rg_fwd(0, 2)
+            rg_fwd(2, 0)
+            rg_fwd(1, 2)
 
         @pl.when(t == 5)
         def _():
             close_pair(0)
-            rg_fwd(2, 0)
+            rg_fwd(2, 1)
 
         @pl.when(t == 6)
         def _():
-            rg_fwd(1, 2)
+            rg_fin(1)
 
         @pl.when(t == 7)
         def _():
-            rg_fwd(2, 1)
+            rg_fwd(3, 0)
+            rg_fwd(2, 2)
 
     close_pair(1)
-    rg_fin(0)
-    out_total = seq_total(1, gown, orecv)
-    o_out[...] = (mid[...] + out_total + row(7))[:T].astype(BF)
+    rg_fwd(3, 1)
 
     @pl.loop(0, 4)
     def _(i):
         seq_stage(i, 2, gpart, gown, grecv, dot_nt(pq[order(i)], wqkv[...]))
 
-    rg_fwd(3, 0)
-    rg_fwd(2, 2)
+        @pl.when(i == 2)
+        def _():
+            rg_fwd(4, 0)
+            rg_fwd(3, 2)
+
+    arrive(orecv.at[2], rs_r.at[1, 2], to_core)
+    arrive(orecv.at[1], rs_r.at[1, 1], to_y)
+    tok[...] = (mid[...] + (oown[...] + orecv[2].astype(F32) + orecv[1].astype(F32)) + row(7))[:T].astype(BF)
+    put(tok, h_out, 6)
+    rg_fin(2)
     arrive(grecv.at[2], rs_r.at[2, 2], to_core)
     here = gown[...] + grecv[2].astype(F32)
     away = gpart[1].astype(F32)
@@ -595,84 +635,122 @@
         j = k // g
         dw_sm[k] = gvec[:, j * 128 : (j + 1) * 128]
     for d in range(1, N):
-        send(dw_sm.at[other(d)], rr_sm.at[d - 1], sg_s.at[d - 1], sg_r.at[d - 1], {"fsdp": other(d)})
-    rg_fwd(4, 0)
-    rg_fin(1)
-    rg_fwd(3, 1)
+        send(dw_sm.at[other(d)], rr_sm.at[d - 1], sg_s.at[0], sg_r.at[0], {"fsdp": other(d)})
+    rg_fwd(4, 1)
+    rg_fin(3)
     total = dw_sm[f]
+    arrive(rr_sm, sg_r.at[0], to_ring[0])
     for d in range(1, N):
-        arrive(rr_sm.at[d - 1], sg_r.at[d - 1], to_ring[0])
         total = total + rr_sm[d - 1]
     o_sm[s] = total
-
-    def sm_slot(k):
-        return o_sm.at[k]
-
-    three = ((to_core, s_core), (to_y, s_y), ({"seq": s_diag}, s_diag))
-    for d, (dev, _) in enumerate(three):
-        send(o_sm.at[s], o_sm.at[s], sm_s.at[d], sm_r.at[d], dev)
-    rg_fwd(4, 1)
-    rg_fin(2)
-    rg_fwd(3, 2)
-    sq_relay(KFIN + 0, fin_slot(0))
+    for dev in (to_core, to_y, {"seq": s_diag}):
+        send(o_sm.at[s], o_sm.at[s], sm_s.at[0], sm_r.at[0], dev)
     rg_fwd(4, 2)
+
+    hbm = [h_dn, h_up, h_ow] + [h_qkv.at[hp] for hp in range(HP)]
+    finals = [(KFIN + m, fin_slot(m)) for m in range(MG)]
+
+    def put_slot(m, k):
+        put(grads[m][2].at[k], hbm[m].at[k], m)
+
+    def relay_out(m):
+        sq_relay(*finals[m])
+        put_slot(m, s_y)
+
+    put_slot(0, s)
+    put_slot(1, s)
+    put_slot(2, s)
+    put_slot(3, s)
+    relay_out(0)
     arrive(grecv.at[1], rs_r.at[2, 1], to_y)
     gn = here + grecv[1].astype(F32)
-    o_tok[...] = (gmid[...] + norm_pull(gn, row(0), unit, rate))[:T].astype(BF)
-    rg_fin(3)
-    sq_relay(KFIN + 1, fin_slot(1))
+    cot[...] = (gmid[...] + norm_pull(gn, row(0), unit, rate))[:T].astype(BF)
+    put(cot, h_tok, 7)
     rg_fin(4)
-    sq_relay(KFIN + 2, fin_slot(2))
-    finals = [(KFIN + m, fin_slot(m)) for m in range(MG)]
-    for kind, ref in (finals[3], finals[4]):
-        sq_relay(kind, ref)
-    for kind, ref in finals:
-        sq_core(kind, ref)
-        sq_diag(kind, ref)
-    for d, (dev, k) in enumerate(three):
-        arrive(o_sm.at[k], sm_r.at[d], dev)
-        sent(o_sm.at[s], sm_s.at[d], dev)
+    put_slot(4, s)
+    for m in range(MG):
+        sq_core(*finals[m])
+        put_slot(m, s_core)
+    for m in range(1, MG):
+        relay_out(m)
+    arrive(o_sm.at[:3], sm_r.at[0], to_core)
+    put(o_sm, h_sm, 5)
+    for m in range(MG):
+        sq_diag(*finals[m])
+        put_slot(m, s_diag)
 
     for m in range(3 + HP):
         ag_sent(m)
     for m in range(MG):
         rg_sent(m)
-    for kind, ref in [(KX, x_slot), (KC, c_slot), (KG, g_slot), (KO, out_slot)] + finals:
-        sq_sent(kind, ref)
+    for kind, ref in ((KX, xg), (KC, cg), (KG, nrm)):
+        sq_sent(kind, ref.at[:3])
+    sq_sent(KO, wout.at[:, : 3 * DH])
     for hp in range(HP):
-        sq_sent(KCTX + hp, ctx_slot(hp))
+        sq_sent(KCTX + hp, ctx.at[:3, :, hp * 128 : hp * 128 + 128])
+    for m in range(MG):
+        sq_sent(KFIN + m, grads[m][2].at[:3])
     seq_sent(1, opart)
     seq_sent(2, gpart)
-    for d in range(1, N):
-        sent(smg.at[f], sa_s.at[d - 1], to_ring[0])
-        sent(dw_sm.at[other(d)], sg_s.at[d - 1], to_ring[0])
-
-
-def finish_kernel(z, out, tok, gq, go, gu, gd, gs, *outs):
-    o_out, o_tok, o_qkv, o_ow, o_up, o_dn = outs[:6]
-    D, wf, HP, N = z["D"], z["wf"], z["HP"], 2 * z["A"]
+    sent(smg.at[: N - 1], sa_s.at[0], to_ring[0])
+    sent(dw_sm.at[: N - 1], sg_s.at[0], to_ring[0])
+    sent(o_sm.at[:3], sm_s.at[0], to_core)
+    for src, dst, k in [(grads[m][2], hbm[m], m) for m in range(MG)] + [(o_sm, h_sm, 5), (tok, h_out, 6), (cot, h_tok, 7)]:
+        pltpu.make_async_copy(src, dst, put_sem.at[k]).wait()
+
+
+def finish_kernel(z, *refs):
+    srcs, dsts = refs[:7], refs[7:22]
+    (out, tok, gq, go, gu, gd, gs), bufs = refs[22:29], refs[29:42]
+    s_in, s_out = refs[42:]
+    D, w, wf, HP, N = z["D"], z["w"], z["wf"], z["HP"], 2 * z["A"]
     DH = D // 4
+    loads = [pltpu.make_async_copy(src, dst, s_in.at[k]) for k, (src, dst) in enumerate(zip(srcs, (out, tok, gq, go, gu, gd, gs)))]
+    saves = []
+
+    def save(src, k):
+        copy = pltpu.make_async_copy(src, dsts[k], s_out.at[k])
+        copy.start()
+        saves.append(copy)
+
+    for k in (5, 4, 2, 3, 6, 0, 1):
+        loads[k].start()
+    f_qkv, f_ow, f_up, f_dn = bufs[:4]
+    loads[5].wait()
+    for s in range(4):
+        f_dn[s * wf : (s + 1) * wf] = gd[s].astype(F32)
+    save(f_dn, 5)
+    loads[4].wait()
+    if z["up_whole"]:
+        for s in range(4):
+            for k in range(N):
+                f_up[:, (k * 4 + s) * wf : (k * 4 + s + 1) * wf] = gu[s, :, k * wf : (k + 1) * wf].astype(F32)
+    else:
+        f_up[...] = gu[...].astype(F32)
+    save(f_up, 4)
+    loads[2].wait()
     for s in range(4):
         for hp in range(HP):
             for part in range(3):
                 lo = part * D + s * DH + hp * 128
-                o_qkv[:, lo : lo + 128] = gq[hp, s, :, part * 128 : part * 128 + 128].astype(F32)
-        o_ow[:, s * DH : (s + 1) * DH] = go[s].astype(F32)
-        if z["up_whole"]:
-            for k in range(N):
-                o_up[:, (k * 4 + s) * wf : (k * 4 + s + 1) * wf] = gu[s, :, k * wf : (k + 1) * wf].astype(F32)
-    if not z["up_whole"]:
-        o_up[...] = gu[...].astype(F32)
-    o_dn[...] = gd[0].astype(F32)
-
-    @pl.when(pl.program_id(0) == 0)
-    def _():
-        o_out[...] = out[...]
-        o_tok[...] = tok[...]
-        total = gs[0] + gs[1] + gs[2] + gs[3]
-        for k in range(8):
-            outs[6 + k][...] = total[k : k + 1]
-        outs[14][...] = jnp.concatenate([gs[s, 8:9] for s in range(4)], axis=1)
+                f_qkv[:, lo : lo + 128] = gq[hp, s, :, part * 128 : part * 128 + 128].astype(F32)
+    save(f_qkv, 2)
+    loads[3].wait()
+    for s in range(4):
+        f_ow[:, s * DH : (s + 1) * DH] = go[s].astype(F32)
+    save(f_ow, 3)
+    loads[6].wait()
+    total = gs[0] + gs[1] + gs[2] + gs[3]
+    for k in range(8):
+        bufs[4 + k][...] = total[k : k + 1]
+        save(bufs[4 + k], 6 + k)
+    bufs[12][...] = jnp.concatenate([gs[s, 8:9] for s in range(4)], axis=1)
+    save(bufs[12], 14)
+    for k, buf in ((0, out), (1, tok)):
+        loads[k].wait()
+        save(buf, k)
+    for copy in saves:
+        copy.wait()
 
 
 def make_body(mesh):
@@ -696,21 +774,24 @@
         s = lax.axis_index("seq")
         f = lax.axis_index("fsdp")
         up_whole = wf % 128 == 0
-        ub = lax.dynamic_slice(up_bias, (s * wf,), (wf,))
-        packed = jnp.stack(
-            [ln1_gain, ln1_bias, q_bias, v_bias, out_bias, ln2_gain, ln2_bias, down_bias, ub]
-            + [jnp.zeros_like(ub)] * 7
-        )
+        plain = (ln1_gain, ln1_bias, q_bias, v_bias, out_bias, ln2_gain, ln2_bias, down_bias)
         if g == 1:
-            small = packed
+            vectors_in = [v.reshape(1, w) for v in plain]
+            ub_in = up_bias.reshape(4, wf)
         else:
-            small = lax.dynamic_update_slice(jnp.zeros((16, 128), BF), packed, (0, lax.rem(f, g) * w))
+            spot = lax.rem(f, g) * w
+            blank = jnp.zeros((1, 128), BF)
+            vectors_in = [lax.dynamic_update_slice(blank, v[None], (0, spot)) for v in plain]
+            mine = lax.dynamic_slice(up_bias, (s * wf,), (wf,))
+            ub_in = lax.dynamic_update_slice(jnp.zeros((4, 128), BF), mine[None], (s, spot))
         if not up_whole:
             up_weight = lax.dynamic_index_in_dim(up_weight.reshape(w, N, 4, wf), s, 2, False).reshape(w, FQ)
         z = dict(D=D, T=T, TP=TP, R=R, A=A, w=w, wf=wf, HP=HP, g=g, up_whole=up_whole)
         vm = pltpu.VMEM
         C = 384
         scratch = [
+            vm((T, D), BF), vm((T, D), BF), pltpu.SMEM((1,), jnp.int32), vm((8, 1, 128), BF), vm((4, 128), BF),
+            vm((HP, 4, w, C), BF), vm((4, w, DH), BF), vm((4, w, FQ), BF), vm((4, wf, D), BF), vm((4, 16, 128), F32),
             vm((4, TP, D), BF),
             vm((4, TP, D), BF),
             vm((4, TP, D), BF),
@@ -733,20 +814,19 @@
             vm((HP, 128, R), F32),
             vm((HP, 128, R), F32),
             vm((3, TP, D), BF), vm((TP, D), F32), vm((3, TP, D), BF),
-            vm((3, TP, D), BF), vm((3, TP, D), BF),
+            vm((3, TP, D), BF), vm((TP, D), F32), vm((3, TP, D), BF),
             vm((1, R), F32),
             vm((HP, N, w, C), BF), vm((N, w, DH), BF), vm((N, w, FQ), BF), vm((N, wf, D), BF), vm((N, 16, 128), F32),
             vm((HP, 2, A, w, C), BF), vm((2, A, w, DH), BF), vm((2, A, w, FQ), BF), vm((2, A, wf, D), BF), vm((N - 1, 16, 128), F32),
         ]
         dma = pltpu.SemaphoreType.DMA
         scratch += [
-            dma((3 + 3 * HP + (N if up_whole else 1),)),
-            dma((3 + HP, 2, A)), dma((3 + HP, 2, A)), dma((3 + HP, 2, A)), dma((3 + HP, 2, A)),
-            dma((7 + 2 * HP, 3)), dma((7 + 2 * HP, 3)),
-            dma((3, 3)), dma((3, 3)),
-            dma((N - 1,)), dma((N - 1,)), dma((N - 1,)), dma((N - 1,)), dma((3,)), dma((3,)),
+            dma((9,)), dma((8,)),
+            dma((3 + HP,)), dma((3 + HP, 2, A)), dma((3 + HP,)), dma((3 + HP, 2, A)),
+            dma((7 + 2 * HP,)), dma((7 + 2 * HP, 3)),
+            dma((3,)), dma((3, 3)),
+            dma((1,)), dma((1,)), dma((1,)), dma((1,)), dma((1,)), dma((1,)),
         ]
-        here = pl.BlockSpec(memory_space=pltpu.VMEM)
         there = pl.BlockSpec(memory_space=pl.ANY)
         out_shapes = [
             jax.ShapeDtypeStruct((T, D), BF),
@@ -758,51 +838,32 @@
             jax.ShapeDtypeStruct((4, 16, 128), F32),
         ]
         out, gtok, gq, go, gu, gd, gs = pl.pallas_call(
-            functools.partial(layer_kernel, z),
+            functools.partial(layer_entry, z),
             out_shape=out_shapes,
-            in_specs=[here, here, pl.BlockSpec(memory_space=pltpu.SMEM), there, there, there, there, there],
-            out_specs=[here] * 7,
+            in_specs=[there] * 16,
+            out_specs=[there] * 7,
             scratch_shapes=scratch,
             compiler_params=pltpu.CompilerParams(
                 collective_id=0, has_side_effects=True, vmem_limit_bytes=67_000_000
             ),
             name="layer",
-        )(tokens[0], cotangent[0], lengths, small, qkv_weight, out_weight, up_weight, down_weight)
+        )(tokens[0], cotangent[0], lengths, *vectors_in, ub_in, qkv_weight, out_weight, up_weight, down_weight)
 
         if not up_whole:
             gu = gu.reshape(4, w, N, wf).transpose(1, 2, 0, 3).reshape(w, FF)
         if g > 1:
             gs = lax.dynamic_slice(gs, (0, 0, lax.rem(f, g) * w), (4, 16, w))
-        parts = 4
-        rb = w // parts
-        whole = lambda shape: pl.BlockSpec(shape, lambda i: (0,) * len(shape))
-        vectors = [jax.ShapeDtypeStruct((1, w), F32)] * 8 + [jax.ShapeDtypeStruct((1, 4 * wf), F32)]
-        up_spec = pl.BlockSpec((4, rb, FQ), lambda i: (0, i, 0)) if up_whole else pl.BlockSpec((rb, FF), lambda i: (i, 0))
+        shapes = [((w, 3 * D), F32), ((w, D), F32), ((w, FF), F32), ((4 * wf, D), F32)]
+        shapes += [((1, w), F32)] * 8 + [((1, 4 * wf), F32)]
+        sources = (out, gtok, gq, go, gu, gd, gs)
         done = pl.pallas_call(
             functools.partial(finish_kernel, z),
-            grid=(parts,),
-            out_shape=[
-                jax.ShapeDtypeStruct((T, D), BF), jax.ShapeDtypeStruct((T, D), BF),
-                jax.ShapeDtypeStruct((w, 3 * D), F32), jax.ShapeDtypeStruct((w, D), F32),
-                jax.ShapeDtypeStruct((w, FF), F32), jax.ShapeDtypeStruct((4 * wf, D), F32),
-            ] + vectors,
-            in_specs=[
-                whole((T, D)), whole((T, D)),
-                pl.BlockSpec((HP, 4, rb, C), lambda i: (0, 0, i, 0)),
-                pl.BlockSpec((4, rb, DH), lambda i: (0, i, 0)),
-                up_spec,
-                pl.BlockSpec((1, wf, D), lambda i: (i, 0, 0)),
-                whole((4, 16, w)),
-            ],
-            out_specs=[
-                whole((T, D)), whole((T, D)),
-                pl.BlockSpec((rb, 3 * D), lambda i: (i, 0)),
-                pl.BlockSpec((rb, D), lambda i: (i, 0)),
-                pl.BlockSpec((rb, FF), lambda i: (i, 0)),
-                pl.BlockSpec((wf, D), lambda i: (i, 0)),
-            ] + [whole((1, w))] * 8 + [whole((1, 4 * wf))],
+            out_shape=[jax.ShapeDtypeStruct(*v) for v in [((T, D), BF)] * 2 + shapes],
+            in_specs=[there] * 7,
+            out_specs=[there] * 15,
+            scratch_shapes=[vm(v.shape, v.dtype) for v in sources] + [vm(*v) for v in shapes] + [dma((7,)), dma((15,))],
             name="finish",
-        )(out, gtok, gq, go, gu, gd, gs)
+        )(*sources)
         out, gtok, g_qkv, g_out, g_up, g_down = done[:6]
         sums = [v.reshape(-1) for v in done[6:]]
         return (

time: 170 us -> 157 us (0.924)
  Pallas kernels: 166 us -> 156 us
  local copies, waits for them, and re-layouts: 2.08 us -> 0 us
    pallas_call x2, Pallas kernels: 166 us -> 156 us  [the longest x1 151 us: body(): pl.pallas_call(functools.partial(layer_entry, z), out_shape=out_shapes, i...]
    another operation x5 -> x0, local copies, waits for them, and re-layouts: 2.06 us -> none  [body(): jnp.stack([ln1_gain, ln1_bias, q_bias, v_bias, out_bias, ln2_gain, ln2_bi...]
where the time goes in v4:
time: 157 us
  Pallas kernels  156 us (99%)
    pallas_call x1, Pallas kernels, body(): pl.pallas_call(functools.partial(layer_entry, z), out_shape=out_shapes, i...  151 us
    pallas_call x1, Pallas kernels, body(): pl.pallas_call(functools.partial(finish_kernel, z), out_shape=[jax.ShapeD...  4.57 us

profile of v4, /device:TPU:0, one launch (start us, length us, event | category | flops | bytes accessed | tf_op | source)
XLA Modules:
  0.0 157.2 jit_solution(8797709458849723368)
XLA Ops:
  1.3 151.2 %layer.1 = (bf16[258,1024]{1,0:T(8,128)(2,1)}, bf16[258,1024]{1,0:T(8,128)(2,1)}, bf16[2,4,128,384]{3,2,1,0:T(8,128)(2,1)}, bf16[4,128,256]{2,1,0:T(8,128)(2,1)}...) custom-call(bf16[258,1024]{1,0:T(8,128)(2,1)} %bitcast.22, ...), custom_call_target="tpu_custom_call" | custom-call | tf_op jit(solution)/shard_map/layer/pallas_call | solution.py:840
  152.5 4.6 %finish.1 = (bf16[258,1024]{1,0:T(8,128)(2,1)}, bf16[258,1024]{1,0:T(8,128)(2,1)}, f32[128,3072]{1,0:T(8,128)}, f32[128,1024]{1,0:T(8,128)}, f32[128,4096]{1,0:T...) custom-call(bf16[258,1024]{1,0:T(8,128)(2,1)} %get-tuple-element.37., ...), custom_call_target="tpu_custom_call" | custom-call | tf_op jit(solution)/shard_map/finish/pallas_call | solution.py:859

commit v5 on v4

--- a/solution.py
+++ b/solution.py
@@ -118,14 +118,14 @@
     def ag_own(m):
         for way in range(2):
             ref = ag_block(m, way, 1, 0)
-            send(ref, ref, ag_s.at[m], ag_r.at[m, way, 0], to_ring[way])
+            send(ref, ref, ag_s.at[m], ag_r.at[m, 0], to_ring[way])
 
     def ag_take(m, d):
+        arrive(ag_rows(m, 1 if d == H else 2), ag_r.at[m, d - 1], to_ring[0])
         for way in range(2):
-            arrive(ag_block(m, way, d, d), ag_r.at[m, way, d - 1], to_ring[way])
             if d < H:
                 ref = ag_block(m, way, d + 1, d)
-                send(ref, ref, ag_s.at[m], ag_r.at[m, way, d], to_ring[way])
+                send(ref, ref, ag_s.at[m], ag_r.at[m, d], to_ring[way])
 
     def ag_fwd(m, third):
         for d in thirds(1, H)[third]:
@@ -134,10 +134,13 @@
     def ag_last(m):
         ag_take(m, H)
 
+    def ag_rows(m, shards):
+        size = shards * (wf if m == DN else w)
+        every = {OUT: wout.at[:size, quarter], UP: wup.at[:size], DN: wdn.at[:size]}
+        return every[m] if m in every else wqkv.at[:size, m * 384 : m * 384 + 384]
+
     def ag_sent(m):
-        size = (N - 1) * (wf if m == DN else w)
-        every = {OUT: wout.at[:size, quarter], UP: wup.at[:size], DN: wdn.at[:size]}
-        sent(every[m] if m in every else wqkv.at[:size, m * 384 : m * 384 + 384], ag_s.at[m], to_ring[0])
+        sent(ag_rows(m, N - 1), ag_s.at[m], to_ring[0])
 
     def sq_send(kind, ref):
         send(ref(s), ref(s), sq_s.at[kind], sq_r.at[kind, 0], to_core)
@@ -162,8 +165,8 @@
     def c_slot(k):
         return cg.at[k]
 
-    def g_slot(k):
-        return nrm.at[k]
+    def g_slot(h):
+        return lambda k: nrm.at[k, halves[h]]
 
     def out_slot(k):
         return wout.at[:, pl.ds(pl.multiple_of(k * DH, DH), DH)]
@@ -171,46 +174,63 @@
     def ctx_slot(hp):
         return lambda k: ctx.at[k, :, hp * 128 : hp * 128 + 128]
 
-    KX, KC, KG, KO, KCTX, KFIN = 0, 1, 2, 3, 4, 4 + HP
+    KX, KC, KG, KO, KCTX, KFIN = 0, 1, 2, 4, 5, 5 + HP
 
     def order(i):
         hb, lb = lax.div(3 - i, 2), lax.rem(3 - i, 2)
         return lax.rem(y + hb, 2) * 2 + lax.rem(c + lb, 2)
 
-    def seq_across(kind, part, recv):
-        send(part.at[1], recv.at[1], rs_s.at[kind], rs_r.at[kind, 1], to_y)
-
-    def seq_stage(i, kind, part, own, recv, value, defer=False):
-        @pl.when(i < 3)
-        def _():
-            part[jnp.minimum(i, 2)] = value.astype(BF)
-
-        @pl.when(i == 0)
-        def _():
-            send(part.at[0], recv.at[0], rs_s.at[kind], rs_r.at[kind, 0], to_core)
-
-        @pl.when(i == 1)
-        def _():
-            arrive(recv.at[0], rs_r.at[kind, 0], to_core)
-            part[1] = (part[1].astype(F32) + recv[0].astype(F32)).astype(BF)
+    cut = -(-TP // 32) * 16
+    halves = (slice(0, cut), slice(cut, TP))
+
+    def seq_across(kind, part, recv, h):
+        send(part.at[1, halves[h]], recv.at[1, halves[h]], rs_s.at[kind], rs_r.at[kind, 1, h], to_y)
+
+    def seq_pass(kind, part, own, recv, compute, defer=False, poll=None):
+        def chip_sum(h):
+            rows = halves[h]
+            arrive(recv.at[0, rows], rs_r.at[kind, 0, h], to_core)
+            part[1, rows] = (part[1, rows].astype(F32) + recv[0, rows].astype(F32)).astype(BF)
             if not defer:
-                seq_across(kind, part, recv)
-
-        @pl.when(i == 2)
-        def _():
-            send(part.at[2], recv.at[2], rs_s.at[kind], rs_r.at[kind, 2], to_core)
-
-        @pl.when(i == 3)
-        def _():
-            own[...] = value
+                seq_across(kind, part, recv, h)
+
+        @pl.loop(0, 2)
+        def _(p):
+            chip = lax.rem(y + 1 - p, 2) * 2
+            theirs, ours = chip + 1 - c, chip + c
+            for h, rows in enumerate(halves):
+                count = rows.stop - rows.start
+                value = compute(theirs, ours, rows)
+
+                @pl.when(p == 0)
+                def _():
+                    part[0, rows] = value[:count].astype(BF)
+                    part[1, rows] = value[count:].astype(BF)
+                    send(part.at[0, rows], recv.at[0, rows], rs_s.at[kind], rs_r.at[kind, 0, h], to_core)
+                    if h == 1:
+                        chip_sum(0)
+
+                @pl.when(p == 1)
+                def _():
+                    part[2, rows] = value[:count].astype(BF)
+                    own[rows] = value[count:]
+                    send(part.at[2, rows], recv.at[2, rows], rs_s.at[kind], rs_r.at[kind, 2, h], to_core)
+                    if h == 0:
+                        chip_sum(1)
+                        if poll:
+                            poll()
+
+    def both_rows(ref, theirs, ours, rows):
+        return jnp.concatenate([ref[theirs, rows], ref[ours, rows]], axis=0)
 
     def seq_sent(kind, part):
         sent(part, rs_s.at[kind], to_core)
 
-    def seq_total(kind, own, recv):
-        arrive(recv.at[2], rs_r.at[kind, 2], to_core)
-        arrive(recv.at[1], rs_r.at[kind, 1], to_y)
-        return own[...] + recv[2].astype(F32) + recv[1].astype(F32)
+    def from_core(kind, recv, h):
+        arrive(recv.at[2, halves[h]], rs_r.at[kind, 2, h], to_core)
+
+    def from_y(kind, recv, h):
+        arrive(recv.at[1, halves[h]], rs_r.at[kind, 1, h], to_y)
 
     grads = {0: (dw_dn, rr_dn, o_dn), 1: (dw_up, rr_up, o_up), 2: (dw_out, rr_out, o_ow)}
     for hp in range(HP):
@@ -229,10 +249,10 @@
 
     def rg_send(m, way, j):
         dst = grads[m][1].at[way, j, rg_rows(m, way, j)]
-        send(rg_src(m, way, j), dst, rg_s.at[m], rg_r.at[m, way, j], to_ring[way])
-
-    def rg_arrive(m, way, j):
-        arrive(grads[m][1].at[way, j, rg_rows(m, way, j)], rg_r.at[m, way, j], to_ring[way])
+        send(rg_src(m, way, j), dst, rg_s.at[m], rg_r.at[m, j], to_ring[way])
+
+    def rg_arrive(m, j):
+        arrive(grads[m][0].at[: 1 if j == 0 else 2], rg_r.at[m, j], to_ring[0])
 
     def rg_own(m):
         for way in range(2):
@@ -241,10 +261,10 @@
     def rg_fwd(m, third):
         dw, rr, _ = grads[m]
         for j in thirds(1, H)[third]:
+            rg_arrive(m, j - 1)
             for way in range(2):
                 rows = rg_rows(m, way, j - 1)
                 owner = rg_owner(way, j)
-                rg_arrive(m, way, j - 1)
                 dw[owner, rows] = (dw[owner, rows].astype(F32) + rr[way, j - 1, rows].astype(F32)).astype(dw.dtype)
                 rg_send(m, way, j)
 
@@ -254,8 +274,8 @@
     def rg_fin(m):
         dw, rr, out = grads[m]
         total = dw[f].astype(F32)
+        rg_arrive(m, H - 1)
         for way in range(2):
-            rg_arrive(m, way, H - 1)
             total = total + rr[way, H - 1].astype(F32)
         out[s] = total.astype(out.dtype)
         sq_send(KFIN + m, fin_slot(m))
@@ -446,7 +466,7 @@
         def _():
             mid[...] = value
 
-        @pl.when(i == 0)
+        @pl.when(i == 1)
         def _():
             ag_fwd(DN, 1)
 
@@ -465,7 +485,7 @@
     ag_fwd(DN, 2)
 
     def weight_grad(left, right, dw, size):
-        per = max(256 // size, 1)
+        per = max(512 // size, 1)
 
         @pl.loop(0, dw.shape[0] // per)
         def _(i):
@@ -478,48 +498,46 @@
     rg_own(0)
     ag_last(DN)
 
-    @pl.loop(0, 4)
-    def _(i):
-        k = order(i)
-        grad = (dot_nt(cg[k], wdn[...]) * gbf[k].astype(F32)).astype(BF)
-        gbf[k] = grad
+    def before_grad(theirs, ours, rows):
+        count = rows.stop - rows.start
+        slope = both_rows(gbf, theirs, ours, rows).astype(F32)
+        grad = (dot_nt(both_rows(cg, theirs, ours, rows), wdn[...]) * slope).astype(BF)
+        gbf[theirs, rows] = grad[:count]
+        gbf[ours, rows] = grad[count:]
         gvec[8:9, :] += jnp.sum(grad.astype(F32), axis=0, keepdims=True)
-        seq_stage(i, 0, gpart, gown, grecv, dot_nt(grad, wup[...]))
-
-        @pl.when(i == 2)
-        def _():
-            rg_fwd(0, 0)
-
+        return dot_nt(grad, wup[...])
+
+    seq_pass(0, gpart, gown, grecv, before_grad, poll=lambda: rg_fwd(0, 0))
     weight_grad(n2.reshape(R, D), gbf.reshape(R, D)[...], dw_up, w)
     rg_own(1)
+
+    def branch_rows(h):
+        rows = halves[h]
+        from_core(0, grecv, h)
+        from_y(0, grecv, h)
+        gn = gown[rows] + grecv[2, rows].astype(F32) + grecv[1, rows].astype(F32)
+        unit, rate = unit_rows(mid[rows])
+        c_own = cg[s, rows].astype(F32)
+        gm = c_own + norm_pull(gn, row(5), unit, rate)
+        gmid[rows] = gm
+        branch = gm.astype(BF)
+        nrm[s, rows] = branch
+        sq_send(KG + h, g_slot(h))
+        for k, value in ((5, gn * unit), (6, gn), (7, c_own), (4, branch.astype(F32))):
+            gvec[k : k + 1, :] += jnp.sum(value, axis=0, keepdims=True)
 
     @pl.loop(0, 4)
     def _(k):
         first_norm(k, n2)
 
+    branch_rows(0)
     rg_fwd(0, 1)
 
-    @pl.loop(0, 4)
-    def _(i):
-        seq_stage(i, 1, opart, oown, orecv, dot_nn(hid[order(i)], wdn[...]), defer=True)
-
-    rg_fwd(1, 0)
-
-    gn = seq_total(0, gown, grecv)
+    seq_pass(1, opart, oown, orecv, lambda theirs, ours, rows: dot_nn(both_rows(hid, theirs, ours, rows), wdn[...]), defer=True, poll=lambda: rg_fwd(1, 0))
+    branch_rows(1)
     seq_sent(0, gpart)
-    unit, rate = unit_rows(mid[...])
-    gvec[5:6, :] = jnp.sum(gn * unit, axis=0, keepdims=True)
-    gvec[6:7, :] = jnp.sum(gn, axis=0, keepdims=True)
-    c_own = cg[s].astype(F32)
-    gvec[7:8, :] = jnp.sum(c_own, axis=0, keepdims=True)
-    gm = c_own + norm_pull(gn, row(5), unit, rate)
-    gmid[...] = gm
-    branch = gm.astype(BF)
-    gvec[4:5, :] = jnp.sum(branch.astype(F32), axis=0, keepdims=True)
-    nrm[s] = branch
-    sq_send(KG, g_slot)
-
-    seq_across(1, opart, orecv)
+    for h in range(2):
+        seq_across(1, opart, orecv, h)
 
     flat_g = gctx.reshape(R, DH)
     dkt[...] = jnp.zeros_like(dkt)
@@ -539,7 +557,8 @@
         gvec[3:4, off] = jnp.sum(flat[:, lo + 256 : lo + 384].astype(F32), axis=0, keepdims=True)
 
     branch_back(s)
-    sq_core(KG, g_slot)
+    for h in range(2):
+        sq_core(KG + h, g_slot(h))
     branch_back(s_core)
 
     @pl.loop(0, 8)
@@ -572,13 +591,18 @@
 
         @pl.when(t == 1)
         def _():
+            sq_relay(KG, g_slot(0))
+
+        @pl.when(t == 2)
+        def _():
             rg_fwd(1, 1)
 
         @pl.when(t == 3)
         def _():
-            sq_relay(KG, g_slot)
+            sq_relay(KG + 1, g_slot(1))
             branch_back(s_y)
-            sq_diag(KG, g_slot)
+            for h in range(2):
+                sq_diag(KG + h, g_slot(h))
             branch_back(s_diag)
             right = nrm.reshape(R, D)[:, quarter]
             for j in range(4):
@@ -588,43 +612,31 @@
             rg_own(2)
             rg_fin(0)
 
-        @pl.when(t == 4)
+        @pl.when(t == 5)
         def _():
             rg_fwd(2, 0)
             rg_fwd(1, 2)
-
-        @pl.when(t == 5)
-        def _():
             close_pair(0)
+
+        @pl.when(t == 6)
+        def _():
             rg_fwd(2, 1)
 
-        @pl.when(t == 6)
-        def _():
-            rg_fin(1)
-
-        @pl.when(t == 7)
-        def _():
-            rg_fwd(3, 0)
-            rg_fwd(2, 2)
-
     close_pair(1)
+    rg_fin(1)
+    rg_fwd(3, 0)
+    rg_fwd(2, 2)
+
+    seq_pass(2, gpart, gown, grecv, lambda theirs, ours, rows: dot_nt(both_rows(pq, theirs, ours, rows), wqkv[...]), poll=lambda: rg_fwd(4, 0))
     rg_fwd(3, 1)
-
-    @pl.loop(0, 4)
-    def _(i):
-        seq_stage(i, 2, gpart, gown, grecv, dot_nt(pq[order(i)], wqkv[...]))
-
-        @pl.when(i == 2)
-        def _():
-            rg_fwd(4, 0)
-            rg_fwd(3, 2)
-
-    arrive(orecv.at[2], rs_r.at[1, 2], to_core)
-    arrive(orecv.at[1], rs_r.at[1, 1], to_y)
+    for h in range(2):
+        from_core(1, orecv, h)
+        from_y(1, orecv, h)
     tok[...] = (mid[...] + (oown[...] + orecv[2].astype(F32) + orecv[1].astype(F32)) + row(7))[:T].astype(BF)
     put(tok, h_out, 6)
     rg_fin(2)
-    arrive(grecv.at[2], rs_r.at[2, 2], to_core)
+    for h in range(2):
+        from_core(2, grecv, h)
     here = gown[...] + grecv[2].astype(F32)
     away = gpart[1].astype(F32)
     unit, rate = unit_rows(xg[s].astype(F32))
@@ -637,7 +649,7 @@
     for d in range(1, N):
         send(dw_sm.at[other(d)], rr_sm.at[d - 1], sg_s.at[0], sg_r.at[0], {"fsdp": other(d)})
     rg_fwd(4, 1)
-    rg_fin(3)
+    rg_fwd(3, 2)
     total = dw_sm[f]
     arrive(rr_sm, sg_r.at[0], to_ring[0])
     for d in range(1, N):
@@ -657,12 +669,14 @@
         sq_relay(*finals[m])
         put_slot(m, s_y)
 
-    put_slot(0, s)
-    put_slot(1, s)
-    put_slot(2, s)
+    for m in range(3):
+        put_slot(m, s)
+    relay_out(0)
+    rg_fin(3)
     put_slot(3, s)
-    relay_out(0)
-    arrive(grecv.at[1], rs_r.at[2, 1], to_y)
+    relay_out(1)
+    for h in range(2):
+        from_y(2, grecv, h)
     gn = here + grecv[1].astype(F32)
     cot[...] = (gmid[...] + norm_pull(gn, row(0), unit, rate))[:T].astype(BF)
     put(cot, h_tok, 7)
@@ -671,7 +685,7 @@
     for m in range(MG):
         sq_core(*finals[m])
         put_slot(m, s_core)
-    for m in range(1, MG):
+    for m in range(2, MG):
         relay_out(m)
     arrive(o_sm.at[:3], sm_r.at[0], to_core)
     put(o_sm, h_sm, 5)
@@ -683,8 +697,10 @@
         ag_sent(m)
     for m in range(MG):
         rg_sent(m)
-    for kind, ref in ((KX, xg), (KC, cg), (KG, nrm)):
+    for kind, ref in ((KX, xg), (KC, cg)):
         sq_sent(kind, ref.at[:3])
+    for h in range(2):
+        sq_sent(KG + h, nrm.at[:3, halves[h]])
     sq_sent(KO, wout.at[:, : 3 * DH])
     for hp in range(HP):
         sq_sent(KCTX + hp, ctx.at[:3, :, hp * 128 : hp * 128 + 128])
@@ -822,9 +838,9 @@
         dma = pltpu.SemaphoreType.DMA
         scratch += [
             dma((9,)), dma((8,)),
-            dma((3 + HP,)), dma((3 + HP, 2, A)), dma((3 + HP,)), dma((3 + HP, 2, A)),
-            dma((7 + 2 * HP,)), dma((7 + 2 * HP, 3)),
-            dma((3,)), dma((3, 3)),
+            dma((3 + HP,)), dma((3 + HP, A)), dma((3 + HP,)), dma((3 + HP, A)),
+            dma((8 + 2 * HP,)), dma((8 + 2 * HP, 3)),
+            dma((3,)), dma((3, 3, 2)),
             dma((1,)), dma((1,)), dma((1,)), dma((1,)), dma((1,)), dma((1,)),
         ]
         there = pl.BlockSpec(memory_space=pl.ANY)

time: 157 us -> 153 us (0.975)
  Pallas kernels: 156 us -> 151 us
    pallas_call x1, Pallas kernels: 151 us -> 146 us  [body(): pl.pallas_call(functools.partial(layer_entry, z), out_shape=out_shapes, i...]
where the time goes in v5:
time: 153 us; the launch traced here: 152 us
  Pallas kernels  151 us (99%)
    pallas_call x1, Pallas kernels, body(): pl.pallas_call(functools.partial(layer_entry, z), out_shape=out_shapes, i...  146 us
    pallas_call x1, Pallas kernels, body(): pl.pallas_call(functools.partial(finish_kernel, z), out_shape=[jax.ShapeD...  4.57 us

profile of v5, /device:TPU:0, one launch (start us, length us, event | category | flops | bytes accessed | tf_op | source)
XLA Modules:
  0.0 152.3 jit_solution(14568408742303552463)
XLA Ops:
  1.3 146.3 %layer.1 = (bf16[258,1024]{1,0:T(8,128)(2,1)}, bf16[258,1024]{1,0:T(8,128)(2,1)}, bf16[2,4,128,384]{3,2,1,0:T(8,128)(2,1)}, bf16[4,128,256]{2,1,0:T(8,128)(2,1)}...) custom-call(bf16[258,1024]{1,0:T(8,128)(2,1)} %bitcast.22, ...), custom_call_target="tpu_custom_call" | custom-call | tf_op jit(solution)/shard_map/layer/pallas_call | solution.py:856
  147.6 4.6 %finish.1 = (bf16[258,1024]{1,0:T(8,128)(2,1)}, bf16[258,1024]{1,0:T(8,128)(2,1)}, f32[128,3072]{1,0:T(8,128)}, f32[128,1024]{1,0:T(8,128)}, f32[128,4096]{1,0:T...) custom-call(bf16[258,1024]{1,0:T(8,128)(2,1)} %get-tuple-element.37., ...), custom_call_target="tpu_custom_call" | custom-call | tf_op jit(solution)/shard_map/finish/pallas_call | solution.py:875

commit v6 on v5

--- a/solution.py
+++ b/solution.py
@@ -102,11 +102,14 @@
             return pl.ds(pl.multiple_of(k * size, size), size)
         return pl.ds(pl.multiple_of(k * size + half * (size // 2), size // 2), size // 2)
 
-    OUT, UP, DN = HP, HP + 1, HP + 2
+    OUT, UP, DNA, DNB = HP, HP + 1, HP + 2, HP + 3
+    MA = HP + 4
+    low, high = slice(0, D // 2), slice(D // 2, D)
     blocks = {
         OUT: lambda k, half=None: wout.at[rows_of(k, w, half), quarter],
         UP: lambda k, half=None: wup.at[rows_of(k, w, half)],
-        DN: lambda k, half=None: wdn.at[rows_of(k, wf, half)],
+        DNA: lambda k, half=None: wdn.at[rows_of(k, wf, half), low],
+        DNB: lambda k, half=None: wdn.at[rows_of(k, wf, half), high],
     }
     for hp in range(HP):
         blocks[hp] = lambda k, half=None, hp=hp: wqkv.at[rows_of(k, w, half), hp * 384 : hp * 384 + 384]
@@ -135,8 +138,8 @@
         ag_take(m, H)
 
     def ag_rows(m, shards):
-        size = shards * (wf if m == DN else w)
-        every = {OUT: wout.at[:size, quarter], UP: wup.at[:size], DN: wdn.at[:size]}
+        size = shards * (wf if m in (DNA, DNB) else w)
+        every = {OUT: wout.at[:size, quarter], UP: wup.at[:size], DNA: wdn.at[:size, low], DNB: wdn.at[:size, high]}
         return every[m] if m in every else wqkv.at[:size, m * 384 : m * 384 + 384]
 
     def ag_sent(m):
@@ -232,10 +235,16 @@
     def from_y(kind, recv, h):
         arrive(recv.at[1, halves[h]], rs_r.at[kind, 1, h], to_y)
 
-    grads = {0: (dw_dn, rr_dn, o_dn), 1: (dw_up, rr_up, o_up), 2: (dw_out, rr_out, o_ow)}
-    for hp in range(HP):
-        grads[3 + hp] = (dw_qkv.at[hp], rr_qkv.at[hp], o_qkv.at[hp])
-    MG = 3 + HP
+    grads = {0: (dw_dn, rr_dn, o_dn), 2: (dw_out, rr_out, o_ow)}
+    FQ = dw_up.shape[2]
+    sides = (slice(0, FQ // 2), slice(FQ // 2, FQ))
+    for m, side in zip((1, 6), sides):
+        grads[m] = (dw_up.at[:, :, side], rr_up.at[:, :, :, side], o_up.at[:, :, side])
+    grads[3] = (dw_qkv.at[0], rr_qkv.at[0], o_qkv.at[0])
+    split = (slice(0, w // 2), slice(w // 2, w))
+    for h in range(2):
+        grads[4 + h] = (dw_qkv.at[1, :, split[h]], rr_qkv.at[1, :, :, split[h]], o_qkv.at[1, :, split[h]])
+    MG = 7
 
     def rg_rows(m, way, j):
         size = grads[m][0].shape[1]
@@ -383,7 +392,8 @@
     ag_fwd(1, 2)
     ag_fwd(OUT, 2)
     ag_own(UP)
-    ag_own(DN)
+    ag_own(DNA)
+    ag_own(DNB)
     sq_diag(KX, x_slot)
     first_norm(s_diag)
     ag_last(0)
@@ -434,23 +444,25 @@
         def _():
             sq_send(KCTX, ctx_slot(0))
 
-        @pl.when(t == 6)
-        def _():
-            ag_fwd(UP, 1)
-            ag_fwd(DN, 0)
+        @pl.when(t == 5)
+        def _():
+            ag_fwd(DNA, 0)
 
         @pl.when(t == 7)
         def _():
             sq_send(KCTX + 1, ctx_slot(1))
 
     sq_relay(KO, out_slot)
+    ag_fwd(UP, 1)
+    ag_fwd(DNB, 0)
     sq_relay(KCTX, ctx_slot(0))
     sq_core(KO, out_slot)
     sq_diag(KO, out_slot)
     sq_core(KCTX, ctx_slot(0))
     sq_core(KCTX + 1, ctx_slot(1))
+    sq_relay(KCTX + 1, ctx_slot(1))
     ag_fwd(UP, 2)
-    sq_relay(KCTX + 1, ctx_slot(1))
+    ag_fwd(DNA, 1)
     sq_diag(KCTX, ctx_slot(0))
     sq_diag(KCTX + 1, ctx_slot(1))
 
@@ -468,7 +480,7 @@
 
         @pl.when(i == 1)
         def _():
-            ag_fwd(DN, 1)
+            ag_fwd(DNB, 1)
 
     sq_core(KC, c_slot)
     sq_diag(KC, c_slot)
@@ -482,7 +494,11 @@
         hid[k] = (before * cdf).astype(BF)
         gbf[k] = slope.astype(BF)
 
-    ag_fwd(DN, 2)
+        @pl.when(k == 1)
+        def _():
+            ag_fwd(DNA, 2)
+
+    ag_fwd(DNB, 2)
 
     def weight_grad(left, right, dw, size):
         per = max(512 // size, 1)
@@ -496,7 +512,8 @@
 
     weight_grad(hid.reshape(R, D), cg.reshape(R, D)[...], dw_dn, wf)
     rg_own(0)
-    ag_last(DN)
+    ag_last(DNA)
+    ag_last(DNB)
 
     def before_grad(theirs, ours, rows):
         count = rows.stop - rows.start
@@ -510,6 +527,7 @@
     seq_pass(0, gpart, gown, grecv, before_grad, poll=lambda: rg_fwd(0, 0))
     weight_grad(n2.reshape(R, D), gbf.reshape(R, D)[...], dw_up, w)
     rg_own(1)
+    rg_own(6)
 
     def branch_rows(h):
         rows = halves[h]
@@ -533,7 +551,11 @@
     branch_rows(0)
     rg_fwd(0, 1)
 
-    seq_pass(1, opart, oown, orecv, lambda theirs, ours, rows: dot_nn(both_rows(hid, theirs, ours, rows), wdn[...]), defer=True, poll=lambda: rg_fwd(1, 0))
+    def up_poll():
+        rg_fwd(1, 0)
+        rg_fwd(6, 0)
+
+    seq_pass(1, opart, oown, orecv, lambda theirs, ours, rows: dot_nn(both_rows(hid, theirs, ours, rows), wdn[...]), defer=True, poll=up_poll)
     branch_rows(1)
     seq_sent(0, gpart)
     for h in range(2):
@@ -551,7 +573,8 @@
         flat[:, lo + 128 : lo + 256] = dkt[hp].T.astype(BF)
         flat[:, lo + 256 : lo + 384] = dvt[hp].T.astype(BF)
         weight_grad(n2.reshape(R, D), flat[:, lo : lo + 384], dw_qkv.at[hp], w)
-        rg_own(3 + hp)
+        for m in ((3,), (4, 5))[hp]:
+            rg_own(m)
         off = lanes_at(s * DH + hp * 128)
         gvec[2:3, off] = jnp.sum(flat[:, lo : lo + 128].astype(F32), axis=0, keepdims=True)
         gvec[3:4, off] = jnp.sum(flat[:, lo + 256 : lo + 384].astype(F32), axis=0, keepdims=True)
@@ -596,6 +619,7 @@
         @pl.when(t == 2)
         def _():
             rg_fwd(1, 1)
+            rg_fwd(6, 1)
 
         @pl.when(t == 3)
         def _():
@@ -612,28 +636,40 @@
             rg_own(2)
             rg_fin(0)
 
+        @pl.when(t == 4)
+        def _():
+            rg_fwd(1, 2)
+
         @pl.when(t == 5)
         def _():
             rg_fwd(2, 0)
-            rg_fwd(1, 2)
+            rg_fwd(6, 2)
             close_pair(0)
 
         @pl.when(t == 6)
         def _():
+            rg_fin(1)
             rg_fwd(2, 1)
 
+        @pl.when(t == 7)
+        def _():
+            rg_fin(6)
+
     close_pair(1)
-    rg_fin(1)
     rg_fwd(3, 0)
     rg_fwd(2, 2)
 
-    seq_pass(2, gpart, gown, grecv, lambda theirs, ours, rows: dot_nt(both_rows(pq, theirs, ours, rows), wqkv[...]), poll=lambda: rg_fwd(4, 0))
+    def last_poll():
+        rg_fwd(4, 0)
+        rg_fwd(5, 0)
+
+    seq_pass(2, gpart, gown, grecv, lambda theirs, ours, rows: dot_nt(both_rows(pq, theirs, ours, rows), wqkv[...]), poll=last_poll)
     rg_fwd(3, 1)
     for h in range(2):
         from_core(1, orecv, h)
         from_y(1, orecv, h)
     tok[...] = (mid[...] + (oown[...] + orecv[2].astype(F32) + orecv[1].astype(F32)) + row(7))[:T].astype(BF)
-    put(tok, h_out, 6)
+    put(tok, h_out, 8)
     rg_fin(2)
     for h in range(2):
         from_core(2, grecv, h)
@@ -649,7 +685,10 @@
     for d in range(1, N):
         send(dw_sm.at[other(d)], rr_sm.at[d - 1], sg_s.at[0], sg_r.at[0], {"fsdp": other(d)})
     rg_fwd(4, 1)
+    rg_fwd(5, 1)
     rg_fwd(3, 2)
+    rg_fwd(4, 2)
+    rg_fwd(5, 2)
     total = dw_sm[f]
     arrive(rr_sm, sg_r.at[0], to_ring[0])
     for d in range(1, N):
@@ -657,9 +696,9 @@
     o_sm[s] = total
     for dev in (to_core, to_y, {"seq": s_diag}):
         send(o_sm.at[s], o_sm.at[s], sm_s.at[0], sm_r.at[0], dev)
-    rg_fwd(4, 2)
-
-    hbm = [h_dn, h_up, h_ow] + [h_qkv.at[hp] for hp in range(HP)]
+
+    hbm = [h_dn, h_up.at[:, :, sides[0]], h_ow, h_qkv.at[0]]
+    hbm += [h_qkv.at[1, :, split[h]] for h in range(2)] + [h_up.at[:, :, sides[1]]]
     finals = [(KFIN + m, fin_slot(m)) for m in range(MG)]
 
     def put_slot(m, k):
@@ -669,31 +708,33 @@
         sq_relay(*finals[m])
         put_slot(m, s_y)
 
-    for m in range(3):
+    for m in (0, 1, 6, 2):
         put_slot(m, s)
     relay_out(0)
+    relay_out(1)
     rg_fin(3)
     put_slot(3, s)
-    relay_out(1)
+    for m in (4, 5):
+        rg_fin(m)
+        put_slot(m, s)
+    relay_out(6)
     for h in range(2):
         from_y(2, grecv, h)
     gn = here + grecv[1].astype(F32)
     cot[...] = (gmid[...] + norm_pull(gn, row(0), unit, rate))[:T].astype(BF)
-    put(cot, h_tok, 7)
-    rg_fin(4)
-    put_slot(4, s)
+    put(cot, h_tok, 9)
     for m in range(MG):
         sq_core(*finals[m])
         put_slot(m, s_core)
-    for m in range(2, MG):
+    for m in (2, 3, 4, 5):
         relay_out(m)
     arrive(o_sm.at[:3], sm_r.at[0], to_core)
-    put(o_sm, h_sm, 5)
+    put(o_sm, h_sm, 7)
     for m in range(MG):
         sq_diag(*finals[m])
         put_slot(m, s_diag)
 
-    for m in range(3 + HP):
+    for m in range(MA):
         ag_sent(m)
     for m in range(MG):
         rg_sent(m)
@@ -711,7 +752,7 @@
     sent(smg.at[: N - 1], sa_s.at[0], to_ring[0])
     sent(dw_sm.at[: N - 1], sg_s.at[0], to_ring[0])
     sent(o_sm.at[:3], sm_s.at[0], to_core)
-    for src, dst, k in [(grads[m][2], hbm[m], m) for m in range(MG)] + [(o_sm, h_sm, 5), (tok, h_out, 6), (cot, h_tok, 7)]:
+    for src, dst, k in [(grads[m][2], hbm[m], m) for m in range(MG)] + [(o_sm, h_sm, 7), (tok, h_out, 8), (cot, h_tok, 9)]:
         pltpu.make_async_copy(src, dst, put_sem.at[k]).wait()
 
 
@@ -837,9 +878,9 @@
         ]
         dma = pltpu.SemaphoreType.DMA
         scratch += [
-            dma((9,)), dma((8,)),
-            dma((3 + HP,)), dma((3 + HP, A)), dma((3 + HP,)), dma((3 + HP, A)),
-            dma((8 + 2 * HP,)), dma((8 + 2 * HP, 3)),
+            dma((9,)), dma((10,)),
+            dma((4 + HP,)), dma((4 + HP, A)), dma((7,)), dma((7, A)),
+            dma((12 + HP,)), dma((12 + HP, 3)),
             dma((3,)), dma((3, 3, 2)),
             dma((1,)), dma((1,)), dma((1,)), dma((1,)), dma((1,)), dma((1,)),
         ]

time: 153 us -> 149 us (0.974)
  Pallas kernels: 151 us -> 147 us
    pallas_call x1, Pallas kernels: 146 us -> 142 us  [body(): pl.pallas_call(functools.partial(layer_entry, z), out_shape=out_shapes, i...]
where the time goes in v6:
time: 149 us
  Pallas kernels  147 us (99%)
  between operations  1.49 us (1%)
    pallas_call x1, Pallas kernels, body(): pl.pallas_call(functools.partial(layer_entry, z), out_shape=out_shapes, i...  142 us
    pallas_call x1, Pallas kernels, body(): pl.pallas_call(functools.partial(finish_kernel, z), out_shape=[jax.ShapeD...  4.57 us

profile of v6, /device:TPU:0, one launch (start us, length us, event | category | flops | bytes accessed | tf_op | source)
XLA Modules:
  0.0 148.5 jit_solution(11995501197491076206)
XLA Ops:
  1.3 142.5 %layer.1 = (bf16[258,1024]{1,0:T(8,128)(2,1)}, bf16[258,1024]{1,0:T(8,128)(2,1)}, bf16[2,4,128,384]{3,2,1,0:T(8,128)(2,1)}, bf16[4,128,256]{2,1,0:T(8,128)(2,1)}...) custom-call(bf16[258,1024]{1,0:T(8,128)(2,1)} %bitcast.22, ...), custom_call_target="tpu_custom_call" | custom-call | tf_op jit(solution)/shard_map/layer/pallas_call | solution.py:897
  143.8 4.6 %finish.1 = (bf16[258,1024]{1,0:T(8,128)(2,1)}, bf16[258,1024]{1,0:T(8,128)(2,1)}, f32[128,3072]{1,0:T(8,128)}, f32[128,1024]{1,0:T(8,128)}, f32[128,4096]{1,0:T...) custom-call(bf16[258,1024]{1,0:T(8,128)(2,1)} %get-tuple-element.37., ...), custom_call_target="tpu_custom_call" | custom-call | tf_op jit(solution)/shard_map/finish/pallas_call | solution.py:916

commit v7 on v6

--- a/solution.py
+++ b/solution.py
@@ -670,7 +670,7 @@
         from_y(1, orecv, h)
     tok[...] = (mid[...] + (oown[...] + orecv[2].astype(F32) + orecv[1].astype(F32)) + row(7))[:T].astype(BF)
     put(tok, h_out, 8)
-    rg_fin(2)
+    rg_fwd(4, 1)
     for h in range(2):
         from_core(2, grecv, h)
     here = gown[...] + grecv[2].astype(F32)
@@ -684,8 +684,8 @@
         dw_sm[k] = gvec[:, j * 128 : (j + 1) * 128]
     for d in range(1, N):
         send(dw_sm.at[other(d)], rr_sm.at[d - 1], sg_s.at[0], sg_r.at[0], {"fsdp": other(d)})
-    rg_fwd(4, 1)
     rg_fwd(5, 1)
+    rg_fin(2)
     rg_fwd(3, 2)
     rg_fwd(4, 2)
     rg_fwd(5, 2)
@@ -770,8 +770,11 @@
         copy.start()
         saves.append(copy)
 
-    for k in (5, 4, 2, 3, 6, 0, 1):
+    for k in (0, 1, 5, 4, 2, 3, 6):
         loads[k].start()
+    for k, buf in ((0, out), (1, tok)):
+        loads[k].wait()
+        save(buf, k)
     f_qkv, f_ow, f_up, f_dn = bufs[:4]
     loads[5].wait()
     for s in range(4):
@@ -803,9 +806,6 @@
         save(bufs[4 + k], 6 + k)
     bufs[12][...] = jnp.concatenate([gs[s, 8:9] for s in range(4)], axis=1)
     save(bufs[12], 14)
-    for k, buf in ((0, out), (1, tok)):
-        loads[k].wait()
-        save(buf, k)
     for copy in saves:
         copy.wait()
 

time: 149 us -> 149 us (level)
  no operation moved by 1% of the time
where the time goes in v7:
time: 149 us
  Pallas kernels  147 us (99%)
  between operations  1.49 us (1%)
    pallas_call x1, Pallas kernels, body(): pl.pallas_call(functools.partial(layer_entry, z), out_shape=out_shapes, i...  142 us
    pallas_call x1, Pallas kernels, body(): pl.pallas_call(functools.partial(finish_kernel, z), out_shape=[jax.ShapeD...  4.56 us

profile of v7, /device:TPU:0, one launch (start us, length us, event | category | flops | bytes accessed | tf_op | source)
XLA Modules:
  0.0 148.5 jit_solution(10275412805964747149)
XLA Ops:
  1.3 142.5 %layer.1 = (bf16[258,1024]{1,0:T(8,128)(2,1)}, bf16[258,1024]{1,0:T(8,128)(2,1)}, bf16[2,4,128,384]{3,2,1,0:T(8,128)(2,1)}, bf16[4,128,256]{2,1,0:T(8,128)(2,1)}...) custom-call(bf16[258,1024]{1,0:T(8,128)(2,1)} %bitcast.22, ...), custom_call_target="tpu_custom_call" | custom-call | tf_op jit(solution)/shard_map/layer/pallas_call | solution.py:897
  143.8 4.6 %finish.1 = (bf16[258,1024]{1,0:T(8,128)(2,1)}, bf16[258,1024]{1,0:T(8,128)(2,1)}, f32[128,3072]{1,0:T(8,128)}, f32[128,1024]{1,0:T(8,128)}, f32[128,4096]{1,0:T...) custom-call(bf16[258,1024]{1,0:T(8,128)(2,1)} %get-tuple-element.37., ...), custom_call_target="tpu_custom_call" | custom-call | tf_op jit(solution)/shard_map/finish/pallas_call | solution.py:916
